TPU v7x, 512 devices: a whole 4x8x8 slice. The times are simulated.
512 devices in a mesh: seq: 64 (over x, y, core), tp: 8 (over z).
Axes of the slice: x: 4, y: 8, z: 8, core: 2. Of those that a mesh axis runs over, the one named last changes fastest.
Arguments:
- img: bfloat16 [4, 2048, 3072], P(None, 'seq', 'tp'), may hold values from -6 to 6
- txt: bfloat16 [4, 256, 3072], P(None, 'seq', 'tp'), may hold values from -6 to 6
- prev_mod: bfloat16 [4, 2048, 3072], P(None, 'seq', 'tp'), may hold values from -47 to 47
- cache: float32 [4, 2048, 3072], P(None, 'seq', 'tp'), may hold values from -6 to 6
- modulation: bfloat16 [3, 4, 3072], P(None, None, 'tp'), may hold values from -4 to 4
- w_qkv: bfloat16 [3072, 3, 2048], P('seq', None, 'tp'), may hold values from -1 to 1, as said below
- qk_gain: float32 [2, 2048], P(None, 'tp'), may hold values from 0.5 to 6, as said below
- output_weight: bfloat16 [2048, 3072], P('tp'), may hold values from -0.1875 to 0.1875
- text_len: int32 [4], replicated, may hold values from 1 to 256
- refresh: int32 [4], replicated, may hold values from 0 to 1, as said below
Outputs:
- out_img: float32 [4, 2048, 3072], P(None, 'seq', 'tp')
- new_cache: float32 [4, 2048, 3072], P(None, 'seq', 'tp')
- rel_l1: float32 [4], replicated
Inputs may be any that keep to these rules, and one draw needn't show every extreme that they name: `refresh`: at least one sequence has flag 1 and at least one has flag 0. `w_qkv`: entries of spread about one over the square root of 3072. `qk_gain`: positive.
All inputs are finite; a program needn't handle non-finite values.
Results may differ from a plain program's by a relative error of at most 0.013.
The roundings to bfloat16 on the way count: a program that leaves them out, or rounds other values in their place, can miss the bound.
Values may be sent and summed in bfloat16 or wider, within the bound.
No kernel may reach another device: no remote copies, remote signals or barrier semaphores. Data moves between devices by JAX's collectives and lax.ppermute only.
A program may use at most 128 MiB of HBM per device.

v0:
```python
import functools

import jax
import jax.numpy as jnp
from jax import lax
from jax.sharding import Mesh
from jax.sharding import PartitionSpec as P

HD = 128
SEQ_TP = ("seq_0", "seq_1", "seq_2", "tp")
SEQ = ("seq_0", "seq_1", "seq_2")


EPS = 0.1
NEG = -1e30


def turned_gather(arrays, axis, dims):
    turned = [jnp.moveaxis(a, dim, 0) for a, dim in zip(arrays, dims)]
    widths = [t[0].size for t in turned]
    both = jnp.concatenate([t.reshape(-1, w) for t, w in zip(turned, widths)], axis=1)
    out = lax.all_gather(both, axis, axis=0, tiled=True)
    blocks = jnp.split(out, [sum(widths[:k]) for k in range(1, len(widths))], axis=1)
    return tuple(
        (
            jnp.moveaxis(b.reshape(-1, *t.shape[1:]), 0, dim)
            for b, t, dim in zip(blocks, turned, dims)
        )
    )


def one_axis_at_a_time(value, axes):
    return functools.reduce(lax.psum, axes, value)


def unit_heads(block, gain):
    shaped = block.reshape(block.shape[:-1] + (block.shape[-1] // HD, HD))
    scaled = shaped * lax.rsqrt(jnp.mean(jnp.square(shaped), axis=-1, keepdims=True) + EPS)
    return scaled.reshape(block.shape) * gain


def local(img, txt, prev_mod, cache, modulation, w_qkv, qk_gain, output_weight, text_len, refresh):
    batch, img_rows, width_loc = img.shape
    txt_rows = txt.shape[1]
    rows = txt_rows + img_rows
    joined = jnp.concatenate([txt, img], axis=1)
    local_mods = modulation.astype(jnp.float32)
    wide, wide_mod = turned_gather((joined, modulation), "tp", (2, 2))
    wide_mods = wide_mod.astype(jnp.float32)
    values = wide.astype(jnp.float32)
    center = jnp.mean(values, axis=2, keepdims=True)
    spread = jnp.mean(jnp.square(values - center), axis=2, keepdims=True)
    normed = (values - center) * lax.rsqrt(spread + EPS)
    modded = (normed * (1.0 + wide_mods[1][:, None, :]) + wide_mods[0][:, None, :]).astype(
        jnp.bfloat16
    )
    offset = lax.axis_index("tp") * width_loc
    own_image = lax.dynamic_slice_in_dim(modded[:, txt_rows:, :], offset, width_loc, 2)
    previous = prev_mod.astype(jnp.float32)
    gap = jnp.sum(jnp.abs(own_image.astype(jnp.float32) - previous), axis=(1, 2))
    base_sum = jnp.sum(jnp.abs(previous), axis=(1, 2))
    numer, denom = (one_axis_at_a_time(gap, SEQ_TP), one_axis_at_a_time(base_sum, SEQ_TP))
    rel_l1 = numer / jnp.maximum(denom, 1.0)
    columns = w_qkv.shape[2]
    projected = jnp.einsum(
        "btd,dkc->btkc",
        modded,
        lax.all_gather(w_qkv, SEQ, axis=0, tiled=True),
        preferred_element_type=jnp.float32,
    )
    heads = columns // HD
    query = unit_heads(projected[:, txt_rows:, 0, :], qk_gain[0]).astype(jnp.bfloat16)
    query_heads = query.reshape(batch, img_rows, heads, HD)
    keyed = unit_heads(projected[:, :, 1, :], qk_gain[1]).astype(jnp.bfloat16)
    valued = projected[:, :, 2, :].astype(jnp.bfloat16)
    paired = jnp.stack([keyed, valued], axis=2)
    score_scale = 1.0 / HD**0.5
    start_top = jnp.full((batch, heads, img_rows), NEG, jnp.float32)
    piece = lax.all_gather(paired, SEQ, axis=1, tiled=True)
    top = start_top
    count = piece.shape[1]
    index = jnp.arange(count, dtype=jnp.int32)
    slot = index % rows
    text_pos = index // rows * txt_rows + slot
    valid = (slot >= txt_rows)[None, :] | (text_pos[None, :] < text_len[:, None])
    keys = piece[:, :, 0, :].reshape(batch, count, heads, HD)
    vals = piece[:, :, 1, :].reshape(batch, count, heads, HD)
    logit_scores = (
        jnp.einsum("bqhc,bkhc->bhqk", query_heads, keys, preferred_element_type=jnp.float32)
        * score_scale
    )
    logit_scores = jnp.where(valid[:, None, None, :], logit_scores, NEG)
    new_top = jnp.maximum(top, jnp.max(logit_scores, axis=3))
    attention_weights = jnp.where(
        valid[:, None, None, :], jnp.exp(logit_scores - new_top[..., None]), 0.0
    )
    total = jnp.sum(attention_weights, axis=3)
    summed_output = jnp.einsum(
        "bhqk,bkhc->bhqc",
        attention_weights.astype(jnp.bfloat16),
        vals,
        preferred_element_type=jnp.float32,
    )
    top, total, summed_output = (new_top, total, summed_output)
    attended_values = (summed_output / total[..., None]).astype(jnp.bfloat16)
    attended_values = attended_values.transpose(0, 2, 1, 3).reshape(batch, img_rows, columns)
    partial_output = jnp.einsum(
        "pxr,ro->pxo", attended_values, output_weight, preferred_element_type=jnp.float32
    )
    mixed_heads = lax.psum_scatter(
        partial_output.astype(jnp.bfloat16), "tp", scatter_dimension=2, tiled=True
    ).astype(jnp.float32)
    resid = local_mods[2][:, None, :] * mixed_heads
    flag = (refresh == 1)[:, None, None]
    new_cache = jnp.where(flag, resid, cache)
    out_img = img.astype(jnp.float32) + new_cache
    return (out_img, new_cache, rel_l1)


def solution(mesh):
    finer = Mesh(mesh.devices.reshape(4, 8, 2, mesh.shape["tp"]), ("seq_0", "seq_1", "seq_2", "tp"))
    in_specs = (
        P(None, SEQ, "tp"),
        P(None, SEQ, "tp"),
        P(None, SEQ, "tp"),
        P(None, SEQ, "tp"),
        P(None, None, "tp"),
        P(SEQ, None, "tp"),
        P(None, "tp"),
        P("tp", None),
        P(),
        P(),
    )
    out_specs = (P(None, SEQ, "tp"), P(None, SEQ, "tp"), P())
    return jax.shard_map(local, mesh=finer, in_specs=in_specs, out_specs=out_specs, check_vma=False)
```

profile of v0, /device:TPU:2, one launch (start us, length us, event | category | flops | bytes accessed | tf_op | source)
XLA Modules:
  0.0 297.1 jit_solution(4172694604840349083)
XLA Ops:
  7.2 0.0 all-gather.3.cloned.1.call-start
  7.2 0.7 all-gather.3.cloned.1.call-update
  7.9 0.0 all-gather.5.cloned.1.call-start
  8.0 0.7 reshape.138
  8.7 0.9 maximum_bitcast_fusion
  9.7 33.4 %all_gather.9 = bf16[3072,156]{0,1:T(8,128)(2,1)S(1)} all-gather(bf16[384,156]{0,1:T(8,128)(2,1)S(1)} %pad_maximum_fusion.1), channel_id=1, replica_groups=mesh['seq_0'=4,'seq_1'=8,'seq_2'=2,'tp'=8] {'tp'}, dimensions={0}, use_global_device_ids=true | all-gather | bytes 1078272 | tf_op jit(solution)/shard_map/all_gather | solution.py:22
  43.1 0.7 reshape.142
  43.8 1.4 slice_convert_fusion
  45.3 1.7 reshape.141
  46.9 0.2 bitcast_reduce_fusion
  47.1 0.4 multiply_reduce_fusion
  47.5 0.1 copy-done.6
  47.6 0.2 copy-done.3
  47.9 1.4 add_convert_fusion
  49.3 50.0 %all-gather.3.cloned.1.call-done = bf16[3072,3,256]{2,0,1:T(8,128)(2,1)} async-done(((bf16[48,3,256]{2,0,1:T(8,128)(2,1)}), bf16[3072,3,256]{2,0,1:T(8,128)(2,1)}) %all-gather.3.cloned.1.call-update) | async-done | bytes 4718608 | tf_op jit(solution)/shard_map/all_gather | solution.py:68
  99.3 3.6 %fusion = f32[4,36,3,256]{3,1,2,0:T(8,128)S(1)} fusion(bf16[3072,3,256]{2,0,1:T(8,128)(2,1)} %all-gather.3.cloned.1.call-done, bf16[4,36,3072]{2,1,0:T(8,128)(2,1)} %add_convert_fusion), kind=kOutput, calls=%fused_computation | convolution fusion | flops 679477248 | bytes 6045696 | tf_op jit(solution)/shard_map/btd,dkc->btkc/dot_general | solution.py:65
  103.0 0.1 reshape.146
  103.1 0.2 reduce_sum.66
  103.4 0.2 mul.102
  103.6 0.1 mul.103
  103.8 0.7 copy.54
  104.5 0.0 all-gather.5.cloned.1.call-update
  104.6 0.0 reduce-scatter.4.cloned.1.call-start
  104.7 0.1 compare_or_fusion
  104.8 0.1 reshape_squeeze.10
  104.8 0.2 multiply_reduce_fusion.1
  105.1 0.2 multiply_convert_fusion
  105.3 86.7 %all-gather.5.cloned.1.call-done = bf16[4,2304,2,256]{3,0,2,1:T(4,128)(2,1)} async-done(((bf16[4,36,2,256]{3,0,2,1:T(4,128)(2,1)}), bf16[4,2304,2,256]{3,0,2,1:T(4,128)(2,1)}) %all-gather.5.cloned.1.call-update) | async-done | bytes 9437200 | tf_op jit(solution)/shard_map/all_gather | solution.py:79
  192.0 10.4 %fusion.42 = (bf16[4,2304,1,256]{3,0,2,1:T(4,128)(2,1)}, bf16[4,2304,1,256]{3,0,2,1:T(4,128)(2,1)}) fusion(bf16[4,2304,2,256]{3,0,2,1:T(4,128)(2,1)} %all-gather.5.cloned.1.call-done), kind=kLoop, calls=%fused_computation.70 | loop fusion | bytes 18874368 | tf_op jit(solution)/shard_map/slice | solution.py:86
  202.5 8.5 %copy.68 = bf16[4,2304,1,256]{1,3,0,2:T(8,128)(2,1)} copy(bf16[4,2304,1,256]{3,0,2,1:T(4,128)(2,1)} %get-tuple-element.15) | data formatting | bytes 9437184
  211.0 4.6 %fusion.44 = (f32[4,2,32]{2,1,0:T(2,128)S(1)}, f32[4,2,32,2304]{3,2,1,0:T(8,128)}) fusion(bf16[4,2304,2,128]{1,3,2,0:T(8,128)(2,1)} %bitcast.67, bf16[4,32,2,128]{3,2,1,0:T(2,128)(2,1)S(1)} %multiply_convert_fusion, pred[4,2304]{1,0:T(4,128)(4,1)S(1)} %compare_or_fusion), kind=kOutput, calls=%fused_computation.72 | convolution fusion | flops 152764160 | bytes 7153664 | tf_op jit(solution)/shard_map/bqhc,bkhc->bhqk/dot_general | solution.py:89
  215.6 8.5 %copy.69 = bf16[4,2304,1,256]{1,3,0,2:T(8,128)(2,1)} copy(bf16[4,2304,1,256]{3,0,2,1:T(4,128)(2,1)} %get-tuple-element.16) | data formatting | bytes 9437184
  224.1 2.4 fusion.3
  226.5 4.1 %fusion.20 = bf16[4,2,4,8,128]{4,3,2,1,0:T(8,128)(2,1)S(1)} fusion(bf16[4,2304,2,128]{1,3,2,0:T(8,128)(2,1)} %bitcast.68, f32[4,2,32,2304]{3,2,1,0:T(8,128)S(1)} %copy-done.1, f32[4,2,32]{2,1,0:T(2,128)S(1)} %broadcast_maximum_fusion, pred[4,2304]{1,0:T(4,128)(4,1)S(1)} %compare_or_fusion, f32[4,32,2]{1,2,0:T(2,128)S(1)} %bitcast.72), kind=kOutput, calls=%fused_computation.20 | convolution fusion | flops 152829952 | bytes 7154688 | tf_op jit(solution)/shard_map/bhqk,bkhc->bhqc/dot_general | solution.py:98
  230.6 0.4 convolution_convert_fusion
  231.0 3.6 %copy.65 = bf16[4,32,3072]{1,0,2:T(4,128)(2,1)} copy(bf16[4,32,3072]{2,1,0:T(8,128)(2,1)S(1)} %convolution_convert_fusion) | data formatting | bytes 1572864
  234.6 4.8 %reshape.147 = bf16[3072,128]{1,0:T(8,128)(2,1)} reshape(bf16[3072,4,32]{2,1,0:T(4,128)(2,1)} %bitcast.69) | data formatting | bytes 1572864
  239.5 0.2 slice.53
  239.7 0.2 fusion.26
  239.8 9.5 %all-reduce.2 = (f32[4]{0:T(128)S(1)}, f32[4]{0:T(128)S(1)}) all-reduce(f32[4]{0:T(128)S(1)} %get-tuple-element.4, f32[4]{0:T(128)S(1)} %get-tuple-element.3), channel_id=1, replica_groups=mesh['seq_0'=4,'seq_1'=8,'seq_2'=2,'tp'=8] {'seq_0'}, use_global_device_ids=true, to_apply=%region_8.0 | all-reduce | flops 8 | bytes 64 | tf_op jit(solution)/shard_map/psum | solution.py:33
  249.4 16.3 %all-reduce.1 = (f32[4]{0:T(128)S(1)}, f32[4]{0:T(128)S(1)}) all-reduce(f32[4]{0:T(128)S(1)} %get-tuple-element.9, f32[4]{0:T(128)S(1)} %get-tuple-element.10), channel_id=1, replica_groups=mesh['seq_0'=4,'seq_1'=8,'seq_2'=2,'tp'=8] {'seq_1'}, use_global_device_ids=true, to_apply=%region_9.0 | all-reduce | flops 8 | bytes 64 | tf_op jit(solution)/shard_map/psum | solution.py:33
  265.7 2.5 all-reduce.3
  268.1 18.1 %all-reduce = (f32[4]{0:T(128)S(1)}, f32[4]{0:T(128)S(1)}) all-reduce(f32[4]{0:T(128)S(1)} %get-tuple-element.11, f32[4]{0:T(128)S(1)} %get-tuple-element.12), channel_id=1, replica_groups=mesh['seq_0'=4,'seq_1'=8,'seq_2'=2,'tp'=8] {'tp'}, use_global_device_ids=true, to_apply=%region_11.0 | all-reduce | flops 8 | bytes 64 | tf_op jit(solution)/shard_map/psum | solution.py:33
  286.2 0.5 maximum_divide_fusion
  286.7 0.7 bitcast_convert_fusion
  287.4 1.1 reshape.148
  288.5 0.2 copy.66
  288.8 1.8 convert_add_fusion
  (37 shorter events, 0.3 us)
Async XLA Ops:
  7.2 223.5 %copy-start = (bf16[256,3072]{1,0:T(8,128)(2,1)S(1)}, bf16[256,3072]{1,0:T(8,128)(2,1)}, u32[]{:S(2)}) copy-start(bf16[256,3072]{1,0:T(8,128)(2,1)} %param.17) | copy-start | bytes 4718596
  7.2 92.1 %all-gather.3.cloned.1.call-start = ((), (), s32[]{:S(2)}) async-start(), calls=%async_computation.1 | async-start | bytes 4792320 | tf_op jit(solution)/shard_map/all_gather | solution.py:68
  7.9 184.1 %all-gather.5.cloned.1.call-start = ((), (), s32[]{:S(2)}) async-start(), calls=%async_computation.2 | async-start | bytes 9584640 | tf_op jit(solution)/shard_map/all_gather | solution.py:79
  46.9 0.7 copy-start.6
  46.9 0.9 copy-start.3
  102.9 1.7 copy-start.7
  104.6 182.9 %reduce-scatter.4.cloned.1.call-start = ((), (), s32[]{:S(2)}) async-start(), calls=%async_computation.3 | async-start | bytes 884736
  224.1 2.4 copy-start.1
  234.6 4.8 %copy-start.2 = (bf16[4,36,3072]{2,1,0:T(8,128)(2,1)S(1)}, bf16[4,36,3072]{2,1,0:T(8,128)(2,1)}, u32[]{:S(2)}) copy-start(bf16[4,36,3072]{2,1,0:T(8,128)(2,1)} %add_convert_fusion) | copy-start | bytes 2654212
  234.6 5.0 %copy-start.5 = (bf16[4,32,384]{2,1,0:T(8,128)(2,1)S(1)}, bf16[4,32,384]{2,1,0:T(8,128)(2,1)}, u32[]{:S(2)}) copy-start(bf16[4,32,384]{2,1,0:T(8,128)(2,1)} %param.12) | copy-start | bytes 294916
  234.6 51.6 %copy-start.8 = (s32[4]{0:T(128)S(1)}, s32[4]{0:T(128)}, u32[]{:S(2)}) copy-start(s32[4]{0:T(128)} %param.19) | copy-start | bytes 52
  239.4 49.4 %copy-start.4 = (bf16[4,32,384]{2,1,0:T(8,128)(2,1)S(1)}, bf16[4,32,384]{2,1,0:T(8,128)(2,1)}, u32[]{:S(2)}) copy-start(bf16[4,32,384]{2,1,0:T(8,128)(2,1)} %param.10) | copy-start | bytes 294916
Sparse Core Ops, SparseCore 0:
  11.4 87.8 all-gather.2
  104.7 87.3 all-gather.4
  239.6 40.5 reduce-scatter.3
where the time goes:
time: 298 us; the launch traced here: 297 us
  waiting for transfers between devices  137 us (46%)
  blocking collectives  79.8 us (27%)
  local copies, waits for them, and re-layouts  42.1 us (14%)
  between operations  14 us (5%)
  matrix products  12.8 us (4%)
  other arithmetic  10.8 us (4%)
    all_gather x1, waiting for transfers between devices, local(): piece = lax.all_gather(paired, SEQ, axis=1, tiled=True)  86.7 us
    all_gather x1, waiting for transfers between devices, local(): lax.all_gather(w_qkv, SEQ, axis=0, tiled=True)  50 us
    psum x4, blocking collectives, one_axis_at_a_time(): return functools.reduce(lax.psum, axes, value)  46.4 us
    all_gather x1, blocking collectives, turned_gather(): out = lax.all_gather(both, axis, axis=0, tiled=True)  33.4 us
    unnamed x24, local copies, waits for them, and re-layouts  27.1 us
    slice x1, local copies, waits for them, and re-layouts, local(): keys = piece[:, :, 0, :].reshape(batch, count, heads, HD)  10.4 us
  transfers between devices with their start and end apart: 3, of which 2 were waited for; matrix products, arithmetic and copies ran while one was open for 3% of the time, Pallas kernels for 0%

commit v1 on v0

v1 whole, which is shorter than its diff:
```python
import functools

import jax
import jax.numpy as jnp
from jax import lax
from jax.experimental import pallas as pl
from jax.experimental.pallas import tpu as pltpu
from jax.sharding import Mesh
from jax.sharding import PartitionSpec as P

HD = 128
SEQ = ("seq_0", "seq_1", "seq_2")
EPS = 0.1
NEG = -1e30
F32 = jnp.float32
BF16 = jnp.bfloat16

IMG_R = 32
TXT_R = 4
ROWS = 40
REL_ROW = IMG_R + TXT_R

VMEM = pl.BlockSpec(memory_space=pltpu.VMEM)
SMEM = pl.BlockSpec(memory_space=pltpu.SMEM)


def call(body, out_shape, in_specs, limit=40 << 20):
    outs = jax.tree.map(lambda _: VMEM, out_shape)
    return pl.pallas_call(
        body,
        out_shape=out_shape,
        in_specs=in_specs,
        out_specs=outs,
        compiler_params=pltpu.CompilerParams(vmem_limit_bytes=limit),
    )


def swap(value, axis):
    return lax.all_to_all(value, axis, 0, 0, tiled=True)


def spread_copies(value, count):
    return jnp.broadcast_to(value[None], (count,) + value.shape)


def split_three(value):
    high = value.astype(BF16).astype(F32)
    rest = value - high
    middle = rest.astype(BF16).astype(F32)
    return high, middle, rest - middle


def norm_body(tp_ref, x_ref, prev_ref, mod_ref, rel_ref):
    groups, rows, width = x_ref.shape
    batch = rows // ROWS
    features = groups * width
    sums = jnp.zeros((rows, 1), F32)
    for g in range(groups):
        sums = sums + jnp.sum(x_ref[g].astype(F32), axis=1, keepdims=True)
    center = sums / features
    squares = jnp.zeros((rows, 1), F32)
    for g in range(groups):
        squares = squares + jnp.sum(
            jnp.square(x_ref[g].astype(F32) - center), axis=1, keepdims=True
        )
    inv = lax.rsqrt(squares / features + EPS)
    for g in range(groups):
        normed = (x_ref[g].astype(F32) - center) * inv
        values = x_ref[g].astype(F32)
        parts = []
        for b in range(batch):
            at = b * ROWS
            shift = values[at + REL_ROW : at + REL_ROW + 1]
            scale = values[at + REL_ROW + 1 : at + REL_ROW + 2]
            parts.append(normed[at : at + ROWS] * (1.0 + scale) + shift)
        mod_ref[g] = jnp.concatenate(parts, axis=0).astype(BF16)
    own = mod_ref[tp_ref[0]].astype(F32)
    lane = lax.broadcasted_iota(jnp.int32, (8, 128), 1)
    rel = jnp.zeros((8, 128), F32)
    for b in range(batch):
        previous = prev_ref[b].astype(F32)
        gap = jnp.abs(own[b * ROWS : b * ROWS + IMG_R] - previous)
        rel = jnp.where(lane == b, jnp.sum(gap), rel)
        rel = jnp.where(lane == batch + b, jnp.sum(jnp.abs(previous)), rel)
    rel_ref[...] = rel


def project_body(mod_ref, w_ref, gain_ref, rel_ref, out_ref):
    groups, rows, width = mod_ref.shape
    cores, xs, ys, kinds, deep, columns = w_ref.shape
    batch = rows // ROWS
    heads = columns // HD
    high, middle, low = split_three(rel_ref[0:1, :])
    row = lax.broadcasted_iota(jnp.int32, (ROWS, HD), 0)
    per_group = width // (cores * deep)
    for kind in range(kinds):
        total = jnp.zeros((rows, columns), F32)
        for g in range(groups):
            pieces = []
            for step in range(per_group):
                flat = g * per_group + step
                for core in range(cores):
                    pieces.append(w_ref[core, flat // ys, flat % ys, kind])
            total = total + jnp.dot(
                mod_ref[g], jnp.concatenate(pieces, axis=0), preferred_element_type=F32
            )
        for h in range(heads):
            part = total[:, h * HD : (h + 1) * HD]
            if kind < 2:
                mean = jnp.mean(jnp.square(part), axis=1, keepdims=True)
                part = part * lax.rsqrt(mean + EPS) * gain_ref[kind : kind + 1, h * HD : (h + 1) * HD]
            for b in range(batch):
                block = part[b * ROWS : (b + 1) * ROWS]
                if kind == 1:
                    block = jnp.where(row == REL_ROW, high, block)
                    block = jnp.where(row == REL_ROW + 1, middle, block)
                    block = jnp.where(row == REL_ROW + 2, low, block)
                out_ref[b * heads + h, :, kind * HD : (kind + 1) * HD] = block.astype(BF16)


def attend_body(limit_ref, qkv_ref, kv_ref, out_ref, rel_ref):
    ys = qkv_ref.shape[0]
    spots = kv_ref.shape[0]
    count = spots * ys * ROWS
    query = jnp.concatenate([qkv_ref[y, :IMG_R, :HD] for y in range(ys)], axis=0)
    pairs = kv_ref[...].reshape(count, 2 * HD)
    keys = pairs[:, :HD]
    values = pairs[:, HD:]
    scores = lax.dot_general(
        query, keys, (((1,), (1,)), ((), ())), preferred_element_type=F32
    ) * (1.0 / HD**0.5)
    index = lax.broadcasted_iota(jnp.int32, (1, count), 1)
    slot = index % ROWS
    block = index // ROWS
    y = block % ys
    spot = block // ys
    place = (spot // 2) * (2 * ys) + y * 2 + spot % 2
    text = place * TXT_R + slot - IMG_R
    valid = (slot < IMG_R) | ((slot < IMG_R + TXT_R) & (text < limit_ref[0]))
    scores = jnp.where(valid, scores, NEG)
    top = jnp.max(scores, axis=1, keepdims=True)
    weights = jnp.where(valid, jnp.exp(scores - top), 0.0)
    total = jnp.sum(weights, axis=1, keepdims=True)
    summed = jnp.dot(weights.astype(BF16), values, preferred_element_type=F32)
    attended = (summed / total).astype(BF16)
    for y in range(ys):
        out_ref[y] = attended[y * IMG_R : (y + 1) * IMG_R]
    down = lax.broadcasted_iota(jnp.int32, (ROWS, HD), 0)
    held = (down >= REL_ROW) & (down < REL_ROW + 3)
    rel = jnp.zeros((1, HD), F32)
    for spot in range(spots):
        for y in range(ys):
            block = kv_ref[spot, y, :, :HD].astype(F32)
            rel = rel + jnp.sum(jnp.where(held, block, 0.0), axis=0, keepdims=True)
    rel_ref[...] = jnp.broadcast_to(rel, (8, HD))


def mix_body(att_ref, w_ref, rel_ref, out_ref):
    pairs = att_ref.shape[0]
    groups, _, width = out_ref.shape
    heads = w_ref.shape[0] // HD
    batch = pairs // heads
    rows = batch * IMG_R
    lefts = []
    for h in range(heads):
        lefts.append(jnp.concatenate([att_ref[b * heads + h] for b in range(batch)], axis=0))
    left = jnp.concatenate(lefts, axis=1)
    high, middle, low = split_three(rel_ref[0:1, :])
    row = lax.broadcasted_iota(jnp.int32, (8, HD), 0)
    tail = jnp.where(row == 0, high, jnp.where(row == 1, middle, jnp.where(row == 2, low, 0.0)))
    tail = jnp.concatenate([tail, jnp.zeros((8, width - HD), F32)], axis=1).astype(BF16)
    for g in range(groups):
        mixed = jnp.dot(left, w_ref[:, g * width : (g + 1) * width], preferred_element_type=F32)
        out_ref[g, :rows] = mixed.astype(BF16)
        out_ref[g, rows:] = tail


def final_body(flag_ref, part_ref, cache_ref, img_ref, mod_ref, out_ref, new_ref, rel_ref):
    groups = part_ref.shape[0]
    batch = img_ref.shape[0]
    rows = batch * IMG_R
    mixed = part_ref[0, :rows].astype(F32)
    rel = part_ref[0, rows:, :HD].astype(F32)
    for g in range(1, groups):
        mixed = mixed + part_ref[g, :rows].astype(F32)
        rel = rel + part_ref[g, rows:, :HD].astype(F32)
    for b in range(batch):
        gate = mod_ref[2, b : b + 1].astype(F32)
        resid = gate * mixed[b * IMG_R : (b + 1) * IMG_R]
        fresh = jnp.where(flag_ref[b] == 1, resid, cache_ref[b])
        new_ref[b] = fresh
        out_ref[b] = img_ref[b].astype(F32) + fresh
    sums = jnp.sum(rel, axis=0, keepdims=True)
    lane = lax.broadcasted_iota(jnp.int32, (1, HD), 1)
    ratio = jnp.zeros((8, HD), F32)
    for b in range(batch):
        numer = jnp.sum(jnp.where(lane == b, sums, 0.0), axis=1, keepdims=True)
        denom = jnp.sum(jnp.where(lane == batch + b, sums, 0.0), axis=1, keepdims=True)
        wide = lax.broadcasted_iota(jnp.int32, (8, HD), 1)
        ratio = jnp.where(wide == b, numer / jnp.maximum(denom, 1.0), ratio)
    rel_ref[...] = ratio


def local(img, txt, prev_mod, cache, modulation, w_qkv, qk_gain, output_weight, text_len, refresh):
    batch, img_rows, width = img.shape
    xs, ys, cores = (lax.axis_size(a) for a in SEQ)
    tps = lax.axis_size("tp")
    kinds, columns = w_qkv.shape[1:]
    deep = w_qkv.shape[0]
    heads = columns // HD

    with jax.named_scope("xgather"):
        pads = jnp.zeros((batch, ROWS - img_rows - txt.shape[1] - 2, width), BF16)
        joined = jnp.concatenate(
            [img, txt, modulation[0][:, None], modulation[1][:, None], pads], axis=1
        ).reshape(batch * ROWS, width)
        wide = swap(spread_copies(joined, tps), "tp")

    with jax.named_scope("wy"):
        weight = w_qkv.transpose(1, 0, 2)
        weight = swap(spread_copies(weight, ys), "seq_1")
    with jax.named_scope("wx"):
        weight = swap(spread_copies(weight, xs).reshape(xs, ys * kinds * deep, columns), "seq_0")
    with jax.named_scope("wc"):
        weight = swap(
            spread_copies(weight.reshape(xs * ys * kinds * deep, columns), cores), "seq_2"
        )
        weight = weight.reshape(cores, xs, ys, kinds, deep, columns)

    tp_index = lax.axis_index("tp").astype(jnp.int32)[None]
    modded, rel = call(
        norm_body,
        (
            jax.ShapeDtypeStruct((tps, batch * ROWS, width), BF16),
            jax.ShapeDtypeStruct((8, 128), F32),
        ),
        [SMEM, VMEM, VMEM],
    )(tp_index, wide, prev_mod)

    pairs = call(
        project_body,
        jax.ShapeDtypeStruct((batch * heads, ROWS, kinds * HD), BF16),
        [VMEM] * 4,
    )(modded, weight, qk_gain, rel)

    with jax.named_scope("qkvy"):
        pairs = swap(pairs, "seq_1")
    with jax.named_scope("kvxc"):
        gathered = swap(spread_copies(pairs[:, :, HD:], xs * cores), ("seq_0", "seq_2"))

    mine = lax.axis_index("seq_1") // heads
    limit = lax.dynamic_slice_in_dim(text_len, mine, 1)
    attended, rel = call(
        attend_body,
        (
            jax.ShapeDtypeStruct((ys, IMG_R, HD), BF16),
            jax.ShapeDtypeStruct((8, HD), F32),
        ),
        [SMEM, VMEM, VMEM],
    )(limit, pairs, gathered)

    with jax.named_scope("atty"):
        attended = swap(attended, "seq_1")
    parts = call(
        mix_body,
        jax.ShapeDtypeStruct((tps, batch * IMG_R + 8, width), BF16),
        [VMEM] * 3,
    )(attended, output_weight, rel)
    with jax.named_scope("mixz"):
        parts = swap(parts, "tp")

    shape = jax.ShapeDtypeStruct((batch, img_rows, width), F32)
    out_img, new_cache, ratio = call(
        final_body,
        (shape, shape, jax.ShapeDtypeStruct((8, HD), F32)),
        [SMEM, VMEM, VMEM, VMEM, VMEM],
    )(refresh, parts, cache, img, modulation)
    return (out_img, new_cache, ratio[0, :batch])


def solution(mesh):
    finer = Mesh(mesh.devices.reshape(4, 8, 2, mesh.shape["tp"]), ("seq_0", "seq_1", "seq_2", "tp"))
    in_specs = (
        P(None, SEQ, "tp"),
        P(None, SEQ, "tp"),
        P(None, SEQ, "tp"),
        P(None, SEQ, "tp"),
        P(None, None, "tp"),
        P(SEQ, None, "tp"),
        P(None, "tp"),
        P("tp", None),
        P(),
        P(),
    )
    out_specs = (P(None, SEQ, "tp"), P(None, SEQ, "tp"), P())
    return jax.shard_map(local, mesh=finer, in_specs=in_specs, out_specs=out_specs, check_vma=False)
```

time: 298 us -> 190 us (0.64)
  waiting for transfers between devices: 137 us -> 58.7 us
  local copies, waits for them, and re-layouts: 42.1 us -> 10.1 us
  starting transfers between devices: 0.12 us -> 17.3 us
  blocking collectives: 79.8 us -> 95.9 us
  between operations: 14 us -> 0.76 us
  matrix products: 12.8 us -> 0 us
  other arithmetic: 10.8 us -> 0 us
  Pallas kernels: 0 us -> 6.65 us
    all_gather x2 -> x0, waiting for transfers between devices: 137 us -> none  [the longest x1 86.7 us: local(): piece = lax.all_gather(paired, SEQ, axis=1, tiled=True)]
    all_to_all x0 -> x5, blocking collectives: none -> 95.9 us  [swap(): return lax.all_to_all(value, axis, 0, 0, tiled=True)]
    all_to_all x0 -> x3, waiting for transfers between devices: none -> 58.7 us  [swap(): return lax.all_to_all(value, axis, 0, 0, tiled=True)]
    psum x4 -> x0, blocking collectives: 46.4 us -> none  [one_axis_at_a_time(): return functools.reduce(lax.psum, axes, value)]
    all_gather x1 -> x0, blocking collectives: 33.4 us -> none  [turned_gather(): out = lax.all_gather(both, axis, axis=0, tiled=True)]
    unnamed x24 -> x16, local copies, waits for them, and re-layouts: 27.1 us -> 0.05 us
    all_to_all x0 -> x3, starting transfers between devices: none -> 17.3 us  [swap(): return lax.all_to_all(value, axis, 0, 0, tiled=True)]
    dot_general x4 -> x0, matrix products: 12.8 us -> none  [the longest x1 4.63 us: local(): jnp.einsum('bqhc,bkhc->bhqk', query_heads, keys, preferred_element_type=j...]
  transfers between devices with their start and end apart: 3 -> 3, of which waited for: 2 -> 3; matrix products, arithmetic and copies ran while one was open for 3% -> 2% of each run, Pallas kernels for 0% -> 1%
where the time goes in v1:
time: 190 us; the launch traced here: 189 us
  blocking collectives  95.9 us (50%)
  waiting for transfers between devices  58.7 us (31%)
  starting transfers between devices  17.3 us (9%)
  local copies, waits for them, and re-layouts  10.1 us (5%)
  Pallas kernels  6.65 us (4%)
    all_to_all x5, blocking collectives, swap(): return lax.all_to_all(value, axis, 0, 0, tiled=True)  95.9 us
    all_to_all x3, waiting for transfers between devices, swap(): return lax.all_to_all(value, axis, 0, 0, tiled=True)  58.7 us
    all_to_all x3, starting transfers between devices, swap(): return lax.all_to_all(value, axis, 0, 0, tiled=True)  17.3 us
    broadcast_in_dim x5, local copies, waits for them, and re-layouts, spread_copies(): return jnp.broadcast_to(value[None], (count,) + value.shape)  6.53 us
  transfers between devices with their start and end apart: 3, of which 3 were waited for; matrix products, arithmetic and copies ran while one was open for 2% of the time, Pallas kernels for 1%

profile of v1, /device:TPU:2, one launch (start us, length us, event | category | flops | bytes accessed | tf_op | source)
XLA Modules:
  0.0 189.4 jit_solution(13120022701643416174)
XLA Ops:
  0.6 1.7 broadcast_in_dim.44
  2.4 7.1 %all-to-all-start.1 = ((bf16[8,3,48,256]{3,2,1,0:T(8,128)(2,1)}), bf16[8,3,48,256]{3,2,1,0:T(8,128)(2,1)S(1)}, u32[]{:S(2)}, u32[]{:S(2)}) async-start(bf16[8,3,48,256]{3,2,1,0:T(8,128)(2,1)} %broadcast_in_dim.44), calls=%async_computation.1 | async-start | bytes 1179648 | tf_op jit(solution)/shard_map/wy/all_to_all | solution.py:39
  9.5 0.7 slice_bitcast_fusion
  10.2 1.7 concatenate.3
  11.9 16.5 %all-to-all-done.1 = bf16[8,3,48,256]{3,2,1,0:T(8,128)(2,1)S(1)} async-done(((bf16[8,3,48,256]{3,2,1,0:T(8,128)(2,1)}), bf16[8,3,48,256]{3,2,1,0:T(8,128)(2,1)S(1)}, u32[]{:S(2)}, u32[]{:S(2)}) %all-to-all-start.1) | async-done | bytes 589856 | tf_op jit(solution)/shard_map/wy/all_to_all | solution.py:39
  28.4 0.1 broadcast_in_dim.43
  28.5 37.6 %all_to_all.40.x_ref = bf16[8,160,384]{2,1,0:T(8,128)(2,1)S(1)} all-to-all(bf16[8,160,384]{2,1,0:T(8,128)(2,1)S(1)} %broadcast_in_dim.43), channel_id=1, replica_groups=mesh['seq_0'=4,'seq_1'=8,'seq_2'=2,'tp'=8] {'tp'}, dimensions={0} | all-to-all | bytes 1966080 | tf_op jit(solution)/shard_map/xgather/all_to_all | solution.py:39
  66.1 1.6 broadcast_in_dim.46
  67.7 0.0 copy-start.3
  67.7 5.1 %all-to-all-start.2 = ((bf16[4,1152,256]{2,1,0:T(8,128)(2,1)}), bf16[4,1152,256]{2,1,0:T(8,128)(2,1)}, u32[]{:S(2)}, u32[]{:S(2)}) async-start(bf16[4,1152,256]{2,1,0:T(8,128)(2,1)} %broadcast_in_dim.46), calls=%async_computation.2 | async-start | bytes 4718592 | tf_op jit(solution)/shard_map/wx/all_to_all | solution.py:39
  72.8 0.0 copy-done.3
  72.8 1.3 shard_map.121
  74.1 25.5 %all-to-all-done.2 = bf16[4,1152,256]{2,1,0:T(8,128)(2,1)} async-done(((bf16[4,1152,256]{2,1,0:T(8,128)(2,1)}), bf16[4,1152,256]{2,1,0:T(8,128)(2,1)}, u32[]{:S(2)}, u32[]{:S(2)}) %all-to-all-start.2) | async-done | bytes 2359328 | tf_op jit(solution)/shard_map/wx/all_to_all | solution.py:39
  99.6 2.0 %broadcast_in_dim.48 = bf16[2,4608,256]{2,1,0:T(8,128)(2,1)S(1)} broadcast(bf16[4608,256]{1,0:T(8,128)(2,1)} %bitcast.6), dimensions={1,2} | broadcast | bytes 7077888 | tf_op jit(solution)/shard_map/wc/broadcast_in_dim | solution.py:43
  101.5 0.0 copy-start.5
  101.6 7.5 %all_to_all.41 = bf16[2,4608,256]{2,1,0:T(8,128)(2,1)S(1)} all-to-all(bf16[2,4608,256]{2,1,0:T(8,128)(2,1)S(1)} %broadcast_in_dim.48), channel_id=1, replica_groups=mesh['seq_0'=4,'seq_1'=8,'seq_2'=2,'tp'=8] {'seq_2'}, dimensions={0} | all-to-all | bytes 9437184 | tf_op jit(solution)/shard_map/wc/all_to_all | solution.py:39
  109.1 0.0 copy-done.5
  109.1 1.2 shard_map.122
  110.3 0.0 copy-start.7
  110.3 14.5 %all_to_all.42.qkv_ref = bf16[8,40,384]{2,1,0:T(8,128)(2,1)S(1)} all-to-all(bf16[8,40,384]{2,1,0:T(8,128)(2,1)S(1)} %shard_map.122), channel_id=1, replica_groups=mesh['seq_0'=4,'seq_1'=8,'seq_2'=2,'tp'=8] {'seq_1'}, dimensions={0} | all-to-all | bytes 491520 | tf_op jit(solution)/shard_map/qkvy/all_to_all | solution.py:39
  124.8 1.2 broadcast_in_dim.49
  126.0 0.0 copy-start
  126.0 5.1 %all-to-all-start.5 = ((bf16[8,8,40,256]{3,2,1,0:T(8,128)(2,1)}), bf16[8,8,40,256]{3,2,1,0:T(8,128)(2,1)S(1)}, u32[]{:S(2)}, u32[]{:S(2)}) async-start(bf16[8,8,40,256]{3,2,1,0:T(8,128)(2,1)} %broadcast_in_dim.49), calls=%async_computation.5 | async-start | bytes 2621440 | tf_op jit(solution)/shard_map/kvxc/all_to_all | solution.py:39
  131.1 0.0 copy-done.7
  131.1 0.6 dynamic_slice.3.limit_ref
  131.7 16.7 %all-to-all-done.5.kv_ref = bf16[8,8,40,256]{3,2,1,0:T(8,128)(2,1)S(1)} async-done(((bf16[8,8,40,256]{3,2,1,0:T(8,128)(2,1)}), bf16[8,8,40,256]{3,2,1,0:T(8,128)(2,1)S(1)}, u32[]{:S(2)}, u32[]{:S(2)}) %all-to-all-start.5) | async-done | bytes 1310752 | tf_op jit(solution)/shard_map/kvxc/all_to_all | solution.py:39
  148.4 2.3 %shard_map.123 = (bf16[8,32,128]{2,1,0:T(8,128)(2,1)S(1)}, f32[8,128]{1,0:T(8,128)S(1)}) custom-call(s32[1]{0:T(128)} %dynamic_slice.3.limit_ref, bf16[8,40,384]{2,1,0:T(8,128)(2,1)S(1)} %all_to_all.42.qkv_ref, bf16[8,8,40,256]{3,2,1,0:T(8,128)(2,1)S(1)} %all-to-all-done.5.kv_ref), custom_call_target="tpu_custom_call" | custom-call | tf_op jit(solution)/shard_map/pallas_call | solution.py:253
  150.7 0.0 copy-start.1
  150.7 0.0 copy-start.2
  150.7 0.0 copy-start.4
  150.7 0.0 copy-start.6
  150.7 10.9 %all_to_all.43.att_ref = bf16[8,32,128]{2,1,0:T(8,128)(2,1)S(1)} all-to-all(bf16[8,32,128]{2,1,0:T(8,128)(2,1)S(1)} %get-tuple-element.12), channel_id=1, replica_groups=mesh['seq_0'=4,'seq_1'=8,'seq_2'=2,'tp'=8] {'seq_1'}, dimensions={0} | all-to-all | bytes 131072 | tf_op jit(solution)/shard_map/atty/all_to_all | solution.py:39
  161.6 0.0 copy-done
  161.6 0.4 shard_map.124
  162.1 25.4 %all_to_all.44.part_ref = bf16[8,136,384]{2,1,0:T(8,128)(2,1)S(1)} all-to-all(bf16[8,136,384]{2,1,0:T(8,128)(2,1)S(1)} %shard_map.124), channel_id=1, replica_groups=mesh['seq_0'=4,'seq_1'=8,'seq_2'=2,'tp'=8] {'tp'}, dimensions={0} | all-to-all | bytes 1671168 | tf_op jit(solution)/shard_map/mixz/all_to_all | solution.py:39
  187.5 0.0 copy-done.1
  187.5 0.0 copy-done.2
  187.5 0.0 copy-done.4
  187.5 0.0 copy-done.6
  187.5 1.5 shard_map.125
  188.9 0.5 slice_bitcast_fusion.2
  (4 shorter events, 0.0 us)
Async XLA Ops:
  2.4 26.0 %all-to-all-start.1 = ((bf16[8,3,48,256]{3,2,1,0:T(8,128)(2,1)}), bf16[8,3,48,256]{3,2,1,0:T(8,128)(2,1)S(1)}, u32[]{:S(2)}, u32[]{:S(2)}) async-start(bf16[8,3,48,256]{3,2,1,0:T(8,128)(2,1)} %broadcast_in_dim.44), calls=%async_computation.1 | async-start | bytes 1179648 | tf_op jit(solution)/shard_map/wy/all_to_all | solution.py:39
  67.7 5.1 %copy-start.3 = (bf16[4,32,384]{2,1,0:T(8,128)(2,1)S(1)}, bf16[4,32,384]{2,1,0:T(8,128)(2,1)}, u32[]{:S(2)}) copy-start(bf16[4,32,384]{2,1,0:T(8,128)(2,1)} %prev_ref.1) | copy-start | bytes 294916
  67.7 31.9 %all-to-all-start.2 = ((bf16[4,1152,256]{2,1,0:T(8,128)(2,1)}), bf16[4,1152,256]{2,1,0:T(8,128)(2,1)}, u32[]{:S(2)}, u32[]{:S(2)}) async-start(bf16[4,1152,256]{2,1,0:T(8,128)(2,1)} %broadcast_in_dim.46), calls=%async_computation.2 | async-start | bytes 4718592 | tf_op jit(solution)/shard_map/wx/all_to_all | solution.py:39
  101.5 7.5 %copy-start.5 = (f32[2,256]{1,0:T(2,128)S(1)}, f32[2,256]{1,0:T(2,128)}, u32[]{:S(2)}) copy-start(f32[2,256]{1,0:T(2,128)} %gain_ref.1) | copy-start | bytes 6148
  110.3 20.8 %copy-start.7 = (s32[4]{0:T(128)S(1)}, s32[4]{0:T(128)}, u32[]{:S(2)}) copy-start(s32[4]{0:T(128)} %param.18) | copy-start | bytes 52
  126.0 35.6 %copy-start = (bf16[256,3072]{1,0:T(8,128)(2,1)S(1)}, bf16[256,3072]{1,0:T(8,128)(2,1)}, u32[]{:S(2)}) copy-start(bf16[256,3072]{1,0:T(8,128)(2,1)} %w_ref.1) | copy-start | bytes 4718596
  126.0 22.4 %all-to-all-start.5 = ((bf16[8,8,40,256]{3,2,1,0:T(8,128)(2,1)}), bf16[8,8,40,256]{3,2,1,0:T(8,128)(2,1)S(1)}, u32[]{:S(2)}, u32[]{:S(2)}) async-start(bf16[8,8,40,256]{3,2,1,0:T(8,128)(2,1)} %broadcast_in_dim.49), calls=%async_computation.5 | async-start | bytes 2621440 | tf_op jit(solution)/shard_map/kvxc/all_to_all | solution.py:39
  150.7 36.8 %copy-start.1 = (bf16[4,32,384]{2,1,0:T(8,128)(2,1)S(1)}, bf16[4,32,384]{2,1,0:T(8,128)(2,1)}, u32[]{:S(2)}) copy-start(bf16[4,32,384]{2,1,0:T(8,128)(2,1)} %img_ref.1) | copy-start | bytes 294916
  150.7 36.8 %copy-start.2 = (f32[4,32,384]{2,1,0:T(8,128)S(1)}, f32[4,32,384]{2,1,0:T(8,128)}, u32[]{:S(2)}) copy-start(f32[4,32,384]{2,1,0:T(8,128)} %cache_ref.1) | copy-start | bytes 589828
  150.7 36.7 %copy-start.4 = (bf16[3,4,384]{2,1,0:T(4,128)(2,1)S(1)}, bf16[3,4,384]{2,1,0:T(4,128)(2,1)}, u32[]{:S(2)}) copy-start(bf16[3,4,384]{2,1,0:T(4,128)(2,1)} %mod_ref.1) | copy-start | bytes 27652
  150.7 36.7 %copy-start.6 = (s32[4]{0:T(128)S(1)}, s32[4]{0:T(128)}, u32[]{:S(2)}) copy-start(s32[4]{0:T(128)} %flag_ref.1) | copy-start | bytes 52

commit v2 on v1

--- a/solution.py
+++ b/solution.py
@@ -1,5 +1,3 @@
-import functools
-
 import jax
 import jax.numpy as jnp
 from jax import lax
@@ -7,6 +5,7 @@
 from jax.experimental.pallas import tpu as pltpu
 from jax.sharding import Mesh
 from jax.sharding import PartitionSpec as P
+
 
 HD = 128
 SEQ = ("seq_0", "seq_1", "seq_2")
@@ -85,9 +84,20 @@
     rel_ref[...] = rel
 
 
-def project_body(mod_ref, w_ref, gain_ref, rel_ref, out_ref):
+def project_body(core_ref, mod_ref, own_ref, other_ref, gain_ref, rel_ref, out_ref):
+    @pl.when(core_ref[0] == 0)
+    def _():
+        project(mod_ref, (own_ref, other_ref), gain_ref, rel_ref, out_ref)
+
+    @pl.when(core_ref[0] == 1)
+    def _():
+        project(mod_ref, (other_ref, own_ref), gain_ref, rel_ref, out_ref)
+
+
+def project(mod_ref, w_refs, gain_ref, rel_ref, out_ref):
     groups, rows, width = mod_ref.shape
-    cores, xs, ys, kinds, deep, columns = w_ref.shape
+    cores = len(w_refs)
+    _, ys, kinds, deep, columns = w_refs[0].shape
     batch = rows // ROWS
     heads = columns // HD
     high, middle, low = split_three(rel_ref[0:1, :])
@@ -100,7 +110,7 @@
             for step in range(per_group):
                 flat = g * per_group + step
                 for core in range(cores):
-                    pieces.append(w_ref[core, flat // ys, flat % ys, kind])
+                    pieces.append(w_refs[core][flat // ys, flat % ys, kind])
             total = total + jnp.dot(
                 mod_ref[g], jnp.concatenate(pieces, axis=0), preferred_element_type=F32
             )
@@ -209,25 +219,20 @@
     deep = w_qkv.shape[0]
     heads = columns // HD
 
-    with jax.named_scope("xgather"):
-        pads = jnp.zeros((batch, ROWS - img_rows - txt.shape[1] - 2, width), BF16)
-        joined = jnp.concatenate(
-            [img, txt, modulation[0][:, None], modulation[1][:, None], pads], axis=1
-        ).reshape(batch * ROWS, width)
-        wide = swap(spread_copies(joined, tps), "tp")
-
-    with jax.named_scope("wy"):
-        weight = w_qkv.transpose(1, 0, 2)
-        weight = swap(spread_copies(weight, ys), "seq_1")
-    with jax.named_scope("wx"):
-        weight = swap(spread_copies(weight, xs).reshape(xs, ys * kinds * deep, columns), "seq_0")
-    with jax.named_scope("wc"):
-        weight = swap(
-            spread_copies(weight.reshape(xs * ys * kinds * deep, columns), cores), "seq_2"
-        )
-        weight = weight.reshape(cores, xs, ys, kinds, deep, columns)
+    pads = jnp.zeros((batch, ROWS - img_rows - txt.shape[1] - 2, width), BF16)
+    joined = jnp.concatenate(
+        [img, txt, modulation[0][:, None], modulation[1][:, None], pads], axis=1
+    ).reshape(batch * ROWS, width)
+    wide = lax.all_gather(joined, "tp", axis=0, tiled=False)
+
+    weight = w_qkv.transpose(1, 0, 2)
+    weight = swap(spread_copies(weight, ys), "seq_1")
+    weight = swap(spread_copies(weight, xs).reshape(xs, ys * kinds * deep, columns), "seq_0")
+    weight = weight.reshape(xs, ys, kinds, deep, columns)
+    other = lax.ppermute(weight, "seq_2", [(0, 1), (1, 0)])
 
     tp_index = lax.axis_index("tp").astype(jnp.int32)[None]
+    core_index = lax.axis_index("seq_2").astype(jnp.int32)[None]
     modded, rel = call(
         norm_body,
         (
@@ -240,13 +245,11 @@
     pairs = call(
         project_body,
         jax.ShapeDtypeStruct((batch * heads, ROWS, kinds * HD), BF16),
-        [VMEM] * 4,
-    )(modded, weight, qk_gain, rel)
-
-    with jax.named_scope("qkvy"):
-        pairs = swap(pairs, "seq_1")
-    with jax.named_scope("kvxc"):
-        gathered = swap(spread_copies(pairs[:, :, HD:], xs * cores), ("seq_0", "seq_2"))
+        [SMEM] + [VMEM] * 5,
+    )(core_index, modded, weight, other, qk_gain, rel)
+
+    pairs = swap(pairs, "seq_1")
+    gathered = swap(spread_copies(pairs[:, :, HD:], xs * cores), ("seq_0", "seq_2"))
 
     mine = lax.axis_index("seq_1") // heads
     limit = lax.dynamic_slice_in_dim(text_len, mine, 1)
@@ -259,15 +262,13 @@
         [SMEM, VMEM, VMEM],
     )(limit, pairs, gathered)
 
-    with jax.named_scope("atty"):
-        attended = swap(attended, "seq_1")
+    attended = swap(attended, "seq_1")
     parts = call(
         mix_body,
         jax.ShapeDtypeStruct((tps, batch * IMG_R + 8, width), BF16),
         [VMEM] * 3,
     )(attended, output_weight, rel)
-    with jax.named_scope("mixz"):
-        parts = swap(parts, "tp")
+    parts = swap(parts, "tp")
 
     shape = jax.ShapeDtypeStruct((batch, img_rows, width), F32)
     out_img, new_cache, ratio = call(
@@ -293,4 +294,5 @@
         P(),
     )
     out_specs = (P(None, SEQ, "tp"), P(None, SEQ, "tp"), P())
+
     return jax.shard_map(local, mesh=finer, in_specs=in_specs, out_specs=out_specs, check_vma=False)

time: 190 us -> 177 us (0.932)
  blocking collectives: 95.9 us -> 140 us
  waiting for transfers between devices: 58.7 us -> 16.7 us
  starting transfers between devices: 17.3 us -> 7.11 us
  local copies, waits for them, and re-layouts: 10.1 us -> 3.5 us
    all_to_all x3 -> x1, waiting for transfers between devices: 58.7 us -> 16.7 us  [swap(): return lax.all_to_all(value, axis, 0, 0, tiled=True)]
    all_gather x0 -> x1, blocking collectives: none -> 33 us  [local(): wide = lax.all_gather(joined, 'tp', axis=0, tiled=False)]
    all_to_all x3 -> x1, starting transfers between devices: 17.3 us -> 5.07 us  [swap(): return lax.all_to_all(value, axis, 0, 0, tiled=True)]
    all_to_all x5, blocking collectives: 95.9 us -> 107 us  [swap(): return lax.all_to_all(value, axis, 0, 0, tiled=True)]
    broadcast_in_dim x5 -> x3, local copies, waits for them, and re-layouts: 6.53 us -> 2.23 us  [spread_copies(): return jnp.broadcast_to(value[None], (count,) + value.shape)]
    ppermute x0 -> x1, starting transfers between devices: none -> 2.04 us  [local(): other = lax.ppermute(weight, 'seq_2', [(0, 1), (1, 0)])]
  transfers between devices with their start and end apart: 3 -> 2, of which waited for: 3 -> 1; matrix products, arithmetic and copies ran while one was open for 2% -> 0% of each run, Pallas kernels for 1% -> 1%
where the time goes in v2:
time: 177 us
  blocking collectives  140 us (79%)
  waiting for transfers between devices  16.7 us (9%)
  Pallas kernels  8.36 us (5%)
  starting transfers between devices  7.11 us (4%)
  local copies, waits for them, and re-layouts  3.5 us (2%)
    all_to_all x5, blocking collectives, swap(): return lax.all_to_all(value, axis, 0, 0, tiled=True)  107 us
    all_gather x1, blocking collectives, local(): wide = lax.all_gather(joined, 'tp', axis=0, tiled=False)  33 us
    all_to_all x1, waiting for transfers between devices, swap(): return lax.all_to_all(value, axis, 0, 0, tiled=True)  16.7 us
    all_to_all x1, starting transfers between devices, swap(): return lax.all_to_all(value, axis, 0, 0, tiled=True)  5.07 us
  transfers between devices with their start and end apart: 2, of which 1 were waited for; matrix products, arithmetic and copies ran while one was open for 0% of the time, Pallas kernels for 1%

profile of v2, /device:TPU:2, one launch (start us, length us, event | category | flops | bytes accessed | tf_op | source)
XLA Modules:
  0.0 176.9 jit_solution(2313422087105745675)
XLA Ops:
  0.6 0.9 broadcast_in_dim.32
  1.6 25.8 %all_to_all.30 = bf16[8,3,48,256]{3,2,1,0:T(8,128)(2,1)S(1)} all-to-all(bf16[8,3,48,256]{3,2,1,0:T(8,128)(2,1)S(1)} %broadcast_in_dim.32), channel_id=1, replica_groups=mesh['seq_0'=4,'seq_1'=8,'seq_2'=2,'tp'=8] {'seq_1'}, dimensions={0} | all-to-all | bytes 1179648 | tf_op jit(solution)/shard_map/all_to_all | solution.py:38
  27.4 0.2 broadcast_in_dim.34
  27.5 0.0 copy-start.4
  27.5 0.0 copy-start.1
  27.5 0.0 copy-start.7
  27.5 0.0 copy-start.3
  27.6 30.8 %all_to_all.31 = bf16[4,1152,256]{2,1,0:T(8,128)(2,1)S(1)} all-to-all(bf16[4,1152,256]{2,1,0:T(8,128)(2,1)S(1)} %broadcast_in_dim.34), channel_id=1, replica_groups=mesh['seq_0'=4,'seq_1'=8,'seq_2'=2,'tp'=8] {'seq_0'}, dimensions={0} | all-to-all | bytes 4718592 | tf_op jit(solution)/shard_map/all_to_all | solution.py:38
  58.4 0.0 copy-start.5
  58.4 2.0 %collective-permute-start = (bf16[4,8,3,48,256]{4,3,2,1,0:T(8,128)(2,1)S(1)}, bf16[4,8,3,48,256]{4,3,2,1,0:T(8,128)(2,1)}, u32[]{:S(2)}, u32[]{:S(2)}) collective-permute-start(bf16[4,8,3,48,256]{4,3,2,1,0:T(8,128)(2,1)S(1)} %bitcast.12), channel_id=1, source_target_pairs={{0,8},{8,0},{1,9},{9,1},{2,10},{10,2},{3,11},{11,3},{4,12},{12,4},... | collective-permute-start | bytes 7077896 | tf_op jit(solution)/shard_map/ppermute | solution.py:232
  60.4 0.0 copy-done.4
  60.5 0.0 copy-done.1
  60.5 0.0 copy-done.7
  60.5 0.1 concatenate.3
  60.6 33.0 %all_gather.3.x_ref = bf16[8,160,384]{2,1,0:T(8,128)(2,1)S(1)} all-gather(bf16[1,160,384]{2,1,0:T(8,128)(2,1)S(1)} %bitcast.15), channel_id=1, replica_groups=mesh['seq_0'=4,'seq_1'=8,'seq_2'=2,'tp'=8] {'tp'}, dimensions={0}, use_global_device_ids=true | all-gather | bytes 1105920 | tf_op jit(solution)/shard_map/all_gather | solution.py:226
  93.6 0.0 copy-done.3
  93.6 1.3 shard_map.121
  94.9 0.0 collective-permute-done.other_ref
  94.9 0.0 copy-done.5
  94.9 2.9 %shard_map.122 = bf16[8,40,384]{2,1,0:T(8,128)(2,1)S(1)} custom-call(s32[1]{0:T(128)} %bitcast.core_ref, bf16[8,160,384]{2,1,0:T(8,128)(2,1)S(1)} %get-tuple-element.10.mod_ref, bf16[4,8,3,48,256]{4,3,2,1,0:T(8,128)(2,1)S(1)} %bitcast.13, bf16[4,8,3,48,256]{4,3,2,1,0:T(8,128)(2,1)} %collective-permute-done.other_ref, f32[2,256]{1,0:T(2,128)S(1)} %copy-done.5, ...), custom_call_target="tpu_custom_call" | custom-call | tf_op jit(solution)/shard_map/pallas_call | solution.py:245
  97.9 0.0 copy-start.8
  97.9 13.2 %all_to_all.32.qkv_ref = bf16[8,40,384]{2,1,0:T(8,128)(2,1)S(1)} all-to-all(bf16[8,40,384]{2,1,0:T(8,128)(2,1)S(1)} %shard_map.122), channel_id=1, replica_groups=mesh['seq_0'=4,'seq_1'=8,'seq_2'=2,'tp'=8] {'seq_1'}, dimensions={0} | all-to-all | bytes 491520 | tf_op jit(solution)/shard_map/all_to_all | solution.py:38
  111.1 1.2 broadcast_in_dim.35
  112.3 0.0 copy-start
  112.3 5.1 %all-to-all-start.3 = ((bf16[8,8,40,256]{3,2,1,0:T(8,128)(2,1)}), bf16[8,8,40,256]{3,2,1,0:T(8,128)(2,1)S(1)}, u32[]{:S(2)}, u32[]{:S(2)}) async-start(bf16[8,8,40,256]{3,2,1,0:T(8,128)(2,1)} %broadcast_in_dim.35), calls=%async_computation.3 | async-start | bytes 2621440 | tf_op jit(solution)/shard_map/all_to_all | solution.py:38
  117.3 0.0 copy-done.8
  117.3 0.6 dynamic_slice.3.limit_ref
  117.9 16.7 %all-to-all-done.3.kv_ref = bf16[8,8,40,256]{3,2,1,0:T(8,128)(2,1)S(1)} async-done(((bf16[8,8,40,256]{3,2,1,0:T(8,128)(2,1)}), bf16[8,8,40,256]{3,2,1,0:T(8,128)(2,1)S(1)}, u32[]{:S(2)}, u32[]{:S(2)}) %all-to-all-start.3) | async-done | bytes 1310752 | tf_op jit(solution)/shard_map/all_to_all | solution.py:38
  134.6 2.3 %shard_map.123 = (bf16[8,32,128]{2,1,0:T(8,128)(2,1)S(1)}, f32[8,128]{1,0:T(8,128)S(1)}) custom-call(s32[1]{0:T(128)} %dynamic_slice.3.limit_ref, bf16[8,40,384]{2,1,0:T(8,128)(2,1)S(1)} %all_to_all.32.qkv_ref, bf16[8,8,40,256]{3,2,1,0:T(8,128)(2,1)S(1)} %all-to-all-done.3.kv_ref), custom_call_target="tpu_custom_call" | custom-call | tf_op jit(solution)/shard_map/pallas_call | solution.py:256
  136.9 0.0 copy-start.2
  137.0 0.0 copy-start.6
  137.0 10.9 %all_to_all.33.att_ref = bf16[8,32,128]{2,1,0:T(8,128)(2,1)S(1)} all-to-all(bf16[8,32,128]{2,1,0:T(8,128)(2,1)S(1)} %get-tuple-element.12), channel_id=1, replica_groups=mesh['seq_0'=4,'seq_1'=8,'seq_2'=2,'tp'=8] {'seq_1'}, dimensions={0} | all-to-all | bytes 131072 | tf_op jit(solution)/shard_map/all_to_all | solution.py:38
  147.8 0.0 copy-done
  147.9 0.4 shard_map.124
  148.3 26.7 %all_to_all.34.part_ref = bf16[8,136,384]{2,1,0:T(8,128)(2,1)S(1)} all-to-all(bf16[8,136,384]{2,1,0:T(8,128)(2,1)S(1)} %shard_map.124), channel_id=1, replica_groups=mesh['seq_0'=4,'seq_1'=8,'seq_2'=2,'tp'=8] {'tp'}, dimensions={0} | all-to-all | bytes 1671168 | tf_op jit(solution)/shard_map/all_to_all | solution.py:38
  175.0 0.0 copy-done.2
  175.0 0.0 copy-done.6
  175.0 1.5 shard_map.125
  176.4 0.5 slice_bitcast_fusion.2
  (5 shorter events, 0.0 us)
Async XLA Ops:
  27.5 32.9 %copy-start.4 = (bf16[3,4,384]{2,1,0:T(4,128)(2,1)S(1)}, bf16[3,4,384]{2,1,0:T(4,128)(2,1)}, u32[]{:S(2)}) copy-start(bf16[3,4,384]{2,1,0:T(4,128)(2,1)} %mod_ref.1) | copy-start | bytes 27652
  27.5 33.0 %copy-start.1 = (bf16[4,32,384]{2,1,0:T(8,128)(2,1)S(1)}, bf16[4,32,384]{2,1,0:T(8,128)(2,1)}, u32[]{:S(2)}) copy-start(bf16[4,32,384]{2,1,0:T(8,128)(2,1)} %img_ref.1) | copy-start | bytes 294916
  27.5 33.0 %copy-start.7 = (bf16[4,4,384]{2,1,0:T(4,128)(2,1)S(1)}, bf16[4,4,384]{2,1,0:T(4,128)(2,1)}, u32[]{:S(2)}) copy-start(bf16[4,4,384]{2,1,0:T(4,128)(2,1)} %param.11) | copy-start | bytes 36868
  27.5 66.1 %copy-start.3 = (bf16[4,32,384]{2,1,0:T(8,128)(2,1)S(1)}, bf16[4,32,384]{2,1,0:T(8,128)(2,1)}, u32[]{:S(2)}) copy-start(bf16[4,32,384]{2,1,0:T(8,128)(2,1)} %prev_ref.1) | copy-start | bytes 294916
  58.4 36.6 %copy-start.5 = (f32[2,256]{1,0:T(2,128)S(1)}, f32[2,256]{1,0:T(2,128)}, u32[]{:S(2)}) copy-start(f32[2,256]{1,0:T(2,128)} %gain_ref.1) | copy-start | bytes 6148
  58.4 36.5 %collective-permute-start = (bf16[4,8,3,48,256]{4,3,2,1,0:T(8,128)(2,1)S(1)}, bf16[4,8,3,48,256]{4,3,2,1,0:T(8,128)(2,1)}, u32[]{:S(2)}, u32[]{:S(2)}) collective-permute-start(bf16[4,8,3,48,256]{4,3,2,1,0:T(8,128)(2,1)S(1)} %bitcast.12), channel_id=1, source_target_pairs={{0,8},{8,0},{1,9},{9,1},{2,10},{10,2},{3,11},{11,3},{4,12},{12,4},... | collective-permute-start | bytes 7077896 | tf_op jit(solution)/shard_map/ppermute | solution.py:232
  97.9 19.5 %copy-start.8 = (s32[4]{0:T(128)S(1)}, s32[4]{0:T(128)}, u32[]{:S(2)}) copy-start(s32[4]{0:T(128)} %param.18) | copy-start | bytes 52
  112.3 35.6 %copy-start = (bf16[256,3072]{1,0:T(8,128)(2,1)S(1)}, bf16[256,3072]{1,0:T(8,128)(2,1)}, u32[]{:S(2)}) copy-start(bf16[256,3072]{1,0:T(8,128)(2,1)} %w_ref.1) | copy-start | bytes 4718596
  112.3 22.4 %all-to-all-start.3 = ((bf16[8,8,40,256]{3,2,1,0:T(8,128)(2,1)}), bf16[8,8,40,256]{3,2,1,0:T(8,128)(2,1)S(1)}, u32[]{:S(2)}, u32[]{:S(2)}) async-start(bf16[8,8,40,256]{3,2,1,0:T(8,128)(2,1)} %broadcast_in_dim.35), calls=%async_computation.3 | async-start | bytes 2621440 | tf_op jit(solution)/shard_map/all_to_all | solution.py:38
  136.9 38.0 %copy-start.2 = (f32[4,32,384]{2,1,0:T(8,128)S(1)}, f32[4,32,384]{2,1,0:T(8,128)}, u32[]{:S(2)}) copy-start(f32[4,32,384]{2,1,0:T(8,128)} %cache_ref.1) | copy-start | bytes 589828
  137.0 38.0 %copy-start.6 = (s32[4]{0:T(128)S(1)}, s32[4]{0:T(128)}, u32[]{:S(2)}) copy-start(s32[4]{0:T(128)} %flag_ref.1) | copy-start | bytes 52

commit v3 on v2

--- a/solution.py
+++ b/solution.py
@@ -1,3 +1,5 @@
+import functools
+
 import jax
 import jax.numpy as jnp
 from jax import lax
@@ -23,14 +25,14 @@
 SMEM = pl.BlockSpec(memory_space=pltpu.SMEM)
 
 
-def call(body, out_shape, in_specs, limit=40 << 20):
-    outs = jax.tree.map(lambda _: VMEM, out_shape)
+def call(body, out_shape, in_specs, mebibytes, outs=None):
+    outs = outs or jax.tree.map(lambda _: VMEM, out_shape)
     return pl.pallas_call(
         body,
         out_shape=out_shape,
         in_specs=in_specs,
         out_specs=outs,
-        compiler_params=pltpu.CompilerParams(vmem_limit_bytes=limit),
+        compiler_params=pltpu.CompilerParams(vmem_limit_bytes=mebibytes << 20),
     )
 
 
@@ -128,41 +130,41 @@
                 out_ref[b * heads + h, :, kind * HD : (kind + 1) * HD] = block.astype(BF16)
 
 
-def attend_body(limit_ref, qkv_ref, kv_ref, out_ref, rel_ref):
+def attend_body(limit_ref, core_ref, qkv_ref, own_ref, other_ref, out_ref, rel_ref):
     ys = qkv_ref.shape[0]
-    spots = kv_ref.shape[0]
-    count = spots * ys * ROWS
+    xs = own_ref.shape[0]
+    count = xs * ys * ROWS
     query = jnp.concatenate([qkv_ref[y, :IMG_R, :HD] for y in range(ys)], axis=0)
-    pairs = kv_ref[...].reshape(count, 2 * HD)
-    keys = pairs[:, :HD]
-    values = pairs[:, HD:]
-    scores = lax.dot_general(
-        query, keys, (((1,), (1,)), ((), ())), preferred_element_type=F32
-    ) * (1.0 / HD**0.5)
     index = lax.broadcasted_iota(jnp.int32, (1, count), 1)
     slot = index % ROWS
     block = index // ROWS
-    y = block % ys
-    spot = block // ys
-    place = (spot // 2) * (2 * ys) + y * 2 + spot % 2
-    text = place * TXT_R + slot - IMG_R
-    valid = (slot < IMG_R) | ((slot < IMG_R + TXT_R) & (text < limit_ref[0]))
-    scores = jnp.where(valid, scores, NEG)
-    top = jnp.max(scores, axis=1, keepdims=True)
-    weights = jnp.where(valid, jnp.exp(scores - top), 0.0)
-    total = jnp.sum(weights, axis=1, keepdims=True)
-    summed = jnp.dot(weights.astype(BF16), values, preferred_element_type=F32)
+    down = lax.broadcasted_iota(jnp.int32, (ROWS, HD), 0)
+    held = (down >= REL_ROW) & (down < REL_ROW + 3)
+    rel = jnp.zeros((1, HD), F32)
+    parts = []
+    for ref, core in ((own_ref, core_ref[0]), (other_ref, 1 - core_ref[0])):
+        pairs = ref[...].reshape(count, 2 * HD)
+        scores = lax.dot_general(
+            query, pairs[:, :HD], (((1,), (1,)), ((), ())), preferred_element_type=F32
+        ) * (1.0 / HD**0.5)
+        text = (block * 2 + core) * TXT_R + slot - IMG_R
+        valid = (slot < IMG_R) | ((slot < IMG_R + TXT_R) & (text < limit_ref[0]))
+        parts.append((jnp.where(valid, scores, NEG), valid, pairs[:, HD:]))
+        for x in range(xs):
+            for y in range(ys):
+                held_rows = jnp.where(held, ref[x, y, :, :HD].astype(F32), 0.0)
+                rel = rel + jnp.sum(held_rows, axis=0, keepdims=True)
+    rel_ref[...] = jnp.broadcast_to(rel, (8, HD))
+    top = functools.reduce(jnp.maximum, [jnp.max(p[0], axis=1, keepdims=True) for p in parts])
+    total = jnp.zeros((query.shape[0], 1), F32)
+    summed = jnp.zeros(query.shape, F32)
+    for scores, valid, values in parts:
+        weights = jnp.where(valid, jnp.exp(scores - top), 0.0)
+        total = total + jnp.sum(weights, axis=1, keepdims=True)
+        summed = summed + jnp.dot(weights.astype(BF16), values, preferred_element_type=F32)
     attended = (summed / total).astype(BF16)
     for y in range(ys):
         out_ref[y] = attended[y * IMG_R : (y + 1) * IMG_R]
-    down = lax.broadcasted_iota(jnp.int32, (ROWS, HD), 0)
-    held = (down >= REL_ROW) & (down < REL_ROW + 3)
-    rel = jnp.zeros((1, HD), F32)
-    for spot in range(spots):
-        for y in range(ys):
-            block = kv_ref[spot, y, :, :HD].astype(F32)
-            rel = rel + jnp.sum(jnp.where(held, block, 0.0), axis=0, keepdims=True)
-    rel_ref[...] = jnp.broadcast_to(rel, (8, HD))
 
 
 def mix_body(att_ref, w_ref, rel_ref, out_ref):
@@ -202,18 +204,15 @@
         out_ref[b] = img_ref[b].astype(F32) + fresh
     sums = jnp.sum(rel, axis=0, keepdims=True)
     lane = lax.broadcasted_iota(jnp.int32, (1, HD), 1)
-    ratio = jnp.zeros((8, HD), F32)
     for b in range(batch):
-        numer = jnp.sum(jnp.where(lane == b, sums, 0.0), axis=1, keepdims=True)
-        denom = jnp.sum(jnp.where(lane == batch + b, sums, 0.0), axis=1, keepdims=True)
-        wide = lax.broadcasted_iota(jnp.int32, (8, HD), 1)
-        ratio = jnp.where(wide == b, numer / jnp.maximum(denom, 1.0), ratio)
-    rel_ref[...] = ratio
+        numer = jnp.sum(jnp.where(lane == b, sums, 0.0))
+        denom = jnp.sum(jnp.where(lane == batch + b, sums, 0.0))
+        rel_ref[b] = numer / jnp.maximum(denom, 1.0)
 
 
 def local(img, txt, prev_mod, cache, modulation, w_qkv, qk_gain, output_weight, text_len, refresh):
     batch, img_rows, width = img.shape
-    xs, ys, cores = (lax.axis_size(a) for a in SEQ)
+    xs, ys, _ = (lax.axis_size(a) for a in SEQ)
     tps = lax.axis_size("tp")
     kinds, columns = w_qkv.shape[1:]
     deep = w_qkv.shape[0]
@@ -225,9 +224,8 @@
     ).reshape(batch * ROWS, width)
     wide = lax.all_gather(joined, "tp", axis=0, tiled=False)
 
-    weight = w_qkv.transpose(1, 0, 2)
-    weight = swap(spread_copies(weight, ys), "seq_1")
-    weight = swap(spread_copies(weight, xs).reshape(xs, ys * kinds * deep, columns), "seq_0")
+    weight = w_qkv.transpose(1, 0, 2).reshape(kinds * deep, columns)
+    weight = swap(spread_copies(weight, xs * ys), ("seq_0", "seq_1"))
     weight = weight.reshape(xs, ys, kinds, deep, columns)
     other = lax.ppermute(weight, "seq_2", [(0, 1), (1, 0)])
 
@@ -240,16 +238,19 @@
             jax.ShapeDtypeStruct((8, 128), F32),
         ),
         [SMEM, VMEM, VMEM],
+        12,
     )(tp_index, wide, prev_mod)
 
     pairs = call(
         project_body,
         jax.ShapeDtypeStruct((batch * heads, ROWS, kinds * HD), BF16),
         [SMEM] + [VMEM] * 5,
+        16,
     )(core_index, modded, weight, other, qk_gain, rel)
 
     pairs = swap(pairs, "seq_1")
-    gathered = swap(spread_copies(pairs[:, :, HD:], xs * cores), ("seq_0", "seq_2"))
+    gathered = swap(spread_copies(pairs[:, :, HD:], xs), "seq_0")
+    partner = lax.ppermute(gathered, "seq_2", [(0, 1), (1, 0)])
 
     mine = lax.axis_index("seq_1") // heads
     limit = lax.dynamic_slice_in_dim(text_len, mine, 1)
@@ -259,24 +260,28 @@
             jax.ShapeDtypeStruct((ys, IMG_R, HD), BF16),
             jax.ShapeDtypeStruct((8, HD), F32),
         ),
-        [SMEM, VMEM, VMEM],
-    )(limit, pairs, gathered)
+        [SMEM, SMEM, VMEM, VMEM, VMEM],
+        24,
+    )(limit, core_index, pairs, gathered, partner)
 
     attended = swap(attended, "seq_1")
     parts = call(
         mix_body,
         jax.ShapeDtypeStruct((tps, batch * IMG_R + 8, width), BF16),
         [VMEM] * 3,
+        12,
     )(attended, output_weight, rel)
     parts = swap(parts, "tp")
 
     shape = jax.ShapeDtypeStruct((batch, img_rows, width), F32)
     out_img, new_cache, ratio = call(
         final_body,
-        (shape, shape, jax.ShapeDtypeStruct((8, HD), F32)),
+        (shape, shape, jax.ShapeDtypeStruct((batch,), F32)),
         [SMEM, VMEM, VMEM, VMEM, VMEM],
+        8,
+        (VMEM, VMEM, SMEM),
     )(refresh, parts, cache, img, modulation)
-    return (out_img, new_cache, ratio[0, :batch])
+    return (out_img, new_cache, ratio)
 
 
 def solution(mesh):

time: 177 us -> 179 us (1.011)
  the two profiles are of different devices: /device:TPU:2 before, /device:TPU:8 now
where the time goes in v3:
time: 179 us
  blocking collectives  162 us (91%)
  Pallas kernels  8.46 us (5%)
  starting transfers between devices  3.95 us (2%)
  local copies, waits for them, and re-layouts  1.84 us (1%)
    all_to_all x5, blocking collectives, swap(): return lax.all_to_all(value, axis, 0, 0, tiled=True)  129 us
    all_gather x1, blocking collectives, local(): wide = lax.all_gather(joined, 'tp', axis=0, tiled=False)  33 us
  transfers between devices with their start and end apart: 2, of which 1 were waited for; matrix products, arithmetic and copies ran while one was open for 0% of the time, Pallas kernels for 1%

profile of v3, /device:TPU:8, one launch (start us, length us, event | category | flops | bytes accessed | tf_op | source)
XLA Modules:
  0.0 178.6 jit_solution(9686302233812775339)
XLA Ops:
  0.6 1.0 broadcast_in_dim.26
  1.7 0.0 copy-start.4
  1.7 0.0 copy-start.1
  1.7 0.0 copy-start.7
  1.7 0.0 copy-start.3
  1.7 67.3 %all_to_all.25 = bf16[32,144,256]{2,1,0:T(8,128)(2,1)S(1)} all-to-all(bf16[32,144,256]{2,1,0:T(8,128)(2,1)S(1)} %broadcast_in_dim.26), channel_id=1, replica_groups=mesh['seq_0'=4,'seq_1'=8,'seq_2'=2,'tp'=8] {'seq_0','seq_1'}, dimensions={0} | all-to-all | bytes 4718592 | tf_op jit(solution)/shard_map/all_to_all | solution.py:40
  69.0 0.0 copy-start.5
  69.0 2.0 %collective-permute-start = (bf16[4,8,3,48,256]{4,3,2,1,0:T(8,128)(2,1)S(1)}, bf16[4,8,3,48,256]{4,3,2,1,0:T(8,128)(2,1)}, u32[]{:S(2)}, u32[]{:S(2)}) collective-permute-start(bf16[4,8,3,48,256]{4,3,2,1,0:T(8,128)(2,1)S(1)} %bitcast.11), channel_id=1, source_target_pairs={{0,8},{8,0},{1,9},{9,1},{2,10},{10,2},{3,11},{11,3},{4,12},{12,4},... | collective-permute-start | bytes 7077896 | tf_op jit(solution)/shard_map/ppermute | solution.py:230
  71.1 0.0 copy-done.4
  71.1 0.0 copy-done.1
  71.1 0.0 copy-done.7
  71.2 0.1 concatenate.3
  71.2 33.0 %all_gather.3.x_ref = bf16[8,160,384]{2,1,0:T(8,128)(2,1)S(1)} all-gather(bf16[1,160,384]{2,1,0:T(8,128)(2,1)S(1)} %bitcast.13), channel_id=1, replica_groups=mesh['seq_0'=4,'seq_1'=8,'seq_2'=2,'tp'=8] {'tp'}, dimensions={0}, use_global_device_ids=true | all-gather | bytes 1105920 | tf_op jit(solution)/shard_map/all_gather | solution.py:225
  104.3 0.0 copy-done.3
  104.3 1.3 shard_map.121
  105.6 0.0 collective-permute-done.other_ref
  105.6 0.0 copy-done.5
  105.6 2.9 %shard_map.122 = bf16[8,40,384]{2,1,0:T(8,128)(2,1)S(1)} custom-call(s32[1]{0:T(128)} %bitcast.core_ref, bf16[8,160,384]{2,1,0:T(8,128)(2,1)S(1)} %get-tuple-element.7.mod_ref, bf16[4,8,3,48,256]{4,3,2,1,0:T(8,128)(2,1)S(1)} %bitcast.12, bf16[4,8,3,48,256]{4,3,2,1,0:T(8,128)(2,1)} %collective-permute-done.other_ref, f32[2,256]{1,0:T(2,128)S(1)} %copy-done.5, ...), custom_call_target="tpu_custom_call" | custom-call | tf_op jit(solution)/shard_map/pallas_call | solution.py:244
  108.5 0.0 copy-start.8
  108.5 0.0 copy-start
  108.5 12.2 %all_to_all.26.qkv_ref = bf16[8,40,384]{2,1,0:T(8,128)(2,1)S(1)} all-to-all(bf16[8,40,384]{2,1,0:T(8,128)(2,1)S(1)} %shard_map.122), channel_id=1, replica_groups=mesh['seq_0'=4,'seq_1'=8,'seq_2'=2,'tp'=8] {'seq_1'}, dimensions={0} | all-to-all | bytes 491520 | tf_op jit(solution)/shard_map/all_to_all | solution.py:40
  120.8 11.2 %all_to_all.27.own_ref = bf16[4,8,40,256]{3,2,1,0:T(8,128)(2,1)S(1)} all-to-all(bf16[4,8,40,256]{3,2,1,0:T(8,128)(2,1)S(1)} %broadcast_in_dim.27), channel_id=1, replica_groups=mesh['seq_0'=4,'seq_1'=8,'seq_2'=2,'tp'=8] {'seq_0'}, dimensions={0} | all-to-all | bytes 1310720 | tf_op jit(solution)/shard_map/all_to_all | solution.py:40
  132.0 1.9 %collective-permute-start.1 = (bf16[4,8,40,256]{3,2,1,0:T(8,128)(2,1)S(1)}, bf16[4,8,40,256]{3,2,1,0:T(8,128)(2,1)S(1)}, u32[]{:S(2)}, u32[]{:S(2)}) collective-permute-start(bf16[4,8,40,256]{3,2,1,0:T(8,128)(2,1)S(1)} %all_to_all.27.own_ref), channel_id=1, source_target_pairs={{0,8},{8,0},{1,9},{9,1},{2,10},{10,2},{3,11},{11,3},{4,12},{12,4},... | collective-permute-start | bytes 1966088 | tf_op jit(solution)/shard_map/ppermute | solution.py:253
  133.9 0.0 copy-done.8
  133.9 0.6 dynamic_slice.3.limit_ref
  134.5 1.4 collective-permute-done.1.other_ref
  135.9 2.2 %shard_map.123 = (bf16[8,32,128]{2,1,0:T(8,128)(2,1)S(1)}, f32[8,128]{1,0:T(8,128)S(1)}) custom-call(s32[1]{0:T(128)} %dynamic_slice.3.limit_ref, s32[1]{0:T(128)} %bitcast.core_ref, bf16[8,40,384]{2,1,0:T(8,128)(2,1)S(1)} %all_to_all.26.qkv_ref, bf16[4,8,40,256]{3,2,1,0:T(8,128)(2,1)S(1)} %all_to_all.27.own_ref, ...), custom_call_target="tpu_custom_call" | custom-call | tf_op jit(solution)/shard_map/pallas_call | solution.py:257
  138.1 0.0 copy-start.2
  138.1 0.0 copy-start.6
  138.1 11.2 %all_to_all.28.att_ref = bf16[8,32,128]{2,1,0:T(8,128)(2,1)S(1)} all-to-all(bf16[8,32,128]{2,1,0:T(8,128)(2,1)S(1)} %get-tuple-element.9), channel_id=1, replica_groups=mesh['seq_0'=4,'seq_1'=8,'seq_2'=2,'tp'=8] {'seq_1'}, dimensions={0} | all-to-all | bytes 131072 | tf_op jit(solution)/shard_map/all_to_all | solution.py:40
  149.4 0.0 copy-done
  149.4 0.4 shard_map.124
  149.8 27.2 %all_to_all.29.part_ref = bf16[8,136,384]{2,1,0:T(8,128)(2,1)S(1)} all-to-all(bf16[8,136,384]{2,1,0:T(8,128)(2,1)S(1)} %shard_map.124), channel_id=1, replica_groups=mesh['seq_0'=4,'seq_1'=8,'seq_2'=2,'tp'=8] {'tp'}, dimensions={0} | all-to-all | bytes 1671168 | tf_op jit(solution)/shard_map/all_to_all | solution.py:40
  176.9 0.0 copy-done.2
  177.0 0.0 copy-done.6
  177.0 1.7 shard_map.125
  (6 shorter events, 0.1 us)
Async XLA Ops:
  1.7 69.4 %copy-start.4 = (bf16[3,4,384]{2,1,0:T(4,128)(2,1)S(1)}, bf16[3,4,384]{2,1,0:T(4,128)(2,1)}, u32[]{:S(2)}) copy-start(bf16[3,4,384]{2,1,0:T(4,128)(2,1)} %mod_ref.1) | copy-start | bytes 27652
  1.7 69.5 %copy-start.1 = (bf16[4,32,384]{2,1,0:T(8,128)(2,1)S(1)}, bf16[4,32,384]{2,1,0:T(8,128)(2,1)}, u32[]{:S(2)}) copy-start(bf16[4,32,384]{2,1,0:T(8,128)(2,1)} %img_ref.1) | copy-start | bytes 294916
  1.7 69.5 %copy-start.7 = (bf16[4,4,384]{2,1,0:T(4,128)(2,1)S(1)}, bf16[4,4,384]{2,1,0:T(4,128)(2,1)}, u32[]{:S(2)}) copy-start(bf16[4,4,384]{2,1,0:T(4,128)(2,1)} %param.11) | copy-start | bytes 36868
  1.7 102.6 %copy-start.3 = (bf16[4,32,384]{2,1,0:T(8,128)(2,1)S(1)}, bf16[4,32,384]{2,1,0:T(8,128)(2,1)}, u32[]{:S(2)}) copy-start(bf16[4,32,384]{2,1,0:T(8,128)(2,1)} %prev_ref.1) | copy-start | bytes 294916
  69.0 36.6 %copy-start.5 = (f32[2,256]{1,0:T(2,128)S(1)}, f32[2,256]{1,0:T(2,128)}, u32[]{:S(2)}) copy-start(f32[2,256]{1,0:T(2,128)} %gain_ref.1) | copy-start | bytes 6148
  69.0 36.6 %collective-permute-start = (bf16[4,8,3,48,256]{4,3,2,1,0:T(8,128)(2,1)S(1)}, bf16[4,8,3,48,256]{4,3,2,1,0:T(8,128)(2,1)}, u32[]{:S(2)}, u32[]{:S(2)}) collective-permute-start(bf16[4,8,3,48,256]{4,3,2,1,0:T(8,128)(2,1)S(1)} %bitcast.11), channel_id=1, source_target_pairs={{0,8},{8,0},{1,9},{9,1},{2,10},{10,2},{3,11},{11,3},{4,12},{12,4},... | collective-permute-start | bytes 7077896 | tf_op jit(solution)/shard_map/ppermute | solution.py:230
  108.5 25.4 %copy-start.8 = (s32[4]{0:T(128)S(1)}, s32[4]{0:T(128)}, u32[]{:S(2)}) copy-start(s32[4]{0:T(128)} %param.18) | copy-start | bytes 52
  108.5 40.9 %copy-start = (bf16[256,3072]{1,0:T(8,128)(2,1)S(1)}, bf16[256,3072]{1,0:T(8,128)(2,1)}, u32[]{:S(2)}) copy-start(bf16[256,3072]{1,0:T(8,128)(2,1)} %w_ref.1) | copy-start | bytes 4718596
  132.0 4.0 %collective-permute-start.1 = (bf16[4,8,40,256]{3,2,1,0:T(8,128)(2,1)S(1)}, bf16[4,8,40,256]{3,2,1,0:T(8,128)(2,1)S(1)}, u32[]{:S(2)}, u32[]{:S(2)}) collective-permute-start(bf16[4,8,40,256]{3,2,1,0:T(8,128)(2,1)S(1)} %all_to_all.27.own_ref), channel_id=1, source_target_pairs={{0,8},{8,0},{1,9},{9,1},{2,10},{10,2},{3,11},{11,3},{4,12},{12,4},... | collective-permute-start | bytes 1966088 | tf_op jit(solution)/shard_map/ppermute | solution.py:253
  138.1 38.8 %copy-start.2 = (f32[4,32,384]{2,1,0:T(8,128)S(1)}, f32[4,32,384]{2,1,0:T(8,128)}, u32[]{:S(2)}) copy-start(f32[4,32,384]{2,1,0:T(8,128)} %cache_ref.1) | copy-start | bytes 589828
  138.1 38.8 %copy-start.6 = (s32[4]{0:T(128)S(1)}, s32[4]{0:T(128)}, u32[]{:S(2)}) copy-start(s32[4]{0:T(128)} %flag_ref.1) | copy-start | bytes 52

commit v4 on v3

--- a/solution.py
+++ b/solution.py
@@ -10,7 +10,8 @@
 
 
 HD = 128
-SEQ = ("seq_0", "seq_1", "seq_2")
+SEQ = ("seq_0", "seq_1a", "seq_1b", "seq_2")
+AXIS_Y = ("seq_1a", "seq_1b")
 EPS = 0.1
 NEG = -1e30
 F32 = jnp.float32
@@ -99,7 +100,8 @@
 def project(mod_ref, w_refs, gain_ref, rel_ref, out_ref):
     groups, rows, width = mod_ref.shape
     cores = len(w_refs)
-    _, ys, kinds, deep, columns = w_refs[0].shape
+    _, near, far, kinds, deep, columns = w_refs[0].shape
+    ys = near * far
     batch = rows // ROWS
     heads = columns // HD
     high, middle, low = split_three(rel_ref[0:1, :])
@@ -112,7 +114,8 @@
             for step in range(per_group):
                 flat = g * per_group + step
                 for core in range(cores):
-                    pieces.append(w_refs[core][flat // ys, flat % ys, kind])
+                    y = flat % ys
+                    pieces.append(w_refs[core][flat // ys, y % near, y // near, kind])
             total = total + jnp.dot(
                 mod_ref[g], jnp.concatenate(pieces, axis=0), preferred_element_type=F32
             )
@@ -212,7 +215,8 @@
 
 def local(img, txt, prev_mod, cache, modulation, w_qkv, qk_gain, output_weight, text_len, refresh):
     batch, img_rows, width = img.shape
-    xs, ys, _ = (lax.axis_size(a) for a in SEQ)
+    xs, far, near, _ = (lax.axis_size(a) for a in SEQ)
+    ys = far * near
     tps = lax.axis_size("tp")
     kinds, columns = w_qkv.shape[1:]
     deep = w_qkv.shape[0]
@@ -225,8 +229,10 @@
     wide = lax.all_gather(joined, "tp", axis=0, tiled=False)
 
     weight = w_qkv.transpose(1, 0, 2).reshape(kinds * deep, columns)
-    weight = swap(spread_copies(weight, xs * ys), ("seq_0", "seq_1"))
-    weight = weight.reshape(xs, ys, kinds, deep, columns)
+    weight = swap(spread_copies(weight, far), "seq_1a")
+    weight = weight.reshape(far * kinds * deep, columns)
+    weight = swap(spread_copies(weight, xs * near), ("seq_0", "seq_1b"))
+    weight = weight.reshape(xs, near, far, kinds, deep, columns)
     other = lax.ppermute(weight, "seq_2", [(0, 1), (1, 0)])
 
     tp_index = lax.axis_index("tp").astype(jnp.int32)[None]
@@ -248,11 +254,11 @@
         16,
     )(core_index, modded, weight, other, qk_gain, rel)
 
-    pairs = swap(pairs, "seq_1")
+    pairs = swap(pairs, AXIS_Y)
     gathered = swap(spread_copies(pairs[:, :, HD:], xs), "seq_0")
     partner = lax.ppermute(gathered, "seq_2", [(0, 1), (1, 0)])
 
-    mine = lax.axis_index("seq_1") // heads
+    mine = lax.axis_index(AXIS_Y) // heads
     limit = lax.dynamic_slice_in_dim(text_len, mine, 1)
     attended, rel = call(
         attend_body,
@@ -264,7 +270,7 @@
         24,
     )(limit, core_index, pairs, gathered, partner)
 
-    attended = swap(attended, "seq_1")
+    attended = swap(attended, AXIS_Y)
     parts = call(
         mix_body,
         jax.ShapeDtypeStruct((tps, batch * IMG_R + 8, width), BF16),
@@ -285,7 +291,7 @@
 
 
 def solution(mesh):
-    finer = Mesh(mesh.devices.reshape(4, 8, 2, mesh.shape["tp"]), ("seq_0", "seq_1", "seq_2", "tp"))
+    finer = Mesh(mesh.devices.reshape(4, 4, 2, 2, mesh.shape["tp"]), SEQ + ("tp",))
     in_specs = (
         P(None, SEQ, "tp"),
         P(None, SEQ, "tp"),

time: 179 us -> 164 us (0.916)
  the two profiles are of different devices: /device:TPU:8 before, /device:TPU:2 now
where the time goes in v4:
time: 164 us
  blocking collectives  147 us (90%)
  Pallas kernels  8.47 us (5%)
  starting transfers between devices  3.95 us (2%)
  local copies, waits for them, and re-layouts  1.86 us (1%)
    all_to_all x6, blocking collectives, swap(): return lax.all_to_all(value, axis, 0, 0, tiled=True)  114 us
    all_gather x1, blocking collectives, local(): wide = lax.all_gather(joined, 'tp', axis=0, tiled=False)  33 us
  transfers between devices with their start and end apart: 2, of which 1 were waited for; matrix products, arithmetic and copies ran while one was open for 0% of the time, Pallas kernels for 1%

profile of v4, /device:TPU:2, one launch (start us, length us, event | category | flops | bytes accessed | tf_op | source)
XLA Modules:
  0.0 163.6 jit_solution(7823125056109024116)
XLA Ops:
  0.6 0.9 broadcast_in_dim.33
  1.5 18.6 %all_to_all.30 = bf16[4,144,256]{2,1,0:T(8,128)(2,1)S(1)} all-to-all(bf16[4,144,256]{2,1,0:T(8,128)(2,1)S(1)} %broadcast_in_dim.33), channel_id=1, replica_groups=mesh['seq_0'=4,'seq_1a'=4,'seq_1b'=2,'seq_2'=2,'tp'=8] {'seq_1a'}, dimensions={0} | all-to-all | bytes 589824 | tf_op jit(solution)/shard_map/all_to_all | solution.py:41
  20.1 0.2 broadcast_in_dim.35
  20.3 0.0 copy-start.4
  20.3 0.0 copy-start.1
  20.3 0.0 copy-start.7
  20.3 0.0 copy-start.3
  20.3 30.9 %all_to_all.31 = bf16[8,576,256]{2,1,0:T(8,128)(2,1)S(1)} all-to-all(bf16[8,576,256]{2,1,0:T(8,128)(2,1)S(1)} %broadcast_in_dim.35), channel_id=1, replica_groups=mesh['seq_0'=4,'seq_1a'=4,'seq_1b'=2,'seq_2'=2,'tp'=8] {'seq_0','seq_1b'}, dimensions={0} | all-to-all | bytes 4718592 | tf_op jit(solution)/shard_map/all_to_all | solution.py:41
  51.3 0.0 copy-start.5
  51.3 2.0 %collective-permute-start = (bf16[4,2,4,3,48,256]{5,4,3,2,1,0:T(8,128)(2,1)S(1)}, bf16[4,2,4,3,48,256]{5,4,3,2,1,0:T(8,128)(2,1)}, u32[]{:S(2)}, u32[]{:S(2)}) collective-permute-start(bf16[4,2,4,3,48,256]{5,4,3,2,1,0:T(8,128)(2,1)S(1)} %bitcast.12), channel_id=1, source_target_pairs={{0,8},{8,0},{1,9},{9,1},{2,10},{10,2},{3,11},{11,3},{4,12},{12,4},... | collective-permute-start | bytes 7077896 | tf_op jit(solution)/shard_map/ppermute | solution.py:236
  53.3 0.0 copy-done.4
  53.4 0.0 copy-done.1
  53.4 0.0 copy-done.7
  53.4 0.1 concatenate.3
  53.5 33.0 %all_gather.3.x_ref = bf16[8,160,384]{2,1,0:T(8,128)(2,1)S(1)} all-gather(bf16[1,160,384]{2,1,0:T(8,128)(2,1)S(1)} %bitcast.15), channel_id=1, replica_groups=mesh['seq_0'=4,'seq_1a'=4,'seq_1b'=2,'seq_2'=2,'tp'=8] {'tp'}, dimensions={0}, use_global_device_ids=true | all-gather | bytes 1105920 | tf_op jit(solution)/shard_map/all_gather | solution.py:229
  86.5 0.0 copy-done.3
  86.5 1.3 shard_map.121
  87.8 0.0 collective-permute-done.other_ref
  87.8 0.0 copy-done.5
  87.9 2.9 %shard_map.122 = bf16[8,40,384]{2,1,0:T(8,128)(2,1)S(1)} custom-call(s32[1]{0:T(128)} %bitcast.core_ref, bf16[8,160,384]{2,1,0:T(8,128)(2,1)S(1)} %get-tuple-element.7.mod_ref, bf16[4,2,4,3,48,256]{5,4,3,2,1,0:T(8,128)(2,1)S(1)} %bitcast.13, bf16[4,2,4,3,48,256]{5,4,3,2,1,0:T(8,128)(2,1)} %collective-permute-done.other_ref, f32[2,256]{1,0:T(2,128)S(1)} %copy-done.5, ...), custom_call_target="tpu_custom_call" | custom-call | tf_op jit(solution)/shard_map/pallas_call | solution.py:250
  90.8 0.0 copy-start.8
  90.8 0.0 copy-start
  90.8 15.2 %all_to_all.32.qkv_ref = bf16[8,40,384]{2,1,0:T(8,128)(2,1)S(1)} all-to-all(bf16[8,40,384]{2,1,0:T(8,128)(2,1)S(1)} %shard_map.122), channel_id=1, replica_groups=mesh['seq_0'=4,'seq_1a'=4,'seq_1b'=2,'seq_2'=2,'tp'=8] {'seq_1a','seq_1b'}, dimensions={0} | all-to-all | bytes 491520 | tf_op jit(solution)/shard_map/all_to_all | solution.py:41
  106.1 11.2 %all_to_all.33.own_ref = bf16[4,8,40,256]{3,2,1,0:T(8,128)(2,1)S(1)} all-to-all(bf16[4,8,40,256]{3,2,1,0:T(8,128)(2,1)S(1)} %broadcast_in_dim.36), channel_id=1, replica_groups=mesh['seq_0'=4,'seq_1a'=4,'seq_1b'=2,'seq_2'=2,'tp'=8] {'seq_0'}, dimensions={0} | all-to-all | bytes 1310720 | tf_op jit(solution)/shard_map/all_to_all | solution.py:41
  117.3 1.9 %collective-permute-start.1 = (bf16[4,8,40,256]{3,2,1,0:T(8,128)(2,1)S(1)}, bf16[4,8,40,256]{3,2,1,0:T(8,128)(2,1)S(1)}, u32[]{:S(2)}, u32[]{:S(2)}) collective-permute-start(bf16[4,8,40,256]{3,2,1,0:T(8,128)(2,1)S(1)} %all_to_all.33.own_ref), channel_id=1, source_target_pairs={{0,8},{8,0},{1,9},{9,1},{2,10},{10,2},{3,11},{11,3},{4,12},{12,4},... | collective-permute-start | bytes 1966088 | tf_op jit(solution)/shard_map/ppermute | solution.py:259
  119.2 0.0 copy-done.8
  119.2 0.6 dynamic_slice.3.limit_ref
  119.8 1.4 collective-permute-done.1.other_ref
  121.3 2.2 %shard_map.123 = (bf16[8,32,128]{2,1,0:T(8,128)(2,1)S(1)}, f32[8,128]{1,0:T(8,128)S(1)}) custom-call(s32[1]{0:T(128)} %dynamic_slice.3.limit_ref, s32[1]{0:T(128)} %bitcast.core_ref, bf16[8,40,384]{2,1,0:T(8,128)(2,1)S(1)} %all_to_all.32.qkv_ref, bf16[4,8,40,256]{3,2,1,0:T(8,128)(2,1)S(1)} %all_to_all.33.own_ref, ...), custom_call_target="tpu_custom_call" | custom-call | tf_op jit(solution)/shard_map/pallas_call | solution.py:263
  123.5 0.0 copy-start.2
  123.5 0.0 copy-start.6
  123.5 10.9 %all_to_all.34.att_ref = bf16[8,32,128]{2,1,0:T(8,128)(2,1)S(1)} all-to-all(bf16[8,32,128]{2,1,0:T(8,128)(2,1)S(1)} %get-tuple-element.9), channel_id=1, replica_groups=mesh['seq_0'=4,'seq_1a'=4,'seq_1b'=2,'seq_2'=2,'tp'=8] {'seq_1a','seq_1b'}, dimensions={0} | all-to-all | bytes 131072 | tf_op jit(solution)/shard_map/all_to_all | solution.py:41
  134.4 0.0 copy-done
  134.4 0.4 shard_map.124
  134.8 27.1 %all_to_all.35.part_ref = bf16[8,136,384]{2,1,0:T(8,128)(2,1)S(1)} all-to-all(bf16[8,136,384]{2,1,0:T(8,128)(2,1)S(1)} %shard_map.124), channel_id=1, replica_groups=mesh['seq_0'=4,'seq_1a'=4,'seq_1b'=2,'seq_2'=2,'tp'=8] {'tp'}, dimensions={0} | all-to-all | bytes 1671168 | tf_op jit(solution)/shard_map/all_to_all | solution.py:41
  161.9 0.0 copy-done.2
  161.9 0.0 copy-done.6
  161.9 1.7 %shard_map.125 = (f32[4,32,384]{2,1,0:T(8,128)}, f32[4,32,384]{2,1,0:T(8,128)}, f32[4]{0:T(128)}) custom-call(s32[4]{0:T(128)S(1)} %copy-done.6, bf16[8,136,384]{2,1,0:T(8,128)(2,1)S(1)} %all_to_all.35.part_ref, f32[4,32,384]{2,1,0:T(8,128)S(1)} %copy-done.2, bf16[4,32,384]{2,1,0:T(8,128)(2,1)S(1)} %copy-done.1, bf16[3,4,384]{2,1,0:T(4,128)(2,1)S(1)} %copy-done.4), custom_call_target="tpu_custom_call" | custom-call | tf_op jit(solution)/shard_map/pallas_call | solution.py:283
  (6 shorter events, 0.1 us)
Async XLA Ops:
  20.3 33.0 %copy-start.4 = (bf16[3,4,384]{2,1,0:T(4,128)(2,1)S(1)}, bf16[3,4,384]{2,1,0:T(4,128)(2,1)}, u32[]{:S(2)}) copy-start(bf16[3,4,384]{2,1,0:T(4,128)(2,1)} %mod_ref.1) | copy-start | bytes 27652
  20.3 33.1 %copy-start.1 = (bf16[4,32,384]{2,1,0:T(8,128)(2,1)S(1)}, bf16[4,32,384]{2,1,0:T(8,128)(2,1)}, u32[]{:S(2)}) copy-start(bf16[4,32,384]{2,1,0:T(8,128)(2,1)} %img_ref.1) | copy-start | bytes 294916
  20.3 33.1 %copy-start.7 = (bf16[4,4,384]{2,1,0:T(4,128)(2,1)S(1)}, bf16[4,4,384]{2,1,0:T(4,128)(2,1)}, u32[]{:S(2)}) copy-start(bf16[4,4,384]{2,1,0:T(4,128)(2,1)} %param.11) | copy-start | bytes 36868
  20.3 66.2 %copy-start.3 = (bf16[4,32,384]{2,1,0:T(8,128)(2,1)S(1)}, bf16[4,32,384]{2,1,0:T(8,128)(2,1)}, u32[]{:S(2)}) copy-start(bf16[4,32,384]{2,1,0:T(8,128)(2,1)} %prev_ref.1) | copy-start | bytes 294916
  51.3 36.6 %copy-start.5 = (f32[2,256]{1,0:T(2,128)S(1)}, f32[2,256]{1,0:T(2,128)}, u32[]{:S(2)}) copy-start(f32[2,256]{1,0:T(2,128)} %gain_ref.1) | copy-start | bytes 6148
  51.3 36.6 %collective-permute-start = (bf16[4,2,4,3,48,256]{5,4,3,2,1,0:T(8,128)(2,1)S(1)}, bf16[4,2,4,3,48,256]{5,4,3,2,1,0:T(8,128)(2,1)}, u32[]{:S(2)}, u32[]{:S(2)}) collective-permute-start(bf16[4,2,4,3,48,256]{5,4,3,2,1,0:T(8,128)(2,1)S(1)} %bitcast.12), channel_id=1, source_target_pairs={{0,8},{8,0},{1,9},{9,1},{2,10},{10,2},{3,11},{11,3},{4,12},{12,4},... | collective-permute-start | bytes 7077896 | tf_op jit(solution)/shard_map/ppermute | solution.py:236
  90.8 28.5 %copy-start.8 = (s32[4]{0:T(128)S(1)}, s32[4]{0:T(128)}, u32[]{:S(2)}) copy-start(s32[4]{0:T(128)} %param.18) | copy-start | bytes 52
  90.8 43.6 %copy-start = (bf16[256,3072]{1,0:T(8,128)(2,1)S(1)}, bf16[256,3072]{1,0:T(8,128)(2,1)}, u32[]{:S(2)}) copy-start(bf16[256,3072]{1,0:T(8,128)(2,1)} %w_ref.1) | copy-start | bytes 4718596
  117.3 4.0 %collective-permute-start.1 = (bf16[4,8,40,256]{3,2,1,0:T(8,128)(2,1)S(1)}, bf16[4,8,40,256]{3,2,1,0:T(8,128)(2,1)S(1)}, u32[]{:S(2)}, u32[]{:S(2)}) collective-permute-start(bf16[4,8,40,256]{3,2,1,0:T(8,128)(2,1)S(1)} %all_to_all.33.own_ref), channel_id=1, source_target_pairs={{0,8},{8,0},{1,9},{9,1},{2,10},{10,2},{3,11},{11,3},{4,12},{12,4},... | collective-permute-start | bytes 1966088 | tf_op jit(solution)/shard_map/ppermute | solution.py:259
  123.5 38.4 %copy-start.2 = (f32[4,32,384]{2,1,0:T(8,128)S(1)}, f32[4,32,384]{2,1,0:T(8,128)}, u32[]{:S(2)}) copy-start(f32[4,32,384]{2,1,0:T(8,128)} %cache_ref.1) | copy-start | bytes 589828
  123.5 38.4 %copy-start.6 = (s32[4]{0:T(128)S(1)}, s32[4]{0:T(128)}, u32[]{:S(2)}) copy-start(s32[4]{0:T(128)} %flag_ref.1) | copy-start | bytes 52

commit v5 on v4

--- a/solution.py
+++ b/solution.py
@@ -50,6 +50,16 @@
     rest = value - high
     middle = rest.astype(BF16).astype(F32)
     return high, middle, rest - middle
+
+
+def join_body(img_ref, txt_ref, mod_ref, out_ref):
+    batch, _, width = img_ref.shape
+    for b in range(batch):
+        at = b * ROWS
+        tail = [txt_ref[b], mod_ref[0, b : b + 1], mod_ref[1, b : b + 1]]
+        tail = [t.astype(F32) for t in tail] + [jnp.zeros((ROWS - REL_ROW - 2, width), F32)]
+        out_ref[at : at + IMG_R] = img_ref[b]
+        out_ref[at + IMG_R : at + ROWS] = jnp.concatenate(tail, axis=0).astype(BF16)
 
 
 def norm_body(tp_ref, x_ref, prev_ref, mod_ref, rel_ref):
@@ -133,7 +143,7 @@
                 out_ref[b * heads + h, :, kind * HD : (kind + 1) * HD] = block.astype(BF16)
 
 
-def attend_body(limit_ref, core_ref, qkv_ref, own_ref, other_ref, out_ref, rel_ref):
+def attend_body(limit_ref, flag_ref, core_ref, qkv_ref, own_ref, other_ref, out_ref):
     ys = qkv_ref.shape[0]
     xs = own_ref.shape[0]
     count = xs * ys * ROWS
@@ -157,7 +167,6 @@
             for y in range(ys):
                 held_rows = jnp.where(held, ref[x, y, :, :HD].astype(F32), 0.0)
                 rel = rel + jnp.sum(held_rows, axis=0, keepdims=True)
-    rel_ref[...] = jnp.broadcast_to(rel, (8, HD))
     top = functools.reduce(jnp.maximum, [jnp.max(p[0], axis=1, keepdims=True) for p in parts])
     total = jnp.zeros((query.shape[0], 1), F32)
     summed = jnp.zeros(query.shape, F32)
@@ -165,47 +174,54 @@
         weights = jnp.where(valid, jnp.exp(scores - top), 0.0)
         total = total + jnp.sum(weights, axis=1, keepdims=True)
         summed = summed + jnp.dot(weights.astype(BF16), values, preferred_element_type=F32)
-    attended = (summed / total).astype(BF16)
+    attended = summed / total
+    high, middle, low = split_three(rel)
+    row = lax.broadcasted_iota(jnp.int32, (IMG_R, HD), 0)
+    sums = jnp.where(row == 0, high, jnp.where(row == 1, middle, jnp.where(row == 2, low, 0.0)))
     for y in range(ys):
-        out_ref[y] = attended[y * IMG_R : (y + 1) * IMG_R]
-
-
-def mix_body(att_ref, w_ref, rel_ref, out_ref):
-    pairs = att_ref.shape[0]
-    groups, _, width = out_ref.shape
-    heads = w_ref.shape[0] // HD
-    batch = pairs // heads
+        block = attended[y * IMG_R : (y + 1) * IMG_R]
+        block = jnp.where(flag_ref[0] == 1, block, sums).astype(BF16)
+        for z in range(out_ref.shape[1]):
+            out_ref[y, z] = block
+
+
+def deal_body(tp_ref, w_ref, *out_refs):
+    count = len(out_refs)
+    width = out_refs[0].shape[1]
+    for k, out_ref in enumerate(out_refs):
+        target = lax.rem(tp_ref[0] + k, count)
+        out_ref[...] = w_ref[:, pl.ds(pl.multiple_of(target * width, HD), width)]
+
+
+def final_body(tp_ref, flag_ref, att_ref, *refs):
+    *w_refs, cache_ref, img_ref, mod_ref, out_ref, new_ref, rel_ref = refs
+    groups = len(w_refs)
+    batch = img_ref.shape[0]
+    heads = att_ref.shape[0] // batch
     rows = batch * IMG_R
-    lefts = []
-    for h in range(heads):
-        lefts.append(jnp.concatenate([att_ref[b * heads + h] for b in range(batch)], axis=0))
-    left = jnp.concatenate(lefts, axis=1)
-    high, middle, low = split_three(rel_ref[0:1, :])
-    row = lax.broadcasted_iota(jnp.int32, (8, HD), 0)
-    tail = jnp.where(row == 0, high, jnp.where(row == 1, middle, jnp.where(row == 2, low, 0.0)))
-    tail = jnp.concatenate([tail, jnp.zeros((8, width - HD), F32)], axis=1).astype(BF16)
-    for g in range(groups):
-        mixed = jnp.dot(left, w_ref[:, g * width : (g + 1) * width], preferred_element_type=F32)
-        out_ref[g, :rows] = mixed.astype(BF16)
-        out_ref[g, rows:] = tail
-
-
-def final_body(flag_ref, part_ref, cache_ref, img_ref, mod_ref, out_ref, new_ref, rel_ref):
-    groups = part_ref.shape[0]
-    batch = img_ref.shape[0]
-    rows = batch * IMG_R
-    mixed = part_ref[0, :rows].astype(F32)
-    rel = part_ref[0, rows:, :HD].astype(F32)
-    for g in range(1, groups):
-        mixed = mixed + part_ref[g, :rows].astype(F32)
-        rel = rel + part_ref[g, rows:, :HD].astype(F32)
-    for b in range(batch):
+    mixed = jnp.zeros((rows, img_ref.shape[2]), F32)
+    for k, w_ref in enumerate(w_refs):
+        source = lax.rem(tp_ref[0] + groups - k, groups)
+        lefts = []
+        for h in range(heads):
+            lefts.append(
+                jnp.concatenate([att_ref[b * heads + h, source] for b in range(batch)], axis=0)
+            )
+        mixed = mixed + jnp.dot(
+            jnp.concatenate(lefts, axis=1), w_ref[...], preferred_element_type=F32
+        )
+    idle = jnp.int32(0)
+    for b in range(batch - 1, -1, -1):
+        idle = jnp.where(flag_ref[b] == 1, idle, b)
         gate = mod_ref[2, b : b + 1].astype(F32)
         resid = gate * mixed[b * IMG_R : (b + 1) * IMG_R]
         fresh = jnp.where(flag_ref[b] == 1, resid, cache_ref[b])
         new_ref[b] = fresh
         out_ref[b] = img_ref[b].astype(F32) + fresh
-    sums = jnp.sum(rel, axis=0, keepdims=True)
+    sums = jnp.zeros((IMG_R, HD), F32)
+    for z in range(groups):
+        sums = sums + att_ref[idle * heads, z].astype(F32)
+    sums = jnp.sum(sums, axis=0, keepdims=True)
     lane = lax.broadcasted_iota(jnp.int32, (1, HD), 1)
     for b in range(batch):
         numer = jnp.sum(jnp.where(lane == b, sums, 0.0))
@@ -222,10 +238,24 @@
     deep = w_qkv.shape[0]
     heads = columns // HD
 
-    pads = jnp.zeros((batch, ROWS - img_rows - txt.shape[1] - 2, width), BF16)
-    joined = jnp.concatenate(
-        [img, txt, modulation[0][:, None], modulation[1][:, None], pads], axis=1
-    ).reshape(batch * ROWS, width)
+    tp_index = lax.axis_index("tp").astype(jnp.int32)[None]
+    blocks = list(
+        call(
+            deal_body,
+            (jax.ShapeDtypeStruct((output_weight.shape[0], width), BF16),) * tps,
+            [SMEM, VMEM],
+            12,
+        )(tp_index, output_weight)
+    )
+    for k in range(1, tps):
+        blocks[k] = lax.ppermute(blocks[k], "tp", [(i, (i + k) % tps) for i in range(tps)])
+
+    joined = call(
+        join_body,
+        jax.ShapeDtypeStruct((batch * ROWS, width), BF16),
+        [VMEM] * 3,
+        4,
+    )(img, txt, modulation)
     wide = lax.all_gather(joined, "tp", axis=0, tiled=False)
 
     weight = w_qkv.transpose(1, 0, 2).reshape(kinds * deep, columns)
@@ -235,7 +265,6 @@
     weight = weight.reshape(xs, near, far, kinds, deep, columns)
     other = lax.ppermute(weight, "seq_2", [(0, 1), (1, 0)])
 
-    tp_index = lax.axis_index("tp").astype(jnp.int32)[None]
     core_index = lax.axis_index("seq_2").astype(jnp.int32)[None]
     modded, rel = call(
         norm_body,
@@ -260,34 +289,25 @@
 
     mine = lax.axis_index(AXIS_Y) // heads
     limit = lax.dynamic_slice_in_dim(text_len, mine, 1)
-    attended, rel = call(
+    flag = lax.dynamic_slice_in_dim(refresh, mine, 1)
+    attended = call(
         attend_body,
-        (
-            jax.ShapeDtypeStruct((ys, IMG_R, HD), BF16),
-            jax.ShapeDtypeStruct((8, HD), F32),
-        ),
-        [SMEM, SMEM, VMEM, VMEM, VMEM],
+        jax.ShapeDtypeStruct((ys, tps, IMG_R, HD), BF16),
+        [SMEM, SMEM, SMEM, VMEM, VMEM, VMEM],
         24,
-    )(limit, core_index, pairs, gathered, partner)
-
-    attended = swap(attended, AXIS_Y)
-    parts = call(
-        mix_body,
-        jax.ShapeDtypeStruct((tps, batch * IMG_R + 8, width), BF16),
-        [VMEM] * 3,
-        12,
-    )(attended, output_weight, rel)
-    parts = swap(parts, "tp")
+    )(limit, flag, core_index, pairs, gathered, partner)
+
+    attended = swap(attended.reshape(ys * tps, IMG_R, HD), AXIS_Y + ("tp",))
+    attended = attended.reshape(ys, tps, IMG_R, HD)
 
     shape = jax.ShapeDtypeStruct((batch, img_rows, width), F32)
-    out_img, new_cache, ratio = call(
+    return call(
         final_body,
         (shape, shape, jax.ShapeDtypeStruct((batch,), F32)),
-        [SMEM, VMEM, VMEM, VMEM, VMEM],
-        8,
+        [SMEM, SMEM] + [VMEM] * (tps + 4),
+        12,
         (VMEM, VMEM, SMEM),
-    )(refresh, parts, cache, img, modulation)
-    return (out_img, new_cache, ratio)
+    )(tp_index, refresh, attended, *blocks, cache, img, modulation)
 
 
 def solution(mesh):

time: 164 us -> 185 us (1.13)
  the two profiles are of different devices: /device:TPU:2 before, /device:TPU:65 now
where the time goes in v5:
time: 185 us; the launch traced here: 184 us
  blocking collectives  97.2 us (53%)
  starting transfers between devices  45.8 us (25%)
  waiting for transfers between devices  28.6 us (15%)
  Pallas kernels  9.72 us (5%)
  local copies, waits for them, and re-layouts  2.33 us (1%)
    all_to_all x4, blocking collectives, swap(): return lax.all_to_all(value, axis, 0, 0, tiled=True)  70.3 us
    ppermute x7, waiting for transfers between devices, local(): lax.ppermute(blocks[k], 'tp', [(i, (i + k) % tps) for i in range(tps)])  28.1 us
    all_gather x1, blocking collectives, local(): wide = lax.all_gather(joined, 'tp', axis=0, tiled=False)  26.8 us
    ppermute x7, starting transfers between devices, local(): lax.ppermute(blocks[k], 'tp', [(i, (i + k) % tps) for i in range(tps)])  24.7 us
    ppermute x1, starting transfers between devices, local(): partner = lax.ppermute(gathered, 'seq_2', [(0, 1), (1, 0)])  9.9 us
    ppermute x1, starting transfers between devices, local(): other = lax.ppermute(weight, 'seq_2', [(0, 1), (1, 0)])  6.69 us
    all_to_all x1, starting transfers between devices, swap(): return lax.all_to_all(value, axis, 0, 0, tiled=True)  4.5 us
  transfers between devices with their start and end apart: 10, of which 6 were waited for; matrix products, arithmetic and copies ran while one was open for 1% of the time, Pallas kernels for 1%

profile of v5, /device:TPU:65, one launch (start us, length us, event | category | flops | bytes accessed | tf_op | source)
XLA Modules:
  0.0 184.5 jit_solution(13893279201924186439)
XLA Ops:
  0.6 0.9 broadcast_in_dim.29
  1.5 16.6 %all_to_all.25 = bf16[4,144,256]{2,1,0:T(8,128)(2,1)S(1)} all-to-all(bf16[4,144,256]{2,1,0:T(8,128)(2,1)S(1)} %broadcast_in_dim.29), channel_id=1, replica_groups=mesh['seq_0'=4,'seq_1a'=4,'seq_1b'=2,'seq_2'=2,'tp'=8] {'seq_1a'}, dimensions={0} | all-to-all | bytes 589824 | tf_op jit(solution)/shard_map/all_to_all | solution.py:41
  18.2 0.2 broadcast_in_dim.31
  18.3 0.0 copy-start.1
  18.3 0.0 copy-start.4
  18.4 0.0 copy-start.5
  18.4 0.0 copy-start.3
  18.4 30.3 %all_to_all.26 = bf16[8,576,256]{2,1,0:T(8,128)(2,1)S(1)} all-to-all(bf16[8,576,256]{2,1,0:T(8,128)(2,1)S(1)} %broadcast_in_dim.31), channel_id=1, replica_groups=mesh['seq_0'=4,'seq_1a'=4,'seq_1b'=2,'seq_2'=2,'tp'=8] {'seq_0','seq_1b'}, dimensions={0} | all-to-all | bytes 4718592 | tf_op jit(solution)/shard_map/all_to_all | solution.py:41
  48.6 6.7 %collective-permute-start = (bf16[4,2,4,3,48,256]{5,4,3,2,1,0:T(8,128)(2,1)S(1)}, bf16[4,2,4,3,48,256]{5,4,3,2,1,0:T(8,128)(2,1)}, u32[]{:S(2)}, u32[]{:S(2)}) collective-permute-start(bf16[4,2,4,3,48,256]{5,4,3,2,1,0:T(8,128)(2,1)S(1)} %bitcast.10), channel_id=1, source_target_pairs={{0,8},{8,0},{1,9},{9,1},{2,10},{10,2},{3,11},{11,3},{4,12},{12,4},... | collective-permute-start | bytes 7077896 | tf_op jit(solution)/shard_map/ppermute | solution.py:266
  55.3 0.0 copy-done.1
  55.4 0.0 copy-done.4
  55.4 0.0 copy-done.5
  55.4 26.8 %all-gather = bf16[1280,384]{1,0:T(8,128)(2,1)S(1)} all-gather(bf16[160,384]{1,0:T(8,128)(2,1)S(1)} %shard_map.121), channel_id=2, replica_groups=mesh['seq_0'=4,'seq_1a'=4,'seq_1b'=2,'seq_2'=2,'tp'=8] {'tp'}, dimensions={0}, use_global_device_ids=true | all-gather | bytes 1105920 | tf_op jit(solution)/shard_map/all_gather | solution.py:259
  82.2 0.0 copy-done.3
  82.2 1.3 shard_map.122
  83.5 0.0 collective-permute-done.other_ref
  83.5 0.0 copy-done.6
  83.5 2.9 %shard_map.123 = bf16[8,40,384]{2,1,0:T(8,128)(2,1)S(1)} custom-call(s32[1]{0:T(128)} %bitcast.1.core_ref, bf16[8,160,384]{2,1,0:T(8,128)(2,1)S(1)} %get-tuple-element.13.mod_ref, bf16[4,2,4,3,48,256]{5,4,3,2,1,0:T(8,128)(2,1)S(1)} %bitcast.11, bf16[4,2,4,3,48,256]{5,4,3,2,1,0:T(8,128)(2,1)} %collective-permute-done.other_ref, f32[2,256]{1,0:T(2,128)S(1)} %copy-done.6, ...), custom_call_target="tpu_custom_call" | custom-call | tf_op jit(solution)/shard_map/pallas_call | solution.py:279
  86.4 0.0 copy-start.8
  86.4 0.0 copy-start.7
  86.5 13.3 %all_to_all.27.qkv_ref = bf16[8,40,384]{2,1,0:T(8,128)(2,1)S(1)} all-to-all(bf16[8,40,384]{2,1,0:T(8,128)(2,1)S(1)} %shard_map.123), channel_id=1, replica_groups=mesh['seq_0'=4,'seq_1a'=4,'seq_1b'=2,'seq_2'=2,'tp'=8] {'seq_1a','seq_1b'}, dimensions={0} | all-to-all | bytes 491520 | tf_op jit(solution)/shard_map/all_to_all | solution.py:41
  99.8 0.0 copy-start
  99.8 10.2 %all_to_all.28.own_ref = bf16[4,8,40,256]{3,2,1,0:T(8,128)(2,1)S(1)} all-to-all(bf16[4,8,40,256]{3,2,1,0:T(8,128)(2,1)S(1)} %broadcast_in_dim.32), channel_id=1, replica_groups=mesh['seq_0'=4,'seq_1a'=4,'seq_1b'=2,'seq_2'=2,'tp'=8] {'seq_0'}, dimensions={0} | all-to-all | bytes 1310720 | tf_op jit(solution)/shard_map/all_to_all | solution.py:41
  110.0 9.9 %collective-permute-start.1 = (bf16[4,8,40,256]{3,2,1,0:T(8,128)(2,1)S(1)}, bf16[4,8,40,256]{3,2,1,0:T(8,128)(2,1)S(1)}, u32[]{:S(2)}, u32[]{:S(2)}) collective-permute-start(bf16[4,8,40,256]{3,2,1,0:T(8,128)(2,1)S(1)} %all_to_all.28.own_ref), channel_id=1, source_target_pairs={{0,8},{8,0},{1,9},{9,1},{2,10},{10,2},{3,11},{11,3},{4,12},{12,4},... | collective-permute-start | bytes 1966088 | tf_op jit(solution)/shard_map/ppermute | solution.py:288
  119.9 0.6 dynamic_slice.6.limit_ref
  120.5 0.0 copy-done.7
  120.5 0.6 dynamic_slice.7.flag_ref
  121.1 0.5 collective-permute-done.1.other_ref
  121.6 3.6 %shard_map.124 = bf16[8,8,32,128]{3,2,1,0:T(8,128)(2,1)} custom-call(s32[1]{0:T(128)} %dynamic_slice.6.limit_ref, s32[1]{0:T(128)} %dynamic_slice.7.flag_ref, s32[1]{0:T(128)} %bitcast.1.core_ref, bf16[8,40,384]{2,1,0:T(8,128)(2,1)S(1)} %all_to_all.27.qkv_ref, bf16[4,8,40,256]{3,2,1,0:T(8,128)(2,1)S(1)} %all_to_all.28.own_ref, ...), custom_call_target="tpu_custom_call" | custom-call | tf_op jit(solution)/shard_map/pallas_call | solution.py:293
  125.2 4.5 %all-to-all-start.4 = ((bf16[64,32,128]{2,1,0:T(8,128)(2,1)}), bf16[64,32,128]{2,1,0:T(8,128)(2,1)S(1)}, u32[]{:S(2)}, u32[]{:S(2)}) async-start(bf16[64,32,128]{2,1,0:T(8,128)(2,1)} %bitcast.7), calls=%async_computation.4 | async-start | bytes 1048576 | tf_op jit(solution)/shard_map/all_to_all | solution.py:41
  129.7 0.0 copy-done
  129.7 0.2 shard_map.125
  129.9 3.1 %collective-permute-start.2 = (bf16[256,384]{1,0:T(8,128)(2,1)S(1)}, bf16[256,384]{1,0:T(8,128)(2,1)S(1)}, u32[]{:S(2)}, u32[]{:S(2)}) collective-permute-start(bf16[256,384]{1,0:T(8,128)(2,1)S(1)} %get-tuple-element.16), channel_id=1, source_target_pairs={{0,1},{1,2},{2,3},{3,4},{4,5},{5,6},{6,7},{7,0},{8,9},{9,10},{10,1... | collective-permute-start | bytes 589832 | tf_op jit(solution)/shard_map/ppermute | solution.py:251
  133.0 5.2 %collective-permute-start.3 = (bf16[256,384]{1,0:T(8,128)(2,1)S(1)}, bf16[256,384]{1,0:T(8,128)(2,1)S(1)}, u32[]{:S(2)}, u32[]{:S(2)}) collective-permute-start(bf16[256,384]{1,0:T(8,128)(2,1)S(1)} %get-tuple-element.17), channel_id=1, source_target_pairs={{0,2},{1,3},{2,4},{3,5},{4,6},{5,7},{6,0},{7,1},{8,10},{9,11},{10,... | collective-permute-start | bytes 589832 | tf_op jit(solution)/shard_map/ppermute | solution.py:251
  138.2 2.2 %collective-permute-start.4 = (bf16[256,384]{1,0:T(8,128)(2,1)S(1)}, bf16[256,384]{1,0:T(8,128)(2,1)S(1)}, u32[]{:S(2)}, u32[]{:S(2)}) collective-permute-start(bf16[256,384]{1,0:T(8,128)(2,1)S(1)} %get-tuple-element.18), channel_id=1, source_target_pairs={{0,3},{1,4},{2,5},{3,6},{4,7},{5,0},{6,1},{7,2},{8,11},{9,12},{10,... | collective-permute-start | bytes 589832 | tf_op jit(solution)/shard_map/ppermute | solution.py:251
  140.4 4.9 %collective-permute-start.5 = (bf16[256,384]{1,0:T(8,128)(2,1)S(1)}, bf16[256,384]{1,0:T(8,128)(2,1)S(1)}, u32[]{:S(2)}, u32[]{:S(2)}) collective-permute-start(bf16[256,384]{1,0:T(8,128)(2,1)S(1)} %get-tuple-element.19), channel_id=1, source_target_pairs={{0,4},{1,5},{2,6},{3,7},{4,0},{5,1},{6,2},{7,3},{8,12},{9,13},{10,... | collective-permute-start | bytes 589832 | tf_op jit(solution)/shard_map/ppermute | solution.py:251
  145.3 3.6 %collective-permute-start.6 = (bf16[256,384]{1,0:T(8,128)(2,1)S(1)}, bf16[256,384]{1,0:T(8,128)(2,1)S(1)}, u32[]{:S(2)}, u32[]{:S(2)}) collective-permute-start(bf16[256,384]{1,0:T(8,128)(2,1)S(1)} %get-tuple-element.20), channel_id=1, source_target_pairs={{0,5},{1,6},{2,7},{3,0},{4,1},{5,2},{6,3},{7,4},{8,13},{9,14},{10,... | collective-permute-start | bytes 589832 | tf_op jit(solution)/shard_map/ppermute | solution.py:251
  148.9 0.0 collective-permute-done.2.refs_1_
  148.9 3.8 %collective-permute-start.7 = (bf16[256,384]{1,0:T(8,128)(2,1)S(1)}, bf16[256,384]{1,0:T(8,128)(2,1)S(1)}, u32[]{:S(2)}, u32[]{:S(2)}) collective-permute-start(bf16[256,384]{1,0:T(8,128)(2,1)S(1)} %get-tuple-element.21), channel_id=1, source_target_pairs={{0,6},{1,7},{2,0},{3,1},{4,2},{5,3},{6,4},{7,5},{8,14},{9,15},{10,... | collective-permute-start | bytes 589832 | tf_op jit(solution)/shard_map/ppermute | solution.py:251
  152.7 6.1 %collective-permute-done.3.refs_2_ = bf16[256,384]{1,0:T(8,128)(2,1)S(1)} collective-permute-done((bf16[256,384]{1,0:T(8,128)(2,1)S(1)}, bf16[256,384]{1,0:T(8,128)(2,1)S(1)}, u32[]{:S(2)}, u32[]{:S(2)}) %collective-permute-start.3) | collective-permute-done | bytes 196640 | tf_op jit(solution)/shard_map/ppermute | solution.py:251
  158.8 1.9 %collective-permute-start.8 = (bf16[256,384]{1,0:T(8,128)(2,1)S(1)}, bf16[256,384]{1,0:T(8,128)(2,1)S(1)}, u32[]{:S(2)}, u32[]{:S(2)}) collective-permute-start(bf16[256,384]{1,0:T(8,128)(2,1)S(1)} %get-tuple-element.22), channel_id=1, source_target_pairs={{0,7},{1,0},{2,1},{3,2},{4,3},{5,4},{6,5},{7,6},{8,15},{9,8},{10,9... | collective-permute-start | bytes 589832 | tf_op jit(solution)/shard_map/ppermute | solution.py:251
  160.7 8.3 %collective-permute-done.4.refs_3_ = bf16[256,384]{1,0:T(8,128)(2,1)S(1)} collective-permute-done((bf16[256,384]{1,0:T(8,128)(2,1)S(1)}, bf16[256,384]{1,0:T(8,128)(2,1)S(1)}, u32[]{:S(2)}, u32[]{:S(2)}) %collective-permute-start.4) | collective-permute-done | bytes 196640 | tf_op jit(solution)/shard_map/ppermute | solution.py:251
  169.1 0.0 collective-permute-done.5.refs_4_
  169.1 3.3 %collective-permute-done.6.refs_5_ = bf16[256,384]{1,0:T(8,128)(2,1)S(1)} collective-permute-done((bf16[256,384]{1,0:T(8,128)(2,1)S(1)}, bf16[256,384]{1,0:T(8,128)(2,1)S(1)}, u32[]{:S(2)}, u32[]{:S(2)}) %collective-permute-start.6) | collective-permute-done | bytes 196640 | tf_op jit(solution)/shard_map/ppermute | solution.py:251
  172.4 1.1 collective-permute-done.7.refs_6_
  173.5 9.2 %collective-permute-done.8.refs_7_ = bf16[256,384]{1,0:T(8,128)(2,1)S(1)} collective-permute-done((bf16[256,384]{1,0:T(8,128)(2,1)S(1)}, bf16[256,384]{1,0:T(8,128)(2,1)S(1)}, u32[]{:S(2)}, u32[]{:S(2)}) %collective-permute-start.8) | collective-permute-done | bytes 196640 | tf_op jit(solution)/shard_map/ppermute | solution.py:251
  182.7 0.0 all-to-all-done.4
  182.7 1.8 shard_map.126
  (7 shorter events, 0.1 us)
Async XLA Ops:
  18.3 37.0 %copy-start.1 = (bf16[4,32,384]{2,1,0:T(8,128)(2,1)S(1)}, bf16[4,32,384]{2,1,0:T(8,128)(2,1)}, u32[]{:S(2)}) copy-start(bf16[4,32,384]{2,1,0:T(8,128)(2,1)} %refs_9_.1) | copy-start | bytes 294916
  18.3 37.0 %copy-start.4 = (bf16[3,4,384]{2,1,0:T(4,128)(2,1)S(1)}, bf16[3,4,384]{2,1,0:T(4,128)(2,1)}, u32[]{:S(2)}) copy-start(bf16[3,4,384]{2,1,0:T(4,128)(2,1)} %refs_10_.1) | copy-start | bytes 27652
  18.4 37.0 %copy-start.5 = (bf16[4,4,384]{2,1,0:T(4,128)(2,1)S(1)}, bf16[4,4,384]{2,1,0:T(4,128)(2,1)}, u32[]{:S(2)}) copy-start(bf16[4,4,384]{2,1,0:T(4,128)(2,1)} %txt_ref.1) | copy-start | bytes 36868
  18.4 63.9 %copy-start.3 = (bf16[4,32,384]{2,1,0:T(8,128)(2,1)S(1)}, bf16[4,32,384]{2,1,0:T(8,128)(2,1)}, u32[]{:S(2)}) copy-start(bf16[4,32,384]{2,1,0:T(8,128)(2,1)} %prev_ref.1) | copy-start | bytes 294916
  48.6 34.9 %copy-start.6 = (f32[2,256]{1,0:T(2,128)S(1)}, f32[2,256]{1,0:T(2,128)}, u32[]{:S(2)}) copy-start(f32[2,256]{1,0:T(2,128)} %gain_ref.1) | copy-start | bytes 6148
  48.6 34.9 %collective-permute-start = (bf16[4,2,4,3,48,256]{5,4,3,2,1,0:T(8,128)(2,1)S(1)}, bf16[4,2,4,3,48,256]{5,4,3,2,1,0:T(8,128)(2,1)}, u32[]{:S(2)}, u32[]{:S(2)}) collective-permute-start(bf16[4,2,4,3,48,256]{5,4,3,2,1,0:T(8,128)(2,1)S(1)} %bitcast.10), channel_id=1, source_target_pairs={{0,8},{8,0},{1,9},{9,1},{2,10},{10,2},{3,11},{11,3},{4,12},{12,4},... | collective-permute-start | bytes 7077896 | tf_op jit(solution)/shard_map/ppermute | solution.py:266
  86.4 33.5 %copy-start.8 = (s32[4]{0:T(128)S(1)}, s32[4]{0:T(128)}, u32[]{:S(2)}) copy-start(s32[4]{0:T(128)} %param.18) | copy-start | bytes 52
  86.4 34.1 %copy-start.7 = (s32[4]{0:T(128)S(1)}, s32[4]{0:T(128)}, u32[]{:S(2)}) copy-start(s32[4]{0:T(128)} %flag_ref.1) | copy-start | bytes 52
  99.8 29.9 %copy-start = (bf16[256,3072]{1,0:T(8,128)(2,1)S(1)}, bf16[256,3072]{1,0:T(8,128)(2,1)}, u32[]{:S(2)}) copy-start(bf16[256,3072]{1,0:T(8,128)(2,1)} %w_ref.1) | copy-start | bytes 4718596
  110.0 11.6 %collective-permute-start.1 = (bf16[4,8,40,256]{3,2,1,0:T(8,128)(2,1)S(1)}, bf16[4,8,40,256]{3,2,1,0:T(8,128)(2,1)S(1)}, u32[]{:S(2)}, u32[]{:S(2)}) collective-permute-start(bf16[4,8,40,256]{3,2,1,0:T(8,128)(2,1)S(1)} %all_to_all.28.own_ref), channel_id=1, source_target_pairs={{0,8},{8,0},{1,9},{9,1},{2,10},{10,2},{3,11},{11,3},{4,12},{12,4},... | collective-permute-start | bytes 1966088 | tf_op jit(solution)/shard_map/ppermute | solution.py:288
  121.1 61.6 %copy-start.2 = (f32[4,32,384]{2,1,0:T(8,128)S(1)}, f32[4,32,384]{2,1,0:T(8,128)}, u32[]{:S(2)}) copy-start(f32[4,32,384]{2,1,0:T(8,128)} %refs_8_.1) | copy-start | bytes 589828
  125.2 57.5 %all-to-all-start.4 = ((bf16[64,32,128]{2,1,0:T(8,128)(2,1)}), bf16[64,32,128]{2,1,0:T(8,128)(2,1)S(1)}, u32[]{:S(2)}, u32[]{:S(2)}) async-start(bf16[64,32,128]{2,1,0:T(8,128)(2,1)} %bitcast.7), calls=%async_computation.4 | async-start | bytes 1048576 | tf_op jit(solution)/shard_map/all_to_all | solution.py:41
  129.9 19.0 %collective-permute-start.2 = (bf16[256,384]{1,0:T(8,128)(2,1)S(1)}, bf16[256,384]{1,0:T(8,128)(2,1)S(1)}, u32[]{:S(2)}, u32[]{:S(2)}) collective-permute-start(bf16[256,384]{1,0:T(8,128)(2,1)S(1)} %get-tuple-element.16), channel_id=1, source_target_pairs={{0,1},{1,2},{2,3},{3,4},{4,5},{5,6},{6,7},{7,0},{8,9},{9,10},{10,1... | collective-permute-start | bytes 589832 | tf_op jit(solution)/shard_map/ppermute | solution.py:251
  133.0 25.8 %collective-permute-start.3 = (bf16[256,384]{1,0:T(8,128)(2,1)S(1)}, bf16[256,384]{1,0:T(8,128)(2,1)S(1)}, u32[]{:S(2)}, u32[]{:S(2)}) collective-permute-start(bf16[256,384]{1,0:T(8,128)(2,1)S(1)} %get-tuple-element.17), channel_id=1, source_target_pairs={{0,2},{1,3},{2,4},{3,5},{4,6},{5,7},{6,0},{7,1},{8,10},{9,11},{10,... | collective-permute-start | bytes 589832 | tf_op jit(solution)/shard_map/ppermute | solution.py:251
  138.2 30.8 %collective-permute-start.4 = (bf16[256,384]{1,0:T(8,128)(2,1)S(1)}, bf16[256,384]{1,0:T(8,128)(2,1)S(1)}, u32[]{:S(2)}, u32[]{:S(2)}) collective-permute-start(bf16[256,384]{1,0:T(8,128)(2,1)S(1)} %get-tuple-element.18), channel_id=1, source_target_pairs={{0,3},{1,4},{2,5},{3,6},{4,7},{5,0},{6,1},{7,2},{8,11},{9,12},{10,... | collective-permute-start | bytes 589832 | tf_op jit(solution)/shard_map/ppermute | solution.py:251
  140.4 28.6 %collective-permute-start.5 = (bf16[256,384]{1,0:T(8,128)(2,1)S(1)}, bf16[256,384]{1,0:T(8,128)(2,1)S(1)}, u32[]{:S(2)}, u32[]{:S(2)}) collective-permute-start(bf16[256,384]{1,0:T(8,128)(2,1)S(1)} %get-tuple-element.19), channel_id=1, source_target_pairs={{0,4},{1,5},{2,6},{3,7},{4,0},{5,1},{6,2},{7,3},{8,12},{9,13},{10,... | collective-permute-start | bytes 589832 | tf_op jit(solution)/shard_map/ppermute | solution.py:251
  145.3 27.1 %collective-permute-start.6 = (bf16[256,384]{1,0:T(8,128)(2,1)S(1)}, bf16[256,384]{1,0:T(8,128)(2,1)S(1)}, u32[]{:S(2)}, u32[]{:S(2)}) collective-permute-start(bf16[256,384]{1,0:T(8,128)(2,1)S(1)} %get-tuple-element.20), channel_id=1, source_target_pairs={{0,5},{1,6},{2,7},{3,0},{4,1},{5,2},{6,3},{7,4},{8,13},{9,14},{10,... | collective-permute-start | bytes 589832 | tf_op jit(solution)/shard_map/ppermute | solution.py:251
  148.9 24.6 %collective-permute-start.7 = (bf16[256,384]{1,0:T(8,128)(2,1)S(1)}, bf16[256,384]{1,0:T(8,128)(2,1)S(1)}, u32[]{:S(2)}, u32[]{:S(2)}) collective-permute-start(bf16[256,384]{1,0:T(8,128)(2,1)S(1)} %get-tuple-element.21), channel_id=1, source_target_pairs={{0,6},{1,7},{2,0},{3,1},{4,2},{5,3},{6,4},{7,5},{8,14},{9,15},{10,... | collective-permute-start | bytes 589832 | tf_op jit(solution)/shard_map/ppermute | solution.py:251
  158.8 23.9 %collective-permute-start.8 = (bf16[256,384]{1,0:T(8,128)(2,1)S(1)}, bf16[256,384]{1,0:T(8,128)(2,1)S(1)}, u32[]{:S(2)}, u32[]{:S(2)}) collective-permute-start(bf16[256,384]{1,0:T(8,128)(2,1)S(1)} %get-tuple-element.22), channel_id=1, source_target_pairs={{0,7},{1,0},{2,1},{3,2},{4,3},{5,4},{6,5},{7,6},{8,15},{9,8},{10,9... | collective-permute-start | bytes 589832 | tf_op jit(solution)/shard_map/ppermute | solution.py:251

commit v6 on v0

v6 whole, which is shorter than its diff:
```python
import functools

import jax
import jax.numpy as jnp
from jax import lax
from jax.experimental import pallas as pl
from jax.experimental.pallas import tpu as pltpu
from jax.sharding import Mesh
from jax.sharding import PartitionSpec as P


X, FAR, NEAR, CORE, TP = "seq_0", "seq_1a", "seq_1b", "seq_2", "tp"
SEQ = (X, FAR, NEAR, CORE)
HD = 128
EPS = 0.1
NEG = -1e30
F32 = jnp.float32
BF16 = jnp.bfloat16

VMEM = pl.BlockSpec(memory_space=pltpu.VMEM)
SMEM = pl.BlockSpec(memory_space=pltpu.SMEM)


def call(body, out_shape, in_specs, mebibytes, outs=None):
    outs = outs or jax.tree.map(lambda _: VMEM, out_shape)
    return pl.pallas_call(
        body,
        out_shape=out_shape,
        in_specs=in_specs,
        out_specs=outs,
        compiler_params=pltpu.CompilerParams(vmem_limit_bytes=mebibytes << 20),
    )


def shaped(*shape, dtype=BF16):
    return jax.ShapeDtypeStruct(shape, dtype)


def swap(value, axis):
    return lax.all_to_all(value, axis, 0, 0, tiled=True)


def split_three(value):
    high = value.astype(BF16).astype(F32)
    rest = value - high
    middle = rest.astype(BF16).astype(F32)
    return high, middle, rest - middle


def stacked_parts(value, rows):
    row = lax.broadcasted_iota(jnp.int32, (rows, value.shape[1]), 0)
    high, middle, low = split_three(value)
    return jnp.where(row == 0, high, jnp.where(row == 1, middle, jnp.where(row == 2, low, 0.0)))


def pack_body(w_ref, img_ref, prev_ref, txt_ref, out_ref):
    kinds, deep, columns = w_ref.shape
    batch, img_rows, width = img_ref.shape
    cores = columns // HD
    img_half = img_rows // cores
    txt_half = txt_ref.shape[1] // cores
    for b in range(batch):
        for c in range(cores):
            to = b * cores + c
            for kind in range(kinds):
                out_ref[to, :deep, kind * HD : (kind + 1) * HD] = w_ref[
                    kind, :, c * HD : (c + 1) * HD
                ]
            at = deep
            for ref in (img_ref, prev_ref):
                out_ref[to, at : at + img_half] = ref[b, c * img_half : (c + 1) * img_half]
                at += img_half
            text = txt_ref[b].astype(F32)[c * txt_half : (c + 1) * txt_half]
            text = jnp.concatenate([text, jnp.zeros((8 - txt_half, width), F32)], axis=0)
            out_ref[to, at : at + 8] = text.astype(BF16)


def spread_body(got_ref, out_ref):
    copies = out_ref.shape[0]
    sources = got_ref.shape[0]
    deep = out_ref.shape[1] // sources
    for copy in range(copies):
        for source in range(sources):
            out_ref[copy, source * deep : (source + 1) * deep] = got_ref[source, :deep]


def join_body(deep, img_half, txt_half, far_ref, got_ref, mod_ref, out_ref):
    sources = got_ref.shape[0]
    width = got_ref.shape[2]
    for source in range(sources):
        out_ref[source * img_half : (source + 1) * img_half] = got_ref[
            source, deep : deep + img_half
        ]
    at = deep + 2 * img_half
    texts = [got_ref[source, at : at + 8].astype(F32)[:txt_half] for source in range(sources)]
    vectors = []
    for which in range(2):
        chosen = mod_ref[which, 0:1].astype(F32)
        for b in range(1, mod_ref.shape[1]):
            chosen = jnp.where(far_ref[0] == b, mod_ref[which, b : b + 1].astype(F32), chosen)
        vectors.append(chosen)
    tail = jnp.concatenate(texts + vectors + [jnp.zeros((6, width), F32)], axis=0)
    out_ref[sources * img_half :] = tail.astype(BF16)


def norm_body(deep, place_ref, x_ref, got_ref, mod_ref):
    groups, rows, width = x_ref.shape
    sources = got_ref.shape[0]
    vectors = rows - 8
    features = groups * width
    sums = jnp.zeros((rows, 1), F32)
    for g in range(groups):
        sums = sums + jnp.sum(x_ref[g].astype(F32), axis=1, keepdims=True)
    center = sums / features
    squares = jnp.zeros((rows, 1), F32)
    for g in range(groups):
        squares = squares + jnp.sum(
            jnp.square(x_ref[g].astype(F32) - center), axis=1, keepdims=True
        )
    inv = lax.rsqrt(squares / features + EPS)
    for g in range(groups):
        values = x_ref[g].astype(F32)
        shift = values[vectors : vectors + 1]
        scale = values[vectors + 1 : vectors + 2]
        mod_ref[g] = ((values - center) * inv * (1.0 + scale) + shift).astype(BF16)
    far = place_ref[0]
    own = mod_ref.at[place_ref[1]]
    img_half = (got_ref.shape[1] - deep - 8) // 2
    numer = jnp.zeros((img_half, width), F32)
    denom = jnp.zeros((img_half, width), F32)
    for source in range(sources):
        at = deep + img_half
        previous = got_ref[source, at : at + img_half].astype(F32)
        current = own[source * img_half : (source + 1) * img_half].astype(F32)
        numer = numer + jnp.abs(current - previous)
        denom = denom + jnp.abs(previous)
    lane = lax.broadcasted_iota(jnp.int32, (1, width), 1)
    line = jnp.where(lane == far, jnp.sum(numer), 0.0)
    line = jnp.where(lane == 4 + far, jnp.sum(denom), line)
    mod_ref[0, vectors:] = stacked_parts(line, 8).astype(BF16)


def project_body(core_ref, own_ref, other_ref, w_ref, gain_ref, query_ref, pair_ref):
    groups, rows, width = own_ref.shape
    _, sources, deep, columns = w_ref.shape
    near = cores = 2
    ys = near * sources // cores
    per_group = width // deep
    total = jnp.zeros((2 * rows, columns), F32)
    for g in range(groups):
        pieces = []
        for step in range(per_group):
            flat = g * per_group + step
            core = flat % cores
            y = flat // cores % ys
            x = flat // cores // ys
            pieces.append(w_ref[x * near + y % near, y // near * cores + core])
        left = jnp.concatenate([own_ref[g], other_ref[g]], axis=0)
        total = total + jnp.dot(
            left, jnp.concatenate(pieces, axis=0), preferred_element_type=F32
        )
    parts = []
    for kind in range(2):
        part = total[:, kind * HD : (kind + 1) * HD]
        gain = jnp.where(
            core_ref[0] == 0, gain_ref[kind : kind + 1, :HD], gain_ref[kind : kind + 1, HD:]
        )
        mean = jnp.mean(jnp.square(part), axis=1, keepdims=True)
        parts.append(part * lax.rsqrt(mean + EPS) * gain)
    query, keyed = parts
    valued = total[:, 2 * HD :].astype(BF16)
    img = query_ref.shape[1]
    for half, ref in enumerate((own_ref, other_ref)):
        at = half * rows
        query_ref[half] = query[at : at + img].astype(BF16)
        carried = ref[0, rows - 8 :, :HD]
        keys = keyed[at : at + rows - 8].astype(BF16)
        for copy in range(pair_ref.shape[0]):
            pair_ref[copy, half, : rows - 8, :HD] = keys
            pair_ref[copy, half, rows - 8 :, :HD] = carried
            pair_ref[copy, half, :, HD:] = valued[at : at + rows]


def attend_body(img_half, txt_half, limit_ref, place_ref, query_ref, pair_ref, out_ref):
    blocks, halves, rows, _ = pair_ref.shape
    sources = out_ref.shape[0]
    img = sources * img_half
    txt = sources * txt_half
    count = blocks * rows
    far, core = place_ref[0], place_ref[2]
    query = query_ref[...].reshape(2 * img, HD)
    index = lax.broadcasted_iota(jnp.int32, (1, count), 1)
    slot = index % rows
    block = index // rows
    source = (slot - img) // txt_half
    y = source // 2 * 2 + block % 2
    device = (block // 2 * 8 + y) * 2 + source % 2
    scores_of, valid_of = [], []
    rel = jnp.zeros((1, HD), F32)
    for half in range(halves):
        actual = jnp.where(half == 0, core, 1 - core)
        keys = pair_ref[:, half, :, :HD].reshape(count, HD)
        scores = lax.dot_general(
            query, keys, (((1,), (1,)), ((), ())), preferred_element_type=F32
        ) * (1.0 / HD**0.5)
        text = device * 4 + actual * txt_half + (slot - img) % txt_half
        valid = (slot < img) | ((slot < img + txt) & (text < limit_ref[far]))
        scores_of.append(jnp.where(valid, scores, NEG))
        valid_of.append(valid)
        for b in range(blocks):
            carried = pair_ref[b, half, rows - 8 :, :HD].astype(F32)
            rel = rel + jnp.sum(carried, axis=0, keepdims=True)
    top = functools.reduce(
        jnp.maximum, [jnp.max(s, axis=1, keepdims=True) for s in scores_of]
    )
    total = jnp.zeros((2 * img, 1), F32)
    summed = jnp.zeros((2 * img, HD), F32)
    for half in range(halves):
        weights = jnp.where(valid_of[half], jnp.exp(scores_of[half] - top), 0.0)
        total = total + jnp.sum(weights, axis=1, keepdims=True)
        values = pair_ref[:, half, :, HD:].reshape(count, HD)
        summed = summed + jnp.dot(weights.astype(BF16), values, preferred_element_type=F32)
    attended = (summed / total).astype(BF16)
    tail = stacked_parts(rel, 8).astype(BF16)
    for half in range(halves):
        actual = jnp.where(half == 0, core, 1 - core)
        at = pl.multiple_of(actual * img_half, img_half)
        for source in range(sources):
            start = half * img + source * img_half
            out_ref[source, pl.ds(at, img_half)] = attended[start : start + img_half]
    for source in range(sources):
        out_ref[source, 2 * img_half :] = tail


def slots_of(flag_ref, batch, count):
    order = [jnp.int32(0)] * count
    seen = jnp.int32(0)
    slot = []
    for b in range(batch):
        on = flag_ref[b] == 1
        slot.append(seen)
        for i in range(count):
            order[i] = jnp.where(on & (seen == i), jnp.int32(b), order[i])
        seen = seen + jnp.where(on, 1, 0)
    return order, slot


def mix_body(img_rows, flag_ref, att_ref, w_ref, out_ref):
    groups, rows, width = out_ref.shape
    heads = w_ref.shape[0] // HD
    batch = att_ref.shape[0] // heads
    slots = (rows - 8) // img_rows
    order, _ = slots_of(flag_ref, batch, slots)
    lefts = []
    for h in range(heads):
        lefts.append(
            jnp.concatenate([att_ref[order[i] * heads + h, :img_rows] for i in range(slots)], axis=0)
        )
    left = jnp.concatenate(lefts, axis=1)
    rel = jnp.zeros((8, HD), F32)
    for b in range(batch):
        rel = rel + att_ref[b * heads, img_rows:].astype(F32)
    tail = stacked_parts(jnp.sum(rel, axis=0, keepdims=True), 8)
    tail = jnp.concatenate([tail, jnp.zeros((8, width - HD), F32)], axis=1).astype(BF16)
    for g in range(groups):
        mixed = jnp.dot(left, w_ref[:, g * width : (g + 1) * width], preferred_element_type=F32)
        out_ref[g, : rows - 8] = mixed.astype(BF16)
        out_ref[g, rows - 8 :] = tail


def final_body(flag_ref, part_ref, cache_ref, img_ref, mod_ref, out_ref, new_ref, rel_ref, sum_ref):
    groups, rows, _ = part_ref.shape
    batch, img_rows, _ = img_ref.shape
    slots = (rows - 8) // img_rows
    mixed = part_ref[0].astype(F32)
    for g in range(1, groups):
        mixed = mixed + part_ref[g].astype(F32)
    sum_ref[...] = mixed
    _, slot = slots_of(flag_ref, batch, slots)
    for b in range(batch):
        gate = mod_ref[2, b : b + 1].astype(F32)
        at = pl.multiple_of(jnp.minimum(slot[b], slots - 1) * img_rows, img_rows)
        resid = gate * sum_ref[pl.ds(at, img_rows)]
        fresh = jnp.where(flag_ref[b] == 1, resid, cache_ref[b])
        new_ref[b] = fresh
        out_ref[b] = img_ref[b].astype(F32) + fresh
    sums = jnp.sum(mixed[rows - 8 :, :HD], axis=0, keepdims=True)
    lane = lax.broadcasted_iota(jnp.int32, (1, HD), 1)
    for b in range(batch):
        numer = jnp.sum(jnp.where(lane == b, sums, 0.0))
        denom = jnp.sum(jnp.where(lane == 4 + b, sums, 0.0))
        rel_ref[b] = numer / jnp.maximum(denom, 1.0)


def local(img, txt, prev_mod, cache, modulation, w_qkv, qk_gain, output_weight, text_len, refresh):
    batch, img_rows, width = img.shape
    xs, fars, nears, cores = (lax.axis_size(a) for a in SEQ)
    tps = lax.axis_size(TP)
    deep, kinds, _ = w_qkv.shape
    sources = fars * cores
    around = xs * nears
    img_half, txt_half = img_rows // cores, txt.shape[1] // cores
    rows = sources * (img_half + txt_half) + 8
    place = jnp.stack([lax.axis_index(a) for a in (FAR, TP, CORE)]).astype(jnp.int32)
    core_index = lax.axis_index(CORE).astype(jnp.int32)[None]
    far_index = lax.axis_index(FAR).astype(jnp.int32)[None]

    got = call(
        pack_body, shaped(sources, deep + 2 * img_half + 8, width), [VMEM] * 4, 8
    )(w_qkv.transpose(1, 0, 2), img, prev_mod, txt)
    got = swap(got, (FAR, CORE))
    weight = call(spread_body, shaped(around, sources * deep, kinds * HD), [VMEM], 8)(got)
    weight = swap(weight, (X, NEAR)).reshape(around, sources, deep, kinds * HD)

    joined = call(
        functools.partial(join_body, deep, img_half, txt_half),
        shaped(rows, width),
        [SMEM, VMEM, VMEM],
        8,
    )(far_index, got, modulation)
    wide = lax.all_gather(joined, TP, axis=0, tiled=False)
    own = call(
        functools.partial(norm_body, deep), shaped(tps, rows, width), [SMEM, VMEM, VMEM], 12
    )(place, wide, got)
    other = lax.ppermute(own, CORE, [(0, 1), (1, 0)])

    query, pairs = call(
        project_body,
        (shaped(2, sources * img_half, HD), shaped(around, 2, rows, 2 * HD)),
        [SMEM] + [VMEM] * 4,
        16,
    )(core_index, own, other, weight, qk_gain)
    pairs = swap(pairs, (X, NEAR))
    attended = call(
        functools.partial(attend_body, img_half, txt_half),
        shaped(sources, img_rows + 8, HD),
        [SMEM, SMEM, VMEM, VMEM],
        24,
    )(text_len, place, query, pairs)
    attended = swap(attended, (FAR, CORE))

    slots = batch - 1
    parts = call(
        functools.partial(mix_body, img_rows),
        shaped(tps, slots * img_rows + 8, width),
        [SMEM, VMEM, VMEM],
        12,
    )(refresh, attended, output_weight)
    parts = swap(parts, TP)

    whole = shaped(batch, img_rows, width, dtype=F32)
    return pl.pallas_call(
        final_body,
        out_shape=(whole, whole, shaped(batch, dtype=F32)),
        in_specs=[SMEM] + [VMEM] * 4,
        out_specs=(VMEM, VMEM, SMEM),
        scratch_shapes=[pltpu.VMEM((slots * img_rows + 8, width), F32)],
        compiler_params=pltpu.CompilerParams(vmem_limit_bytes=8 << 20),
    )(refresh, parts, cache, img, modulation)


def solution(mesh):
    finer = Mesh(mesh.devices.reshape(4, 4, 2, 2, mesh.shape["tp"]), SEQ + (TP,))
    in_specs = (
        P(None, SEQ, TP),
        P(None, SEQ, TP),
        P(None, SEQ, TP),
        P(None, SEQ, TP),
        P(None, None, TP),
        P(SEQ, None, TP),
        P(None, TP),
        P(TP, None),
        P(),
        P(),
    )
    out_specs = (P(None, SEQ, TP), P(None, SEQ, TP), P())

    return jax.shard_map(local, mesh=finer, in_specs=in_specs, out_specs=out_specs, check_vma=False)
```

time: 298 us -> 141 us (0.47)
  the two profiles are of different devices: /device:TPU:2 before, /device:TPU:1 now
where the time goes in v6:
time: 141 us; the launch traced here: 140 us
  blocking collectives  111 us (79%)
  starting transfers between devices  11.7 us (8%)
  Pallas kernels  8.36 us (6%)
  local copies, waits for them, and re-layouts  6.96 us (5%)
    all_to_all x4, blocking collectives, swap(): return lax.all_to_all(value, axis, 0, 0, tiled=True)  82.3 us
    all_gather x1, blocking collectives, local(): wide = lax.all_gather(joined, TP, axis=0, tiled=False)  28.7 us
    ppermute x1, starting transfers between devices, local(): other = lax.ppermute(own, CORE, [(0, 1), (1, 0)])  7 us
    unnamed x28, local copies, waits for them, and re-layouts  6.96 us
    all_to_all x1, starting transfers between devices, swap(): return lax.all_to_all(value, axis, 0, 0, tiled=True)  4.69 us
  transfers between devices with their start and end apart: 2, of which 1 were waited for; matrix products, arithmetic and copies ran while one was open for 0% of the time, Pallas kernels for 1%

profile of v6, /device:TPU:1, one launch (start us, length us, event | category | flops | bytes accessed | tf_op | source)
XLA Modules:
  0.0 140.1 jit_solution(13414194943581061230)
XLA Ops:
  0.6 0.0 copy-start.4
  0.6 0.9 copy-done.4
  1.5 0.0 copy-start.7
  1.5 0.9 copy-done.7
  2.4 0.0 copy-start.8
  2.4 0.9 copy-done.8
  3.3 0.0 copy-start.10
  3.3 0.7 copy-done.10
  4.0 0.1 shard_map.121
  4.1 25.9 %all_to_all.25.got_ref = bf16[8,88,384]{2,1,0:T(8,128)(2,1)S(1)} all-to-all(bf16[8,88,384]{2,1,0:T(8,128)(2,1)S(1)} %shard_map.121), channel_id=1, replica_groups=mesh['seq_0'=4,'seq_1a'=4,'seq_1b'=2,'seq_2'=2,'tp'=8] {'seq_1a','seq_2'}, dimensions={0} | all-to-all | bytes 1081344 | tf_op jit(solution)/shard_map/all_to_all | solution.py:40
  30.0 0.2 shard_map.124
  30.2 0.0 copy-start
  30.2 1.4 %copy-done = bf16[8,384,384]{2,1,0:T(8,128)(2,1)} copy-done((bf16[8,384,384]{2,1,0:T(8,128)(2,1)}, bf16[8,384,384]{2,1,0:T(8,128)(2,1)S(1)}, u32[]{:S(2)}) %copy-start) | copy-done | bytes 2359320
  31.6 0.0 copy-start.9
  31.6 4.7 %all-to-all-start.1 = ((bf16[8,384,384]{2,1,0:T(8,128)(2,1)}), bf16[8,384,384]{2,1,0:T(8,128)(2,1)S(1)}, u32[]{:S(2)}, u32[]{:S(2)}) async-start(bf16[8,384,384]{2,1,0:T(8,128)(2,1)} %copy-done), calls=%async_computation.1 | async-start | bytes 4718592 | tf_op jit(solution)/shard_map/all_to_all | solution.py:40
  36.3 0.1 pad_add_fusion.place_ref
  36.4 0.0 copy-done.9
  36.4 0.0 copy-start.11
  36.4 28.7 %all-gather = bf16[1216,384]{1,0:T(8,128)(2,1)S(1)} all-gather(bf16[152,384]{1,0:T(8,128)(2,1)S(1)} %shard_map.122), channel_id=2, replica_groups=mesh['seq_0'=4,'seq_1a'=4,'seq_1b'=2,'seq_2'=2,'tp'=8] {'tp'}, dimensions={0}, use_global_device_ids=true | all-gather | bytes 1050624 | tf_op jit(solution)/shard_map/all_gather | solution.py:321
  65.2 1.7 %shard_map.123.own_ref = bf16[8,152,384]{2,1,0:T(8,128)(2,1)S(1)} custom-call(s32[3]{0:T(128)S(1)} %pad_add_fusion.place_ref, bf16[8,152,384]{2,1,0:T(8,128)(2,1)S(1)} %bitcast.7, bf16[8,88,384]{2,1,0:T(8,128)(2,1)S(1)} %all_to_all.25.got_ref), custom_call_target="tpu_custom_call" | custom-call | tf_op jit(solution)/shard_map/pallas_call | solution.py:322
  66.9 7.0 %collective-permute-start = (bf16[8,152,384]{2,1,0:T(8,128)(2,1)S(1)}, bf16[8,152,384]{2,1,0:T(8,128)(2,1)S(1)}, u32[]{:S(2)}, u32[]{:S(2)}) collective-permute-start(bf16[8,152,384]{2,1,0:T(8,128)(2,1)S(1)} %shard_map.123.own_ref), channel_id=1, source_target_pairs={{0,8},{8,0},{1,9},{9,1},{2,10},{10,2},{3,11},{11,3},{4,12},{12,4},... | collective-permute-start | bytes 2801672 | tf_op jit(solution)/shard_map/ppermute | solution.py:325
  73.9 0.0 copy-start.1
  73.9 0.9 copy-done.1
  74.9 1.2 collective-permute-done.other_ref
  76.0 0.0 all-to-all-done.1
  76.0 0.0 copy-done.11
  76.0 0.0 copy-start.2
  76.0 1.2 copy-done.2
  77.2 1.5 %shard_map.125 = (bf16[2,128,128]{2,1,0:T(8,128)(2,1)S(1)}, bf16[8,2,152,256]{3,2,1,0:T(8,128)(2,1)S(1)}) custom-call(s32[1]{0:T(128)} %bitcast.2.core_ref, bf16[8,152,384]{2,1,0:T(8,128)(2,1)S(1)} %copy-done.2, bf16[8,152,384]{2,1,0:T(8,128)(2,1)S(1)} %collective-permute-done.other_ref, bf16[8,8,48,384]{3,2,1,0:T(8,128)(2,1)S(1)} %bitcast.6, ...), custom_call_target="tpu_custom_call" | custom-call | tf_op jit(solution)/shard_map/pallas_call | solution.py:327
  78.8 0.0 copy-start.13
  78.8 0.0 copy-start.3
  78.8 0.0 copy-start.12
  78.8 22.8 %all_to_all.26.pair_ref = bf16[8,2,152,256]{3,2,1,0:T(8,128)(2,1)S(1)} all-to-all(bf16[8,2,152,256]{3,2,1,0:T(8,128)(2,1)S(1)} %get-tuple-element.6), channel_id=1, replica_groups=mesh['seq_0'=4,'seq_1a'=4,'seq_1b'=2,'seq_2'=2,'tp'=8] {'seq_0','seq_1b'}, dimensions={0} | all-to-all | bytes 2490368 | tf_op jit(solution)/shard_map/all_to_all | solution.py:40
  101.6 0.0 copy-done.13
  101.6 2.2 %shard_map.126 = bf16[8,40,128]{2,1,0:T(8,128)(2,1)S(1)} custom-call(s32[4]{0:T(128)S(1)} %copy-done.13, s32[3]{0:T(128)S(1)} %pad_add_fusion.place_ref, bf16[2,128,128]{2,1,0:T(8,128)(2,1)S(1)} %get-tuple-element.5.query_ref, bf16[8,2,152,256]{3,2,1,0:T(8,128)(2,1)S(1)} %all_to_all.26.pair_ref), custom_call_target="tpu_custom_call" | custom-call | tf_op jit(solution)/shard_map/pallas_call | solution.py:334
  103.8 11.4 %all_to_all.27.att_ref = bf16[8,40,128]{2,1,0:T(8,128)(2,1)S(1)} all-to-all(bf16[8,40,128]{2,1,0:T(8,128)(2,1)S(1)} %shard_map.126), channel_id=1, replica_groups=mesh['seq_0'=4,'seq_1a'=4,'seq_1b'=2,'seq_2'=2,'tp'=8] {'seq_1a','seq_2'}, dimensions={0} | all-to-all | bytes 163840 | tf_op jit(solution)/shard_map/all_to_all | solution.py:40
  115.2 0.0 copy-done.3
  115.3 0.0 copy-done.12
  115.3 0.0 copy-start.5
  115.3 0.0 copy-start.6
  115.3 0.9 shard_map.127
  116.2 22.2 %all_to_all.28.part_ref = bf16[8,104,384]{2,1,0:T(8,128)(2,1)S(1)} all-to-all(bf16[8,104,384]{2,1,0:T(8,128)(2,1)S(1)} %shard_map.127), channel_id=1, replica_groups=mesh['seq_0'=4,'seq_1a'=4,'seq_1b'=2,'seq_2'=2,'tp'=8] {'tp'}, dimensions={0} | all-to-all | bytes 1277952 | tf_op jit(solution)/shard_map/all_to_all | solution.py:40
  138.4 0.0 copy-done.5
  138.4 0.0 copy-done.6
  138.4 1.6 %shard_map.128 = (f32[4,32,384]{2,1,0:T(8,128)}, f32[4,32,384]{2,1,0:T(8,128)}, f32[4]{0:T(128)}) custom-call(s32[4]{0:T(128)S(1)} %copy-done.12, bf16[8,104,384]{2,1,0:T(8,128)(2,1)S(1)} %all_to_all.28.part_ref, f32[4,32,384]{2,1,0:T(8,128)S(1)} %copy-done.6, bf16[4,32,384]{2,1,0:T(8,128)(2,1)S(1)} %copy-done.5, bf16[3,4,384]{2,1,0:T(4,128)(2,1)S(1)} %copy-done.9), custom_call_target="tpu_custom_call" | custom-call | tf_op jit(solution)/shard_map/pallas_call | solution.py:352
  (1 shorter events, 0.0 us)
Async XLA Ops:
  0.6 0.9 copy-start.4
  1.5 0.9 copy-start.7
  2.4 0.9 copy-start.8
  3.3 0.7 copy-start.10
  30.2 1.4 %copy-start = (bf16[8,384,384]{2,1,0:T(8,128)(2,1)}, bf16[8,384,384]{2,1,0:T(8,128)(2,1)S(1)}, u32[]{:S(2)}) copy-start(bf16[8,384,384]{2,1,0:T(8,128)(2,1)S(1)} %shard_map.124) | copy-start | bytes 7077892
  31.6 4.8 %copy-start.9 = (bf16[3,4,384]{2,1,0:T(4,128)(2,1)S(1)}, bf16[3,4,384]{2,1,0:T(4,128)(2,1)}, u32[]{:S(2)}) copy-start(bf16[3,4,384]{2,1,0:T(4,128)(2,1)} %mod_ref.3) | copy-start | bytes 27652
  31.6 44.4 %all-to-all-start.1 = ((bf16[8,384,384]{2,1,0:T(8,128)(2,1)}), bf16[8,384,384]{2,1,0:T(8,128)(2,1)S(1)}, u32[]{:S(2)}, u32[]{:S(2)}) async-start(bf16[8,384,384]{2,1,0:T(8,128)(2,1)} %copy-done), calls=%async_computation.1 | async-start | bytes 4718592 | tf_op jit(solution)/shard_map/all_to_all | solution.py:40
  36.4 39.6 %copy-start.11 = (f32[2,256]{1,0:T(2,128)S(1)}, f32[2,256]{1,0:T(2,128)}, u32[]{:S(2)}) copy-start(f32[2,256]{1,0:T(2,128)} %gain_ref.1) | copy-start | bytes 6148
  66.9 9.1 %collective-permute-start = (bf16[8,152,384]{2,1,0:T(8,128)(2,1)S(1)}, bf16[8,152,384]{2,1,0:T(8,128)(2,1)S(1)}, u32[]{:S(2)}, u32[]{:S(2)}) collective-permute-start(bf16[8,152,384]{2,1,0:T(8,128)(2,1)S(1)} %shard_map.123.own_ref), channel_id=1, source_target_pairs={{0,8},{8,0},{1,9},{9,1},{2,10},{10,2},{3,11},{11,3},{4,12},{12,4},... | collective-permute-start | bytes 2801672 | tf_op jit(solution)/shard_map/ppermute | solution.py:325
  73.9 0.9 copy-start.1
  76.0 1.2 copy-start.2
  78.8 22.8 %copy-start.13 = (s32[4]{0:T(128)S(1)}, s32[4]{0:T(128)}, u32[]{:S(2)}) copy-start(s32[4]{0:T(128)} %limit_ref.1) | copy-start | bytes 52
  78.8 36.5 %copy-start.3 = (bf16[256,3072]{1,0:T(8,128)(2,1)S(1)}, bf16[256,3072]{1,0:T(8,128)(2,1)}, u32[]{:S(2)}) copy-start(bf16[256,3072]{1,0:T(8,128)(2,1)} %w_ref.1) | copy-start | bytes 4718596
  78.8 36.5 %copy-start.12 = (s32[4]{0:T(128)S(1)}, s32[4]{0:T(128)}, u32[]{:S(2)}) copy-start(s32[4]{0:T(128)} %flag_ref.3) | copy-start | bytes 52
  115.3 23.2 %copy-start.5 = (bf16[4,32,384]{2,1,0:T(8,128)(2,1)S(1)}, bf16[4,32,384]{2,1,0:T(8,128)(2,1)}, u32[]{:S(2)}) copy-start(bf16[4,32,384]{2,1,0:T(8,128)(2,1)} %img_ref.3) | copy-start | bytes 294916
  115.3 23.2 %copy-start.6 = (f32[4,32,384]{2,1,0:T(8,128)S(1)}, f32[4,32,384]{2,1,0:T(8,128)}, u32[]{:S(2)}) copy-start(f32[4,32,384]{2,1,0:T(8,128)} %cache_ref.1) | copy-start | bytes 589828

commit v7 on v6

--- a/solution.py
+++ b/solution.py
@@ -19,15 +19,17 @@
 
 VMEM = pl.BlockSpec(memory_space=pltpu.VMEM)
 SMEM = pl.BlockSpec(memory_space=pltpu.SMEM)
-
-
-def call(body, out_shape, in_specs, mebibytes, outs=None):
+HBM = pl.BlockSpec(memory_space=pltpu.HBM)
+
+
+def call(body, out_shape, in_specs, mebibytes, outs=None, scratch=()):
     outs = outs or jax.tree.map(lambda _: VMEM, out_shape)
     return pl.pallas_call(
         body,
         out_shape=out_shape,
         in_specs=in_specs,
         out_specs=outs,
+        scratch_shapes=scratch,
         compiler_params=pltpu.CompilerParams(vmem_limit_bytes=mebibytes << 20),
     )
 
@@ -53,7 +55,17 @@
     return jnp.where(row == 0, high, jnp.where(row == 1, middle, jnp.where(row == 2, low, 0.0)))
 
 
-def pack_body(w_ref, img_ref, prev_ref, txt_ref, out_ref):
+def pack_body(w_hbm, img_hbm, prev_hbm, txt_hbm, out_ref, w_ref, img_ref, prev_ref, txt_ref, sems):
+    copies = [
+        pltpu.make_async_copy(source, target, sems.at[i])
+        for i, (source, target) in enumerate(
+            ((w_hbm, w_ref), (img_hbm, img_ref), (prev_hbm, prev_ref), (txt_hbm, txt_ref))
+        )
+    ]
+    for copy in copies:
+        copy.start()
+    for copy in copies:
+        copy.wait()
     kinds, deep, columns = w_ref.shape
     batch, img_rows, width = img_ref.shape
     cores = columns // HD
@@ -75,21 +87,34 @@
             out_ref[to, at : at + 8] = text.astype(BF16)
 
 
-def spread_body(got_ref, out_ref):
-    copies = out_ref.shape[0]
+def spread_body(got_ref, out_hbm, sems):
+    copies = []
     sources = got_ref.shape[0]
-    deep = out_ref.shape[1] // sources
-    for copy in range(copies):
+    deep = out_hbm.shape[1] // sources
+    for copy in range(out_hbm.shape[0]):
         for source in range(sources):
-            out_ref[copy, source * deep : (source + 1) * deep] = got_ref[source, :deep]
-
-
-def join_body(deep, img_half, txt_half, far_ref, got_ref, mod_ref, out_ref):
+            copies.append(
+                pltpu.make_async_copy(
+                    got_ref.at[source, pl.ds(0, deep)],
+                    out_hbm.at[copy, pl.ds(source * deep, deep)],
+                    sems.at[copy, source],
+                )
+            )
+    for copy in copies:
+        copy.start()
+    for copy in copies:
+        copy.wait()
+
+
+def join_body(deep, img_half, txt_half, far_ref, got_ref, mod_ref, out_ref, prev_ref):
     sources = got_ref.shape[0]
     width = got_ref.shape[2]
     for source in range(sources):
         out_ref[source * img_half : (source + 1) * img_half] = got_ref[
             source, deep : deep + img_half
+        ]
+        prev_ref[source * img_half : (source + 1) * img_half] = got_ref[
+            source, deep + img_half : deep + 2 * img_half
         ]
     at = deep + 2 * img_half
     texts = [got_ref[source, at : at + 8].astype(F32)[:txt_half] for source in range(sources)]
@@ -103,9 +128,8 @@
     out_ref[sources * img_half :] = tail.astype(BF16)
 
 
-def norm_body(deep, place_ref, x_ref, got_ref, mod_ref):
+def norm_body(place_ref, x_ref, prev_ref, mod_ref):
     groups, rows, width = x_ref.shape
-    sources = got_ref.shape[0]
     vectors = rows - 8
     features = groups * width
     sums = jnp.zeros((rows, 1), F32)
@@ -125,15 +149,9 @@
         mod_ref[g] = ((values - center) * inv * (1.0 + scale) + shift).astype(BF16)
     far = place_ref[0]
     own = mod_ref.at[place_ref[1]]
-    img_half = (got_ref.shape[1] - deep - 8) // 2
-    numer = jnp.zeros((img_half, width), F32)
-    denom = jnp.zeros((img_half, width), F32)
-    for source in range(sources):
-        at = deep + img_half
-        previous = got_ref[source, at : at + img_half].astype(F32)
-        current = own[source * img_half : (source + 1) * img_half].astype(F32)
-        numer = numer + jnp.abs(current - previous)
-        denom = denom + jnp.abs(previous)
+    previous = prev_ref[...].astype(F32)
+    numer = jnp.abs(own[: prev_ref.shape[0]].astype(F32) - previous)
+    denom = jnp.abs(previous)
     lane = lax.broadcasted_iota(jnp.int32, (1, width), 1)
     line = jnp.where(lane == far, jnp.sum(numer), 0.0)
     line = jnp.where(lane == 4 + far, jnp.sum(denom), line)
@@ -305,23 +323,34 @@
     core_index = lax.axis_index(CORE).astype(jnp.int32)[None]
     far_index = lax.axis_index(FAR).astype(jnp.int32)[None]
 
+    arrays = (w_qkv.transpose(1, 0, 2), img, prev_mod, txt)
     got = call(
-        pack_body, shaped(sources, deep + 2 * img_half + 8, width), [VMEM] * 4, 8
-    )(w_qkv.transpose(1, 0, 2), img, prev_mod, txt)
+        pack_body,
+        shaped(sources, deep + 2 * img_half + 8, width),
+        [HBM] * 4,
+        8,
+        scratch=[pltpu.VMEM(a.shape, a.dtype) for a in arrays]
+        + [pltpu.SemaphoreType.DMA((len(arrays),))],
+    )(*(pltpu.with_memory_space_constraint(a, pltpu.HBM) for a in arrays))
     got = swap(got, (FAR, CORE))
-    weight = call(spread_body, shaped(around, sources * deep, kinds * HD), [VMEM], 8)(got)
+    weight = call(
+        spread_body,
+        pltpu.HBM((around, sources * deep, kinds * HD), BF16),
+        [VMEM],
+        8,
+        outs=HBM,
+        scratch=[pltpu.SemaphoreType.DMA((around, sources))],
+    )(got)
     weight = swap(weight, (X, NEAR)).reshape(around, sources, deep, kinds * HD)
 
-    joined = call(
+    joined, previous = call(
         functools.partial(join_body, deep, img_half, txt_half),
-        shaped(rows, width),
+        (shaped(rows, width), shaped(sources * img_half, width)),
         [SMEM, VMEM, VMEM],
         8,
     )(far_index, got, modulation)
     wide = lax.all_gather(joined, TP, axis=0, tiled=False)
-    own = call(
-        functools.partial(norm_body, deep), shaped(tps, rows, width), [SMEM, VMEM, VMEM], 12
-    )(place, wide, got)
+    own = call(norm_body, shaped(tps, rows, width), [SMEM, VMEM, VMEM], 12)(place, wide, previous)
     other = lax.ppermute(own, CORE, [(0, 1), (1, 0)])
 
     query, pairs = call(

time: 141 us -> 139 us (0.986)
  local copies, waits for them, and re-layouts: 6.96 us -> 2.17 us
  Pallas kernels: 8.36 us -> 11.2 us
    unnamed x28 -> x18, local copies, waits for them, and re-layouts: 6.96 us -> 2.17 us
    pallas_call x4, Pallas kernels: 2.04 us -> 4.88 us  [the longest x1 1.99 us: local(): call(spread_body, pltpu.HBM((around, sources * deep, kinds * HD), BF16),...]
where the time goes in v7:
time: 139 us
  blocking collectives  111 us (80%)
  starting transfers between devices  11.6 us (8%)
  Pallas kernels  11.2 us (8%)
  local copies, waits for them, and re-layouts  2.17 us (2%)
  waiting for transfers between devices  2.1 us (2%)
    all_to_all x4, blocking collectives, swap(): return lax.all_to_all(value, axis, 0, 0, tiled=True)  82.4 us
    all_gather x1, blocking collectives, local(): wide = lax.all_gather(joined, TP, axis=0, tiled=False)  28.7 us
    ppermute x1, starting transfers between devices, local(): other = lax.ppermute(own, CORE, [(0, 1), (1, 0)])  7.01 us
    all_to_all x1, starting transfers between devices, swap(): return lax.all_to_all(value, axis, 0, 0, tiled=True)  4.57 us
  transfers between devices with their start and end apart: 2, of which 1 were waited for; matrix products, arithmetic and copies ran while one was open for 0% of the time, Pallas kernels for 1%

profile of v7, /device:TPU:1, one launch (start us, length us, event | category | flops | bytes accessed | tf_op | source)
XLA Modules:
  0.0 139.0 jit_solution(318459919822582753)
XLA Ops:
  0.6 1.1 shard_map.121
  1.7 25.9 %all_to_all.25.got_ref = bf16[8,88,384]{2,1,0:T(8,128)(2,1)S(1)} all-to-all(bf16[8,88,384]{2,1,0:T(8,128)(2,1)S(1)} %shard_map.121), channel_id=1, replica_groups=mesh['seq_0'=4,'seq_1a'=4,'seq_1b'=2,'seq_2'=2,'tp'=8] {'seq_1a','seq_2'}, dimensions={0} | all-to-all | bytes 1081344 | tf_op jit(solution)/shard_map/all_to_all | solution.py:42
  27.6 2.0 %shard_map.124 = bf16[8,384,384]{2,1,0:T(8,128)(2,1)} custom-call(bf16[8,88,384]{2,1,0:T(8,128)(2,1)S(1)} %all_to_all.25.got_ref), custom_call_target="tpu_custom_call" | custom-call | tf_op jit(solution)/shard_map/pallas_call | solution.py:336
  29.6 0.0 copy-start.5
  29.6 4.6 %all-to-all-start.1 = ((bf16[8,384,384]{2,1,0:T(8,128)(2,1)}), bf16[8,384,384]{2,1,0:T(8,128)(2,1)S(1)}, u32[]{:S(2)}, u32[]{:S(2)}) async-start(bf16[8,384,384]{2,1,0:T(8,128)(2,1)} %shard_map.124), calls=%async_computation.1 | async-start | bytes 4718592 | tf_op jit(solution)/shard_map/all_to_all | solution.py:42
  34.2 0.1 pad_add_fusion.place_ref
  34.3 0.0 copy-done.5
  34.3 0.0 copy-start.6
  34.3 28.7 %all-gather = bf16[1216,384]{1,0:T(8,128)(2,1)S(1)} all-gather(bf16[152,384]{1,0:T(8,128)(2,1)S(1)} %get-tuple-element.7), channel_id=2, replica_groups=mesh['seq_0'=4,'seq_1a'=4,'seq_1b'=2,'seq_2'=2,'tp'=8] {'tp'}, dimensions={0}, use_global_device_ids=true | all-gather | bytes 1050624 | tf_op jit(solution)/shard_map/all_gather | solution.py:352
  63.0 1.8 %shard_map.123.own_ref = bf16[8,152,384]{2,1,0:T(8,128)(2,1)S(1)} custom-call(s32[3]{0:T(128)S(1)} %pad_add_fusion.place_ref, bf16[8,152,384]{2,1,0:T(8,128)(2,1)S(1)} %bitcast.7, bf16[128,384]{1,0:T(8,128)(2,1)S(1)} %get-tuple-element.8.prev_ref), custom_call_target="tpu_custom_call" | custom-call | tf_op jit(solution)/shard_map/pallas_call | solution.py:353
  64.8 7.0 %collective-permute-start = (bf16[8,152,384]{2,1,0:T(8,128)(2,1)S(1)}, bf16[8,152,384]{2,1,0:T(8,128)(2,1)S(1)}, u32[]{:S(2)}, u32[]{:S(2)}) collective-permute-start(bf16[8,152,384]{2,1,0:T(8,128)(2,1)S(1)} %shard_map.123.own_ref), channel_id=1, source_target_pairs={{0,8},{8,0},{1,9},{9,1},{2,10},{10,2},{3,11},{11,3},{4,12},{12,4},... | collective-permute-start | bytes 2801672 | tf_op jit(solution)/shard_map/ppermute | solution.py:354
  71.8 2.1 %collective-permute-done.other_ref = bf16[8,152,384]{2,1,0:T(8,128)(2,1)S(1)} collective-permute-done((bf16[8,152,384]{2,1,0:T(8,128)(2,1)S(1)}, bf16[8,152,384]{2,1,0:T(8,128)(2,1)S(1)}, u32[]{:S(2)}, u32[]{:S(2)}) %collective-permute-start) | collective-permute-done | bytes 933920 | tf_op jit(solution)/shard_map/ppermute | solution.py:354
  73.9 0.0 copy-start.1
  73.9 0.9 copy-done.1
  74.9 0.0 all-to-all-done.1
  74.9 0.0 copy-done.6
  74.9 0.0 copy-start.2
  74.9 1.2 copy-done.2
  76.1 1.5 %shard_map.125 = (bf16[2,128,128]{2,1,0:T(8,128)(2,1)S(1)}, bf16[8,2,152,256]{3,2,1,0:T(8,128)(2,1)S(1)}) custom-call(s32[1]{0:T(128)} %bitcast.2.core_ref, bf16[8,152,384]{2,1,0:T(8,128)(2,1)S(1)} %shard_map.123.own_ref, bf16[8,152,384]{2,1,0:T(8,128)(2,1)S(1)} %copy-done.2, bf16[8,8,48,384]{3,2,1,0:T(8,128)(2,1)S(1)} %bitcast.6, f32[2,256]{1,0:T(2,128)S(1)} %copy-done.6), custom_call_target="tpu_custom_call" | custom-call | tf_op jit(solution)/shard_map/pallas_call | solution.py:356
  77.6 0.0 copy-start.8
  77.6 0.0 copy-start
  77.7 0.0 copy-start.7
  77.7 22.8 %all_to_all.26.pair_ref = bf16[8,2,152,256]{3,2,1,0:T(8,128)(2,1)S(1)} all-to-all(bf16[8,2,152,256]{3,2,1,0:T(8,128)(2,1)S(1)} %get-tuple-element.10), channel_id=1, replica_groups=mesh['seq_0'=4,'seq_1a'=4,'seq_1b'=2,'seq_2'=2,'tp'=8] {'seq_0','seq_1b'}, dimensions={0} | all-to-all | bytes 2490368 | tf_op jit(solution)/shard_map/all_to_all | solution.py:42
  100.5 0.0 copy-done.8
  100.5 2.3 %shard_map.126 = bf16[8,40,128]{2,1,0:T(8,128)(2,1)S(1)} custom-call(s32[4]{0:T(128)S(1)} %copy-done.8, s32[3]{0:T(128)S(1)} %pad_add_fusion.place_ref, bf16[2,128,128]{2,1,0:T(8,128)(2,1)S(1)} %get-tuple-element.9.query_ref, bf16[8,2,152,256]{3,2,1,0:T(8,128)(2,1)S(1)} %all_to_all.26.pair_ref), custom_call_target="tpu_custom_call" | custom-call | tf_op jit(solution)/shard_map/pallas_call | solution.py:363
  102.7 11.4 %all_to_all.27.att_ref = bf16[8,40,128]{2,1,0:T(8,128)(2,1)S(1)} all-to-all(bf16[8,40,128]{2,1,0:T(8,128)(2,1)S(1)} %shard_map.126), channel_id=1, replica_groups=mesh['seq_0'=4,'seq_1a'=4,'seq_1b'=2,'seq_2'=2,'tp'=8] {'seq_1a','seq_2'}, dimensions={0} | all-to-all | bytes 163840 | tf_op jit(solution)/shard_map/all_to_all | solution.py:42
  114.1 0.0 copy-done
  114.1 0.0 copy-done.7
  114.2 0.0 copy-start.3
  114.2 0.0 copy-start.4
  114.2 0.9 shard_map.127
  115.1 22.3 %all_to_all.28.part_ref = bf16[8,104,384]{2,1,0:T(8,128)(2,1)S(1)} all-to-all(bf16[8,104,384]{2,1,0:T(8,128)(2,1)S(1)} %shard_map.127), channel_id=1, replica_groups=mesh['seq_0'=4,'seq_1a'=4,'seq_1b'=2,'seq_2'=2,'tp'=8] {'tp'}, dimensions={0} | all-to-all | bytes 1277952 | tf_op jit(solution)/shard_map/all_to_all | solution.py:42
  137.4 0.0 copy-done.3
  137.4 0.0 copy-done.4
  137.4 1.6 %shard_map.128 = (f32[4,32,384]{2,1,0:T(8,128)}, f32[4,32,384]{2,1,0:T(8,128)}, f32[4]{0:T(128)}) custom-call(s32[4]{0:T(128)S(1)} %copy-done.7, bf16[8,104,384]{2,1,0:T(8,128)(2,1)S(1)} %all_to_all.28.part_ref, f32[4,32,384]{2,1,0:T(8,128)S(1)} %copy-done.4, bf16[4,32,384]{2,1,0:T(8,128)(2,1)S(1)} %copy-done.3, bf16[3,4,384]{2,1,0:T(4,128)(2,1)S(1)} %copy-done.5), custom_call_target="tpu_custom_call" | custom-call | tf_op jit(solution)/shard_map/pallas_call | solution.py:381
  (1 shorter events, 0.0 us)
Async XLA Ops:
  29.6 4.7 %copy-start.5 = (bf16[3,4,384]{2,1,0:T(4,128)(2,1)S(1)}, bf16[3,4,384]{2,1,0:T(4,128)(2,1)}, u32[]{:S(2)}) copy-start(bf16[3,4,384]{2,1,0:T(4,128)(2,1)} %mod_ref.3) | copy-start | bytes 27652
  29.6 45.3 %all-to-all-start.1 = ((bf16[8,384,384]{2,1,0:T(8,128)(2,1)}), bf16[8,384,384]{2,1,0:T(8,128)(2,1)S(1)}, u32[]{:S(2)}, u32[]{:S(2)}) async-start(bf16[8,384,384]{2,1,0:T(8,128)(2,1)} %shard_map.124), calls=%async_computation.1 | async-start | bytes 4718592 | tf_op jit(solution)/shard_map/all_to_all | solution.py:42
  34.3 40.6 %copy-start.6 = (f32[2,256]{1,0:T(2,128)S(1)}, f32[2,256]{1,0:T(2,128)}, u32[]{:S(2)}) copy-start(f32[2,256]{1,0:T(2,128)} %gain_ref.1) | copy-start | bytes 6148
  64.8 9.1 %collective-permute-start = (bf16[8,152,384]{2,1,0:T(8,128)(2,1)S(1)}, bf16[8,152,384]{2,1,0:T(8,128)(2,1)S(1)}, u32[]{:S(2)}, u32[]{:S(2)}) collective-permute-start(bf16[8,152,384]{2,1,0:T(8,128)(2,1)S(1)} %shard_map.123.own_ref), channel_id=1, source_target_pairs={{0,8},{8,0},{1,9},{9,1},{2,10},{10,2},{3,11},{11,3},{4,12},{12,4},... | collective-permute-start | bytes 2801672 | tf_op jit(solution)/shard_map/ppermute | solution.py:354
  73.9 0.9 copy-start.1
  74.9 1.2 copy-start.2
  77.6 22.9 %copy-start.8 = (s32[4]{0:T(128)S(1)}, s32[4]{0:T(128)}, u32[]{:S(2)}) copy-start(s32[4]{0:T(128)} %limit_ref.1) | copy-start | bytes 52
  77.6 36.5 %copy-start = (bf16[256,3072]{1,0:T(8,128)(2,1)S(1)}, bf16[256,3072]{1,0:T(8,128)(2,1)}, u32[]{:S(2)}) copy-start(bf16[256,3072]{1,0:T(8,128)(2,1)} %w_ref.1) | copy-start | bytes 4718596
  77.7 36.5 %copy-start.7 = (s32[4]{0:T(128)S(1)}, s32[4]{0:T(128)}, u32[]{:S(2)}) copy-start(s32[4]{0:T(128)} %flag_ref.3) | copy-start | bytes 52
  114.2 23.2 %copy-start.3 = (bf16[4,32,384]{2,1,0:T(8,128)(2,1)S(1)}, bf16[4,32,384]{2,1,0:T(8,128)(2,1)}, u32[]{:S(2)}) copy-start(bf16[4,32,384]{2,1,0:T(8,128)(2,1)} %img_ref.1) | copy-start | bytes 294916
  114.2 23.2 %copy-start.4 = (f32[4,32,384]{2,1,0:T(8,128)S(1)}, f32[4,32,384]{2,1,0:T(8,128)}, u32[]{:S(2)}) copy-start(f32[4,32,384]{2,1,0:T(8,128)} %cache_ref.1) | copy-start | bytes 589828

commit v8 on v7

--- a/solution.py
+++ b/solution.py
@@ -55,7 +55,9 @@
     return jnp.where(row == 0, high, jnp.where(row == 1, middle, jnp.where(row == 2, low, 0.0)))
 
 
-def pack_body(w_hbm, img_hbm, prev_hbm, txt_hbm, out_ref, w_ref, img_ref, prev_ref, txt_ref, sems):
+def pack_body(
+    w_hbm, img_hbm, prev_hbm, txt_hbm, out_hbm, w_ref, img_ref, prev_ref, txt_ref, out_ref, sems
+):
     copies = [
         pltpu.make_async_copy(source, target, sems.at[i])
         for i, (source, target) in enumerate(
@@ -85,21 +87,34 @@
             text = txt_ref[b].astype(F32)[c * txt_half : (c + 1) * txt_half]
             text = jnp.concatenate([text, jnp.zeros((8 - txt_half, width), F32)], axis=0)
             out_ref[to, at : at + 8] = text.astype(BF16)
-
-
-def spread_body(got_ref, out_hbm, sems):
+    whole = pltpu.make_async_copy(out_ref, out_hbm, sems.at[0])
+    whole.start()
+    whole.wait()
+
+
+def spread_body(got_ref, out_hbm, block_ref, sems):
+    sources = got_ref.shape[0]
+    deep = block_ref.shape[0] // sources
+    for source in range(sources):
+        block_ref[source * deep : (source + 1) * deep] = got_ref[source, :deep]
+    copies = [
+        pltpu.make_async_copy(block_ref, out_hbm.at[copy], sems.at[copy])
+        for copy in range(out_hbm.shape[0])
+    ]
+    for copy in copies:
+        copy.start()
+    for copy in copies:
+        copy.wait()
+
+
+def deal_body(tp_ref, w_hbm, *refs):
+    *out_refs, sems = refs
+    width = out_refs[0].shape[1]
     copies = []
-    sources = got_ref.shape[0]
-    deep = out_hbm.shape[1] // sources
-    for copy in range(out_hbm.shape[0]):
-        for source in range(sources):
-            copies.append(
-                pltpu.make_async_copy(
-                    got_ref.at[source, pl.ds(0, deep)],
-                    out_hbm.at[copy, pl.ds(source * deep, deep)],
-                    sems.at[copy, source],
-                )
-            )
+    for k, out_ref in enumerate(out_refs):
+        target = lax.rem(tp_ref[0] + k, len(out_refs))
+        columns = pl.ds(pl.multiple_of(target * width, HD), width)
+        copies.append(pltpu.make_async_copy(w_hbm.at[:, columns], out_ref, sems.at[k]))
     for copy in copies:
         copy.start()
     for copy in copies:
@@ -158,7 +173,9 @@
     mod_ref[0, vectors:] = stacked_parts(line, 8).astype(BF16)
 
 
-def project_body(core_ref, own_ref, other_ref, w_ref, gain_ref, query_ref, pair_ref):
+def project_body(
+    core_ref, own_ref, other_ref, w_ref, gain_ref, query_ref, pair_hbm, pair_ref, sems
+):
     groups, rows, width = own_ref.shape
     _, sources, deep, columns = w_ref.shape
     near = cores = 2
@@ -193,10 +210,17 @@
         query_ref[half] = query[at : at + img].astype(BF16)
         carried = ref[0, rows - 8 :, :HD]
         keys = keyed[at : at + rows - 8].astype(BF16)
-        for copy in range(pair_ref.shape[0]):
-            pair_ref[copy, half, : rows - 8, :HD] = keys
-            pair_ref[copy, half, rows - 8 :, :HD] = carried
-            pair_ref[copy, half, :, HD:] = valued[at : at + rows]
+        pair_ref[half, : rows - 8, :HD] = keys
+        pair_ref[half, rows - 8 :, :HD] = carried
+        pair_ref[half, :, HD:] = valued[at : at + rows]
+    copies = [
+        pltpu.make_async_copy(pair_ref, pair_hbm.at[copy], sems.at[copy])
+        for copy in range(pair_hbm.shape[0])
+    ]
+    for copy in copies:
+        copy.start()
+    for copy in copies:
+        copy.wait()
 
 
 def attend_body(img_half, txt_half, limit_ref, place_ref, query_ref, pair_ref, out_ref):
@@ -245,64 +269,38 @@
         at = pl.multiple_of(actual * img_half, img_half)
         for source in range(sources):
             start = half * img + source * img_half
-            out_ref[source, pl.ds(at, img_half)] = attended[start : start + img_half]
+            for z in range(out_ref.shape[1]):
+                out_ref[source, z, pl.ds(at, img_half)] = attended[start : start + img_half]
     for source in range(sources):
-        out_ref[source, 2 * img_half :] = tail
-
-
-def slots_of(flag_ref, batch, count):
-    order = [jnp.int32(0)] * count
-    seen = jnp.int32(0)
-    slot = []
-    for b in range(batch):
-        on = flag_ref[b] == 1
-        slot.append(seen)
-        for i in range(count):
-            order[i] = jnp.where(on & (seen == i), jnp.int32(b), order[i])
-        seen = seen + jnp.where(on, 1, 0)
-    return order, slot
-
-
-def mix_body(img_rows, flag_ref, att_ref, w_ref, out_ref):
-    groups, rows, width = out_ref.shape
-    heads = w_ref.shape[0] // HD
-    batch = att_ref.shape[0] // heads
-    slots = (rows - 8) // img_rows
-    order, _ = slots_of(flag_ref, batch, slots)
-    lefts = []
-    for h in range(heads):
-        lefts.append(
-            jnp.concatenate([att_ref[order[i] * heads + h, :img_rows] for i in range(slots)], axis=0)
+        for z in range(out_ref.shape[1]):
+            out_ref[source, z, 2 * img_half :] = tail
+
+
+def final_body(tp_ref, flag_ref, att_ref, *refs):
+    *w_refs, cache_ref, img_ref, mod_ref, out_ref, new_ref, rel_ref = refs
+    groups = len(w_refs)
+    batch, img_rows, width = img_ref.shape
+    heads = att_ref.shape[0] // batch
+    mixed = jnp.zeros((batch * img_rows, width), F32)
+    rel = jnp.zeros((8, HD), F32)
+    for k, w_ref in enumerate(w_refs):
+        source = lax.rem(tp_ref[0] + groups - k, groups)
+        lefts = []
+        for h in range(heads):
+            blocks = [att_ref[b * heads + h, source, :img_rows] for b in range(batch)]
+            lefts.append(jnp.concatenate(blocks, axis=0))
+        mixed = mixed + jnp.dot(
+            jnp.concatenate(lefts, axis=1), w_ref[...], preferred_element_type=F32
         )
-    left = jnp.concatenate(lefts, axis=1)
-    rel = jnp.zeros((8, HD), F32)
-    for b in range(batch):
-        rel = rel + att_ref[b * heads, img_rows:].astype(F32)
-    tail = stacked_parts(jnp.sum(rel, axis=0, keepdims=True), 8)
-    tail = jnp.concatenate([tail, jnp.zeros((8, width - HD), F32)], axis=1).astype(BF16)
-    for g in range(groups):
-        mixed = jnp.dot(left, w_ref[:, g * width : (g + 1) * width], preferred_element_type=F32)
-        out_ref[g, : rows - 8] = mixed.astype(BF16)
-        out_ref[g, rows - 8 :] = tail
-
-
-def final_body(flag_ref, part_ref, cache_ref, img_ref, mod_ref, out_ref, new_ref, rel_ref, sum_ref):
-    groups, rows, _ = part_ref.shape
-    batch, img_rows, _ = img_ref.shape
-    slots = (rows - 8) // img_rows
-    mixed = part_ref[0].astype(F32)
-    for g in range(1, groups):
-        mixed = mixed + part_ref[g].astype(F32)
-    sum_ref[...] = mixed
-    _, slot = slots_of(flag_ref, batch, slots)
+        for b in range(batch):
+            rel = rel + att_ref[b * heads, k, img_rows:].astype(F32)
     for b in range(batch):
         gate = mod_ref[2, b : b + 1].astype(F32)
-        at = pl.multiple_of(jnp.minimum(slot[b], slots - 1) * img_rows, img_rows)
-        resid = gate * sum_ref[pl.ds(at, img_rows)]
+        resid = gate * mixed[b * img_rows : (b + 1) * img_rows]
         fresh = jnp.where(flag_ref[b] == 1, resid, cache_ref[b])
         new_ref[b] = fresh
         out_ref[b] = img_ref[b].astype(F32) + fresh
-    sums = jnp.sum(mixed[rows - 8 :, :HD], axis=0, keepdims=True)
+    sums = jnp.sum(rel, axis=0, keepdims=True)
     lane = lax.broadcasted_iota(jnp.int32, (1, HD), 1)
     for b in range(batch):
         numer = jnp.sum(jnp.where(lane == b, sums, 0.0))
@@ -324,14 +322,28 @@
     far_index = lax.axis_index(FAR).astype(jnp.int32)[None]
 
     arrays = (w_qkv.transpose(1, 0, 2), img, prev_mod, txt)
+    packed = (sources, deep + 2 * img_half + 8, width)
     got = call(
         pack_body,
-        shaped(sources, deep + 2 * img_half + 8, width),
+        pltpu.HBM(packed, BF16),
         [HBM] * 4,
         8,
+        outs=HBM,
         scratch=[pltpu.VMEM(a.shape, a.dtype) for a in arrays]
-        + [pltpu.SemaphoreType.DMA((len(arrays),))],
+        + [pltpu.VMEM(packed, BF16), pltpu.SemaphoreType.DMA((len(arrays),))],
     )(*(pltpu.with_memory_space_constraint(a, pltpu.HBM) for a in arrays))
+    blocks = list(
+        call(
+            deal_body,
+            (pltpu.HBM((output_weight.shape[0], width), BF16),) * tps,
+            [SMEM, HBM],
+            4,
+            outs=(HBM,) * tps,
+            scratch=[pltpu.SemaphoreType.DMA((tps,))],
+        )(place[1:2], pltpu.with_memory_space_constraint(output_weight, pltpu.HBM))
+    )
+    for k in range(1, tps):
+        blocks[k] = lax.ppermute(blocks[k], TP, [(i, (i + k) % tps) for i in range(tps)])
     got = swap(got, (FAR, CORE))
     weight = call(
         spread_body,
@@ -339,7 +351,10 @@
         [VMEM],
         8,
         outs=HBM,
-        scratch=[pltpu.SemaphoreType.DMA((around, sources))],
+        scratch=[
+            pltpu.VMEM((sources * deep, kinds * HD), BF16),
+            pltpu.SemaphoreType.DMA((around,)),
+        ],
     )(got)
     weight = swap(weight, (X, NEAR)).reshape(around, sources, deep, kinds * HD)
 
@@ -355,37 +370,33 @@
 
     query, pairs = call(
         project_body,
-        (shaped(2, sources * img_half, HD), shaped(around, 2, rows, 2 * HD)),
+        (shaped(2, sources * img_half, HD), pltpu.HBM((around, 2, rows, 2 * HD), BF16)),
         [SMEM] + [VMEM] * 4,
         16,
+        outs=(VMEM, HBM),
+        scratch=[
+            pltpu.VMEM((2, rows, 2 * HD), BF16),
+            pltpu.SemaphoreType.DMA((around,)),
+        ],
     )(core_index, own, other, weight, qk_gain)
     pairs = swap(pairs, (X, NEAR))
     attended = call(
         functools.partial(attend_body, img_half, txt_half),
-        shaped(sources, img_rows + 8, HD),
+        shaped(sources, tps, img_rows + 8, HD),
         [SMEM, SMEM, VMEM, VMEM],
         24,
     )(text_len, place, query, pairs)
-    attended = swap(attended, (FAR, CORE))
-
-    slots = batch - 1
-    parts = call(
-        functools.partial(mix_body, img_rows),
-        shaped(tps, slots * img_rows + 8, width),
-        [SMEM, VMEM, VMEM],
+    flat = attended.reshape(sources * tps, img_rows + 8, HD)
+    attended = swap(flat, (FAR, CORE, TP)).reshape(attended.shape)
+
+    whole = shaped(batch, img_rows, width, dtype=F32)
+    return call(
+        final_body,
+        (whole, whole, shaped(batch, dtype=F32)),
+        [SMEM, SMEM] + [VMEM] * (tps + 4),
         12,
-    )(refresh, attended, output_weight)
-    parts = swap(parts, TP)
-
-    whole = shaped(batch, img_rows, width, dtype=F32)
-    return pl.pallas_call(
-        final_body,
-        out_shape=(whole, whole, shaped(batch, dtype=F32)),
-        in_specs=[SMEM] + [VMEM] * 4,
-        out_specs=(VMEM, VMEM, SMEM),
-        scratch_shapes=[pltpu.VMEM((slots * img_rows + 8, width), F32)],
-        compiler_params=pltpu.CompilerParams(vmem_limit_bytes=8 << 20),
-    )(refresh, parts, cache, img, modulation)
+        outs=(VMEM, VMEM, SMEM),
+    )(place[1:2], refresh, attended, *blocks, cache, img, modulation)
 
 
 def solution(mesh):

time: 139 us -> 215 us (1.55)
  the two profiles are of different devices: /device:TPU:1 before, /device:TPU:65 now
where the time goes in v8:
time: 215 us; the launch traced here: 214 us
  blocking collectives  75.7 us (35%)
  Pallas kernels  61.7 us (29%)
  starting transfers between devices  45.2 us (21%)
  waiting for transfers between devices  27.8 us (13%)
  local copies, waits for them, and re-layouts  3.08 us (1%)
    pallas_call x1, Pallas kernels, local(): call(deal_body, (pltpu.HBM((output_weight.shape[0], width), BF16),) * tps...  48.8 us
    all_to_all x2, blocking collectives, swap(): return lax.all_to_all(value, axis, 0, 0, tiled=True)  48 us
    all_gather x1, blocking collectives, local(): wide = lax.all_gather(joined, TP, axis=0, tiled=False)  27.7 us
    ppermute x7, starting transfers between devices, local(): lax.ppermute(blocks[k], TP, [(i, (i + k) % tps) for i in range(tps)])  27.1 us
    ppermute x7, waiting for transfers between devices, local(): lax.ppermute(blocks[k], TP, [(i, (i + k) % tps) for i in range(tps)])  25.7 us
    all_to_all x2, starting transfers between devices, swap(): return lax.all_to_all(value, axis, 0, 0, tiled=True)  11.1 us
    ppermute x1, starting transfers between devices, local(): other = lax.ppermute(own, CORE, [(0, 1), (1, 0)])  7.07 us
  transfers between devices with their start and end apart: 10, of which 5 were waited for; matrix products, arithmetic and copies ran while one was open for 0% of the time, Pallas kernels for 24%

profile of v8, /device:TPU:65, one launch (start us, length us, event | category | flops | bytes accessed | tf_op | source)
XLA Modules:
  0.0 214.4 jit_solution(5265974195416386742)
XLA Ops:
  0.6 1.9 shard_map.121
  2.5 25.4 %all_to_all.20.got_ref = bf16[8,88,384]{2,1,0:T(8,128)(2,1)S(1)} all-to-all(bf16[8,88,384]{2,1,0:T(8,128)(2,1)} %shard_map.121), channel_id=1, replica_groups=mesh['seq_0'=4,'seq_1a'=4,'seq_1b'=2,'seq_2'=2,'tp'=8] {'seq_1a','seq_2'}, dimensions={0} | all-to-all | bytes 1081344 | tf_op jit(solution)/shard_map/all_to_all | solution.py:42
  27.9 1.5 shard_map.124
  29.4 0.0 copy-start.5
  29.4 4.5 %all-to-all-start.1 = ((bf16[8,384,384]{2,1,0:T(8,128)(2,1)}), bf16[8,384,384]{2,1,0:T(8,128)(2,1)S(1)}, u32[]{:S(2)}, u32[]{:S(2)}) async-start(bf16[8,384,384]{2,1,0:T(8,128)(2,1)} %shard_map.124), calls=%async_computation.1 | async-start | bytes 4718592 | tf_op jit(solution)/shard_map/all_to_all | solution.py:42
  33.9 0.1 pad_add_fusion.place_ref
  34.0 0.0 copy-done.5
  34.1 0.0 copy-start.6
  34.1 27.7 %all-gather = bf16[1216,384]{1,0:T(8,128)(2,1)S(1)} all-gather(bf16[152,384]{1,0:T(8,128)(2,1)S(1)} %get-tuple-element.15), channel_id=2, replica_groups=mesh['seq_0'=4,'seq_1a'=4,'seq_1b'=2,'seq_2'=2,'tp'=8] {'tp'}, dimensions={0}, use_global_device_ids=true | all-gather | bytes 1050624 | tf_op jit(solution)/shard_map/all_gather | solution.py:367
  61.8 1.8 shard_map.123.own_ref
  63.5 7.1 %collective-permute-start = (bf16[8,152,384]{2,1,0:T(8,128)(2,1)S(1)}, bf16[8,152,384]{2,1,0:T(8,128)(2,1)S(1)}, u32[]{:S(2)}, u32[]{:S(2)}) collective-permute-start(bf16[8,152,384]{2,1,0:T(8,128)(2,1)S(1)} %shard_map.123.own_ref), channel_id=1, source_target_pairs={{0,8},{8,0},{1,9},{9,1},{2,10},{10,2},{3,11},{11,3},{4,12},{12,4},... | collective-permute-start | bytes 2801672 | tf_op jit(solution)/shard_map/ppermute | solution.py:369
  70.6 2.1 collective-permute-done.other_ref
  72.7 0.0 copy-start
  72.7 0.9 copy-done
  73.7 0.0 all-to-all-done.1
  73.7 0.0 copy-done.6
  73.7 0.0 copy-start.1
  73.7 1.2 copy-done.1
  74.9 2.7 %shard_map.125 = (bf16[2,128,128]{2,1,0:T(8,128)(2,1)S(1)}, bf16[8,2,152,256]{3,2,1,0:T(8,128)(2,1)}) custom-call(s32[1]{0:T(128)} %bitcast.2.core_ref, bf16[8,152,384]{2,1,0:T(8,128)(2,1)S(1)} %shard_map.123.own_ref, bf16[8,152,384]{2,1,0:T(8,128)(2,1)S(1)} %copy-done.1, bf16[8,8,48,384]{3,2,1,0:T(8,128)(2,1)S(1)} %bitcast.8, f32[2,256]{1,0:T(2,128)S(1)} %copy-done.6), custom_call_target="tpu_custom_call" | custom-call | tf_op jit(solution)/shard_map/pallas_call | solution.py:371
  77.5 0.0 copy-start.7
  77.6 22.6 %all_to_all.21.pair_ref = bf16[8,2,152,256]{3,2,1,0:T(8,128)(2,1)S(1)} all-to-all(bf16[8,2,152,256]{3,2,1,0:T(8,128)(2,1)} %get-tuple-element.18), channel_id=1, replica_groups=mesh['seq_0'=4,'seq_1a'=4,'seq_1b'=2,'seq_2'=2,'tp'=8] {'seq_0','seq_1b'}, dimensions={0} | all-to-all | bytes 2490368 | tf_op jit(solution)/shard_map/all_to_all | solution.py:42
  100.2 0.0 copy-done.7
  100.2 3.2 %shard_map.126 = bf16[8,8,40,128]{3,2,1,0:T(8,128)(2,1)} custom-call(s32[4]{0:T(128)S(1)} %copy-done.7, s32[3]{0:T(128)S(1)} %pad_add_fusion.place_ref, bf16[2,128,128]{2,1,0:T(8,128)(2,1)S(1)} %get-tuple-element.17.query_ref, bf16[8,2,152,256]{3,2,1,0:T(8,128)(2,1)S(1)} %all_to_all.21.pair_ref), custom_call_target="tpu_custom_call" | custom-call | tf_op jit(solution)/shard_map/pallas_call | solution.py:383
  103.4 0.0 copy-start.2
  103.4 0.0 copy-start.3
  103.4 6.6 %all-to-all-start.3 = ((bf16[64,40,128]{2,1,0:T(8,128)(2,1)}), bf16[64,40,128]{2,1,0:T(8,128)(2,1)S(1)}, u32[]{:S(2)}, u32[]{:S(2)}) async-start(bf16[64,40,128]{2,1,0:T(8,128)(2,1)} %bitcast.6), calls=%async_computation.3 | async-start | bytes 1310720 | tf_op jit(solution)/shard_map/all_to_all | solution.py:42
  110.0 48.8 %shard_map.127 = (bf16[256,384]{1,0:T(8,128)(2,1)}, bf16[256,384]{1,0:T(8,128)(2,1)}, bf16[256,384]{1,0:T(8,128)(2,1)}, bf16[256,384]{1,0:T(8,128)(2,1)}, bf16[2...) custom-call(s32[1]{0:T(128)} %bitcast.tp_ref, ...), custom_call_target="tpu_custom_call" | custom-call | tf_op jit(solution)/shard_map/pallas_call | solution.py:336
  158.8 3.1 %collective-permute-start.1 = (bf16[256,384]{1,0:T(8,128)(2,1)}, bf16[256,384]{1,0:T(8,128)(2,1)S(1)}, u32[]{:S(2)}, u32[]{:S(2)}) collective-permute-start(bf16[256,384]{1,0:T(8,128)(2,1)} %get-tuple-element.20), channel_id=1, source_target_pairs={{0,1},{1,2},{2,3},{3,4},{4,5},{5,6},{6,7},{7,0},{8,9},{9,10},{10,1... | collective-permute-start | bytes 589832 | tf_op jit(solution)/shard_map/ppermute | solution.py:346
  161.9 5.2 %collective-permute-start.2 = (bf16[256,384]{1,0:T(8,128)(2,1)}, bf16[256,384]{1,0:T(8,128)(2,1)S(1)}, u32[]{:S(2)}, u32[]{:S(2)}) collective-permute-start(bf16[256,384]{1,0:T(8,128)(2,1)} %get-tuple-element.21), channel_id=1, source_target_pairs={{0,2},{1,3},{2,4},{3,5},{4,6},{5,7},{6,0},{7,1},{8,10},{9,11},{10,... | collective-permute-start | bytes 589832 | tf_op jit(solution)/shard_map/ppermute | solution.py:346
  167.1 2.2 %collective-permute-start.3 = (bf16[256,384]{1,0:T(8,128)(2,1)}, bf16[256,384]{1,0:T(8,128)(2,1)S(1)}, u32[]{:S(2)}, u32[]{:S(2)}) collective-permute-start(bf16[256,384]{1,0:T(8,128)(2,1)} %get-tuple-element.22), channel_id=1, source_target_pairs={{0,3},{1,4},{2,5},{3,6},{4,7},{5,0},{6,1},{7,2},{8,11},{9,12},{10,... | collective-permute-start | bytes 589832 | tf_op jit(solution)/shard_map/ppermute | solution.py:346
  169.3 4.9 %collective-permute-start.4 = (bf16[256,384]{1,0:T(8,128)(2,1)}, bf16[256,384]{1,0:T(8,128)(2,1)S(1)}, u32[]{:S(2)}, u32[]{:S(2)}) collective-permute-start(bf16[256,384]{1,0:T(8,128)(2,1)} %get-tuple-element.23), channel_id=1, source_target_pairs={{0,4},{1,5},{2,6},{3,7},{4,0},{5,1},{6,2},{7,3},{8,12},{9,13},{10,... | collective-permute-start | bytes 589832 | tf_op jit(solution)/shard_map/ppermute | solution.py:346
  174.2 3.2 %collective-permute-start.5 = (bf16[256,384]{1,0:T(8,128)(2,1)}, bf16[256,384]{1,0:T(8,128)(2,1)S(1)}, u32[]{:S(2)}, u32[]{:S(2)}) collective-permute-start(bf16[256,384]{1,0:T(8,128)(2,1)} %get-tuple-element.24), channel_id=1, source_target_pairs={{0,5},{1,6},{2,7},{3,0},{4,1},{5,2},{6,3},{7,4},{8,13},{9,14},{10,... | collective-permute-start | bytes 589832 | tf_op jit(solution)/shard_map/ppermute | solution.py:346
  177.4 0.0 collective-permute-done.1.refs_1_
  177.4 4.2 %collective-permute-start.6 = (bf16[256,384]{1,0:T(8,128)(2,1)}, bf16[256,384]{1,0:T(8,128)(2,1)S(1)}, u32[]{:S(2)}, u32[]{:S(2)}) collective-permute-start(bf16[256,384]{1,0:T(8,128)(2,1)} %get-tuple-element.25), channel_id=1, source_target_pairs={{0,6},{1,7},{2,0},{3,1},{4,2},{5,3},{6,4},{7,5},{8,14},{9,15},{10,... | collective-permute-start | bytes 589832 | tf_op jit(solution)/shard_map/ppermute | solution.py:346
  181.6 0.0 collective-permute-done.2.refs_2_
  181.6 4.3 %collective-permute-start.7 = (bf16[256,384]{1,0:T(8,128)(2,1)}, bf16[256,384]{1,0:T(8,128)(2,1)S(1)}, u32[]{:S(2)}, u32[]{:S(2)}) collective-permute-start(bf16[256,384]{1,0:T(8,128)(2,1)} %get-tuple-element.26), channel_id=1, source_target_pairs={{0,7},{1,0},{2,1},{3,2},{4,3},{5,4},{6,5},{7,6},{8,15},{9,8},{10,9... | collective-permute-start | bytes 589832 | tf_op jit(solution)/shard_map/ppermute | solution.py:346
  185.9 3.9 %collective-permute-done.3.refs_3_ = bf16[256,384]{1,0:T(8,128)(2,1)S(1)} collective-permute-done((bf16[256,384]{1,0:T(8,128)(2,1)}, bf16[256,384]{1,0:T(8,128)(2,1)S(1)}, u32[]{:S(2)}, u32[]{:S(2)}) %collective-permute-start.3) | collective-permute-done | bytes 196640 | tf_op jit(solution)/shard_map/ppermute | solution.py:346
  189.8 0.0 collective-permute-done.4.refs_4_
  189.8 10.4 %collective-permute-done.5.refs_5_ = bf16[256,384]{1,0:T(8,128)(2,1)S(1)} collective-permute-done((bf16[256,384]{1,0:T(8,128)(2,1)}, bf16[256,384]{1,0:T(8,128)(2,1)S(1)}, u32[]{:S(2)}, u32[]{:S(2)}) %collective-permute-start.5) | collective-permute-done | bytes 196640 | tf_op jit(solution)/shard_map/ppermute | solution.py:346
  200.2 2.8 %collective-permute-done.6.refs_6_ = bf16[256,384]{1,0:T(8,128)(2,1)S(1)} collective-permute-done((bf16[256,384]{1,0:T(8,128)(2,1)}, bf16[256,384]{1,0:T(8,128)(2,1)S(1)}, u32[]{:S(2)}, u32[]{:S(2)}) %collective-permute-start.6) | collective-permute-done | bytes 196640 | tf_op jit(solution)/shard_map/ppermute | solution.py:346
  203.0 8.6 %collective-permute-done.7.refs_7_ = bf16[256,384]{1,0:T(8,128)(2,1)S(1)} collective-permute-done((bf16[256,384]{1,0:T(8,128)(2,1)}, bf16[256,384]{1,0:T(8,128)(2,1)S(1)}, u32[]{:S(2)}, u32[]{:S(2)}) %collective-permute-start.7) | collective-permute-done | bytes 196640 | tf_op jit(solution)/shard_map/ppermute | solution.py:346
  211.7 0.0 all-to-all-done.3
  211.7 0.0 copy-done.2
  211.7 0.0 copy-done.3
  211.7 0.0 copy-done.8
  211.7 0.0 copy-start.4
  211.7 0.9 copy-done.4
  212.6 1.8 shard_map.128
  (2 shorter events, 0.0 us)
Async XLA Ops:
  29.4 4.6 %copy-start.5 = (bf16[3,4,384]{2,1,0:T(4,128)(2,1)S(1)}, bf16[3,4,384]{2,1,0:T(4,128)(2,1)}, u32[]{:S(2)}) copy-start(bf16[3,4,384]{2,1,0:T(4,128)(2,1)} %refs_10_.1) | copy-start | bytes 27652
  29.4 44.2 %all-to-all-start.1 = ((bf16[8,384,384]{2,1,0:T(8,128)(2,1)}), bf16[8,384,384]{2,1,0:T(8,128)(2,1)S(1)}, u32[]{:S(2)}, u32[]{:S(2)}) async-start(bf16[8,384,384]{2,1,0:T(8,128)(2,1)} %shard_map.124), calls=%async_computation.1 | async-start | bytes 4718592 | tf_op jit(solution)/shard_map/all_to_all | solution.py:42
  34.1 39.6 %copy-start.6 = (f32[2,256]{1,0:T(2,128)S(1)}, f32[2,256]{1,0:T(2,128)}, u32[]{:S(2)}) copy-start(f32[2,256]{1,0:T(2,128)} %gain_ref.1) | copy-start | bytes 6148
  63.5 9.2 %collective-permute-start = (bf16[8,152,384]{2,1,0:T(8,128)(2,1)S(1)}, bf16[8,152,384]{2,1,0:T(8,128)(2,1)S(1)}, u32[]{:S(2)}, u32[]{:S(2)}) collective-permute-start(bf16[8,152,384]{2,1,0:T(8,128)(2,1)S(1)} %shard_map.123.own_ref), channel_id=1, source_target_pairs={{0,8},{8,0},{1,9},{9,1},{2,10},{10,2},{3,11},{11,3},{4,12},{12,4},... | collective-permute-start | bytes 2801672 | tf_op jit(solution)/shard_map/ppermute | solution.py:369
  72.7 0.9 copy-start
  73.7 1.2 copy-start.1
  77.5 22.7 %copy-start.7 = (s32[4]{0:T(128)S(1)}, s32[4]{0:T(128)}, u32[]{:S(2)}) copy-start(s32[4]{0:T(128)} %limit_ref.1) | copy-start | bytes 52
  103.4 108.3 %copy-start.2 = (bf16[4,32,384]{2,1,0:T(8,128)(2,1)S(1)}, bf16[4,32,384]{2,1,0:T(8,128)(2,1)}, u32[]{:S(2)}) copy-start(bf16[4,32,384]{2,1,0:T(8,128)(2,1)} %refs_9_.1) | copy-start | bytes 294916
  103.4 108.3 %copy-start.3 = (f32[4,32,384]{2,1,0:T(8,128)S(1)}, f32[4,32,384]{2,1,0:T(8,128)}, u32[]{:S(2)}) copy-start(f32[4,32,384]{2,1,0:T(8,128)} %refs_8_.1) | copy-start | bytes 589828
  103.4 108.3 %copy-start.8 = (s32[4]{0:T(128)S(1)}, s32[4]{0:T(128)}, u32[]{:S(2)}) copy-start(s32[4]{0:T(128)} %flag_ref.1) | copy-start | bytes 52
  103.4 108.3 %all-to-all-start.3 = ((bf16[64,40,128]{2,1,0:T(8,128)(2,1)}), bf16[64,40,128]{2,1,0:T(8,128)(2,1)S(1)}, u32[]{:S(2)}, u32[]{:S(2)}) async-start(bf16[64,40,128]{2,1,0:T(8,128)(2,1)} %bitcast.6), calls=%async_computation.3 | async-start | bytes 1310720 | tf_op jit(solution)/shard_map/all_to_all | solution.py:42
  158.8 18.6 %collective-permute-start.1 = (bf16[256,384]{1,0:T(8,128)(2,1)}, bf16[256,384]{1,0:T(8,128)(2,1)S(1)}, u32[]{:S(2)}, u32[]{:S(2)}) collective-permute-start(bf16[256,384]{1,0:T(8,128)(2,1)} %get-tuple-element.20), channel_id=1, source_target_pairs={{0,1},{1,2},{2,3},{3,4},{4,5},{5,6},{6,7},{7,0},{8,9},{9,10},{10,1... | collective-permute-start | bytes 589832 | tf_op jit(solution)/shard_map/ppermute | solution.py:346
  161.9 19.7 %collective-permute-start.2 = (bf16[256,384]{1,0:T(8,128)(2,1)}, bf16[256,384]{1,0:T(8,128)(2,1)S(1)}, u32[]{:S(2)}, u32[]{:S(2)}) collective-permute-start(bf16[256,384]{1,0:T(8,128)(2,1)} %get-tuple-element.21), channel_id=1, source_target_pairs={{0,2},{1,3},{2,4},{3,5},{4,6},{5,7},{6,0},{7,1},{8,10},{9,11},{10,... | collective-permute-start | bytes 589832 | tf_op jit(solution)/shard_map/ppermute | solution.py:346
  167.1 22.7 %collective-permute-start.3 = (bf16[256,384]{1,0:T(8,128)(2,1)}, bf16[256,384]{1,0:T(8,128)(2,1)S(1)}, u32[]{:S(2)}, u32[]{:S(2)}) collective-permute-start(bf16[256,384]{1,0:T(8,128)(2,1)} %get-tuple-element.22), channel_id=1, source_target_pairs={{0,3},{1,4},{2,5},{3,6},{4,7},{5,0},{6,1},{7,2},{8,11},{9,12},{10,... | collective-permute-start | bytes 589832 | tf_op jit(solution)/shard_map/ppermute | solution.py:346
  169.3 20.5 %collective-permute-start.4 = (bf16[256,384]{1,0:T(8,128)(2,1)}, bf16[256,384]{1,0:T(8,128)(2,1)S(1)}, u32[]{:S(2)}, u32[]{:S(2)}) collective-permute-start(bf16[256,384]{1,0:T(8,128)(2,1)} %get-tuple-element.23), channel_id=1, source_target_pairs={{0,4},{1,5},{2,6},{3,7},{4,0},{5,1},{6,2},{7,3},{8,12},{9,13},{10,... | collective-permute-start | bytes 589832 | tf_op jit(solution)/shard_map/ppermute | solution.py:346
  174.2 26.0 %collective-permute-start.5 = (bf16[256,384]{1,0:T(8,128)(2,1)}, bf16[256,384]{1,0:T(8,128)(2,1)S(1)}, u32[]{:S(2)}, u32[]{:S(2)}) collective-permute-start(bf16[256,384]{1,0:T(8,128)(2,1)} %get-tuple-element.24), channel_id=1, source_target_pairs={{0,5},{1,6},{2,7},{3,0},{4,1},{5,2},{6,3},{7,4},{8,13},{9,14},{10,... | collective-permute-start | bytes 589832 | tf_op jit(solution)/shard_map/ppermute | solution.py:346
  177.4 25.6 %collective-permute-start.6 = (bf16[256,384]{1,0:T(8,128)(2,1)}, bf16[256,384]{1,0:T(8,128)(2,1)S(1)}, u32[]{:S(2)}, u32[]{:S(2)}) collective-permute-start(bf16[256,384]{1,0:T(8,128)(2,1)} %get-tuple-element.25), channel_id=1, source_target_pairs={{0,6},{1,7},{2,0},{3,1},{4,2},{5,3},{6,4},{7,5},{8,14},{9,15},{10,... | collective-permute-start | bytes 589832 | tf_op jit(solution)/shard_map/ppermute | solution.py:346
  181.6 30.0 %collective-permute-start.7 = (bf16[256,384]{1,0:T(8,128)(2,1)}, bf16[256,384]{1,0:T(8,128)(2,1)S(1)}, u32[]{:S(2)}, u32[]{:S(2)}) collective-permute-start(bf16[256,384]{1,0:T(8,128)(2,1)} %get-tuple-element.26), channel_id=1, source_target_pairs={{0,7},{1,0},{2,1},{3,2},{4,3},{5,4},{6,5},{7,6},{8,15},{9,8},{10,9... | collective-permute-start | bytes 589832 | tf_op jit(solution)/shard_map/ppermute | solution.py:346
  211.7 0.9 copy-start.4

commit v9 on v7

--- a/solution.py
+++ b/solution.py
@@ -87,19 +87,15 @@
             out_ref[to, at : at + 8] = text.astype(BF16)
 
 
-def spread_body(got_ref, out_hbm, sems):
-    copies = []
+def spread_body(got_ref, out_hbm, block_ref, sems):
     sources = got_ref.shape[0]
-    deep = out_hbm.shape[1] // sources
-    for copy in range(out_hbm.shape[0]):
-        for source in range(sources):
-            copies.append(
-                pltpu.make_async_copy(
-                    got_ref.at[source, pl.ds(0, deep)],
-                    out_hbm.at[copy, pl.ds(source * deep, deep)],
-                    sems.at[copy, source],
-                )
-            )
+    deep = block_ref.shape[0] // sources
+    for source in range(sources):
+        block_ref[source * deep : (source + 1) * deep] = got_ref[source, :deep]
+    copies = [
+        pltpu.make_async_copy(block_ref, out_hbm.at[copy], sems.at[copy])
+        for copy in range(out_hbm.shape[0])
+    ]
     for copy in copies:
         copy.start()
     for copy in copies:
@@ -158,15 +154,24 @@
     mod_ref[0, vectors:] = stacked_parts(line, 8).astype(BF16)
 
 
-def project_body(core_ref, own_ref, other_ref, w_ref, gain_ref, query_ref, pair_ref):
+def project_body(
+    core_ref, own_ref, other_ref, w_hbm, gain_ref, query_ref, pair_ref, w_ref, sems
+):
     groups, rows, width = own_ref.shape
     _, sources, deep, columns = w_ref.shape
     near = cores = 2
+    fetches = []
+    for x in range(w_ref.shape[0] // near):
+        at = pl.ds(x * near, near)
+        fetches.append(pltpu.make_async_copy(w_hbm.at[at], w_ref.at[at], sems.at[x]))
+        fetches[-1].start()
     ys = near * sources // cores
     per_group = width // deep
     total = jnp.zeros((2 * rows, columns), F32)
     for g in range(groups):
         pieces = []
+        if g % 2 == 0:
+            fetches[g // 2].wait()
         for step in range(per_group):
             flat = g * per_group + step
             core = flat % cores
@@ -339,7 +344,10 @@
         [VMEM],
         8,
         outs=HBM,
-        scratch=[pltpu.SemaphoreType.DMA((around, sources))],
+        scratch=[
+            pltpu.VMEM((sources * deep, kinds * HD), BF16),
+            pltpu.SemaphoreType.DMA((around,)),
+        ],
     )(got)
     weight = swap(weight, (X, NEAR)).reshape(around, sources, deep, kinds * HD)
 
@@ -356,9 +364,13 @@
     query, pairs = call(
         project_body,
         (shaped(2, sources * img_half, HD), shaped(around, 2, rows, 2 * HD)),
-        [SMEM] + [VMEM] * 4,
+        [SMEM, VMEM, VMEM, HBM, VMEM],
         16,
-    )(core_index, own, other, weight, qk_gain)
+        scratch=[
+            pltpu.VMEM((around, sources, deep, kinds * HD), BF16),
+            pltpu.SemaphoreType.DMA((xs,)),
+        ],
+    )(core_index, own, other, pltpu.with_memory_space_constraint(weight, pltpu.HBM), qk_gain)
     pairs = swap(pairs, (X, NEAR))
     attended = call(
         functools.partial(attend_body, img_half, txt_half),

time: 139 us -> 138 us (level)
  local copies, waits for them, and re-layouts: 2.17 us -> 0.04 us
    unnamed x18 -> x14, local copies, waits for them, and re-layouts: 2.17 us -> 0.04 us
where the time goes in v9:
time: 138 us; the launch traced here: 137 us
  blocking collectives  112 us (81%)
  Pallas kernels  11.9 us (9%)
  starting transfers between devices  10.7 us (8%)
  waiting for transfers between devices  2.1 us (2%)
    all_to_all x4, blocking collectives, swap(): return lax.all_to_all(value, axis, 0, 0, tiled=True)  82.3 us
    all_gather x1, blocking collectives, local(): wide = lax.all_gather(joined, TP, axis=0, tiled=False)  29.5 us
    ppermute x1, starting transfers between devices, local(): other = lax.ppermute(own, CORE, [(0, 1), (1, 0)])  6.14 us
    all_to_all x1, starting transfers between devices, swap(): return lax.all_to_all(value, axis, 0, 0, tiled=True)  4.57 us
    pallas_call x1, Pallas kernels, local(): call(project_body, (shaped(2, sources * img_half, HD), shaped(around, 2,...  2.79 us
  transfers between devices with their start and end apart: 2, of which 1 were waited for; matrix products, arithmetic and copies ran while one was open for 0% of the time, Pallas kernels for 1%

profile of v9, /device:TPU:1, one launch (start us, length us, event | category | flops | bytes accessed | tf_op | source)
XLA Modules:
  0.0 137.4 jit_solution(13067504477039493450)
XLA Ops:
  0.6 1.1 shard_map.121
  1.7 25.9 %all_to_all.25.got_ref = bf16[8,88,384]{2,1,0:T(8,128)(2,1)S(1)} all-to-all(bf16[8,88,384]{2,1,0:T(8,128)(2,1)S(1)} %shard_map.121), channel_id=1, replica_groups=mesh['seq_0'=4,'seq_1a'=4,'seq_1b'=2,'seq_2'=2,'tp'=8] {'seq_1a','seq_2'}, dimensions={0} | all-to-all | bytes 1081344 | tf_op jit(solution)/shard_map/all_to_all | solution.py:42
  27.6 1.5 %shard_map.124 = bf16[8,384,384]{2,1,0:T(8,128)(2,1)} custom-call(bf16[8,88,384]{2,1,0:T(8,128)(2,1)S(1)} %all_to_all.25.got_ref), custom_call_target="tpu_custom_call" | custom-call | tf_op jit(solution)/shard_map/pallas_call | solution.py:341
  29.1 0.0 copy-start.3
  29.1 4.6 %all-to-all-start.1 = ((bf16[8,384,384]{2,1,0:T(8,128)(2,1)}), bf16[8,384,384]{2,1,0:T(8,128)(2,1)}, u32[]{:S(2)}, u32[]{:S(2)}) async-start(bf16[8,384,384]{2,1,0:T(8,128)(2,1)} %shard_map.124), calls=%async_computation.1 | async-start | bytes 4718592 | tf_op jit(solution)/shard_map/all_to_all | solution.py:42
  33.7 0.1 pad_add_fusion.place_ref
  33.8 0.0 copy-done.3
  33.8 0.0 copy-start.4
  33.8 29.5 %all-gather = bf16[1216,384]{1,0:T(8,128)(2,1)S(1)} all-gather(bf16[152,384]{1,0:T(8,128)(2,1)S(1)} %get-tuple-element.7), channel_id=2, replica_groups=mesh['seq_0'=4,'seq_1a'=4,'seq_1b'=2,'seq_2'=2,'tp'=8] {'tp'}, dimensions={0}, use_global_device_ids=true | all-gather | bytes 1050624 | tf_op jit(solution)/shard_map/all_gather | solution.py:360
  63.3 1.8 %shard_map.123.own_ref = bf16[8,152,384]{2,1,0:T(8,128)(2,1)S(1)} custom-call(s32[3]{0:T(128)S(1)} %pad_add_fusion.place_ref, bf16[8,152,384]{2,1,0:T(8,128)(2,1)S(1)} %bitcast.6, bf16[128,384]{1,0:T(8,128)(2,1)S(1)} %get-tuple-element.8.prev_ref), custom_call_target="tpu_custom_call" | custom-call | tf_op jit(solution)/shard_map/pallas_call | solution.py:361
  65.1 6.1 %collective-permute-start = (bf16[8,152,384]{2,1,0:T(8,128)(2,1)S(1)}, bf16[8,152,384]{2,1,0:T(8,128)(2,1)S(1)}, u32[]{:S(2)}, u32[]{:S(2)}) collective-permute-start(bf16[8,152,384]{2,1,0:T(8,128)(2,1)S(1)} %shard_map.123.own_ref), channel_id=1, source_target_pairs={{0,8},{8,0},{1,9},{9,1},{2,10},{10,2},{3,11},{11,3},{4,12},{12,4},... | collective-permute-start | bytes 2801672 | tf_op jit(solution)/shard_map/ppermute | solution.py:362
  71.3 2.1 %collective-permute-done.other_ref = bf16[8,152,384]{2,1,0:T(8,128)(2,1)S(1)} collective-permute-done((bf16[8,152,384]{2,1,0:T(8,128)(2,1)S(1)}, bf16[8,152,384]{2,1,0:T(8,128)(2,1)S(1)}, u32[]{:S(2)}, u32[]{:S(2)}) %collective-permute-start) | collective-permute-done | bytes 933920 | tf_op jit(solution)/shard_map/ppermute | solution.py:362
  73.4 0.0 all-to-all-done.1
  73.4 0.0 copy-done.4
  73.4 2.8 %shard_map.125 = (bf16[2,128,128]{2,1,0:T(8,128)(2,1)S(1)}, bf16[8,2,152,256]{3,2,1,0:T(8,128)(2,1)S(1)}) custom-call(s32[1]{0:T(128)} %bitcast.2.core_ref, bf16[8,152,384]{2,1,0:T(8,128)(2,1)S(1)} %shard_map.123.own_ref, bf16[8,152,384]{2,1,0:T(8,128)(2,1)S(1)} %collective-permute-done.other_ref, bf16[8,8,48,384]{3,2,1,0:T(8,128)(2,1)} %bitcast.5.w_hbm, ...), custom_call_target="tpu_custom_call" | custom-call | tf_op jit(solution)/shard_map/pallas_call | solution.py:364
  76.2 0.0 copy-start.6
  76.2 0.0 copy-start
  76.2 0.0 copy-start.5
  76.2 22.8 %all_to_all.26.pair_ref = bf16[8,2,152,256]{3,2,1,0:T(8,128)(2,1)S(1)} all-to-all(bf16[8,2,152,256]{3,2,1,0:T(8,128)(2,1)S(1)} %get-tuple-element.10), channel_id=1, replica_groups=mesh['seq_0'=4,'seq_1a'=4,'seq_1b'=2,'seq_2'=2,'tp'=8] {'seq_0','seq_1b'}, dimensions={0} | all-to-all | bytes 2490368 | tf_op jit(solution)/shard_map/all_to_all | solution.py:42
  99.0 0.0 copy-done.6
  99.0 2.2 %shard_map.126 = bf16[8,40,128]{2,1,0:T(8,128)(2,1)S(1)} custom-call(s32[4]{0:T(128)S(1)} %copy-done.6, s32[3]{0:T(128)S(1)} %pad_add_fusion.place_ref, bf16[2,128,128]{2,1,0:T(8,128)(2,1)S(1)} %get-tuple-element.9.query_ref, bf16[8,2,152,256]{3,2,1,0:T(8,128)(2,1)S(1)} %all_to_all.26.pair_ref), custom_call_target="tpu_custom_call" | custom-call | tf_op jit(solution)/shard_map/pallas_call | solution.py:375
  101.2 11.4 %all_to_all.27.att_ref = bf16[8,40,128]{2,1,0:T(8,128)(2,1)S(1)} all-to-all(bf16[8,40,128]{2,1,0:T(8,128)(2,1)S(1)} %shard_map.126), channel_id=1, replica_groups=mesh['seq_0'=4,'seq_1a'=4,'seq_1b'=2,'seq_2'=2,'tp'=8] {'seq_1a','seq_2'}, dimensions={0} | all-to-all | bytes 163840 | tf_op jit(solution)/shard_map/all_to_all | solution.py:42
  112.7 0.0 copy-done
  112.7 0.0 copy-done.5
  112.7 0.0 copy-start.1
  112.7 0.0 copy-start.2
  112.7 0.9 shard_map.127
  113.6 22.2 %all_to_all.28.part_ref = bf16[8,104,384]{2,1,0:T(8,128)(2,1)S(1)} all-to-all(bf16[8,104,384]{2,1,0:T(8,128)(2,1)S(1)} %shard_map.127), channel_id=1, replica_groups=mesh['seq_0'=4,'seq_1a'=4,'seq_1b'=2,'seq_2'=2,'tp'=8] {'tp'}, dimensions={0} | all-to-all | bytes 1277952 | tf_op jit(solution)/shard_map/all_to_all | solution.py:42
  135.8 0.0 copy-done.1
  135.8 0.0 copy-done.2
  135.8 1.6 %shard_map.128 = (f32[4,32,384]{2,1,0:T(8,128)}, f32[4,32,384]{2,1,0:T(8,128)}, f32[4]{0:T(128)}) custom-call(s32[4]{0:T(128)S(1)} %copy-done.5, bf16[8,104,384]{2,1,0:T(8,128)(2,1)S(1)} %all_to_all.28.part_ref, f32[4,32,384]{2,1,0:T(8,128)S(1)} %copy-done.2, bf16[4,32,384]{2,1,0:T(8,128)(2,1)S(1)} %copy-done.1, bf16[3,4,384]{2,1,0:T(4,128)(2,1)S(1)} %copy-done.3), custom_call_target="tpu_custom_call" | custom-call | tf_op jit(solution)/shard_map/pallas_call | solution.py:393
  (1 shorter events, 0.0 us)
Async XLA Ops:
  29.1 4.7 %copy-start.3 = (bf16[3,4,384]{2,1,0:T(4,128)(2,1)S(1)}, bf16[3,4,384]{2,1,0:T(4,128)(2,1)}, u32[]{:S(2)}) copy-start(bf16[3,4,384]{2,1,0:T(4,128)(2,1)} %mod_ref.3) | copy-start | bytes 27652
  29.1 44.3 %all-to-all-start.1 = ((bf16[8,384,384]{2,1,0:T(8,128)(2,1)}), bf16[8,384,384]{2,1,0:T(8,128)(2,1)}, u32[]{:S(2)}, u32[]{:S(2)}) async-start(bf16[8,384,384]{2,1,0:T(8,128)(2,1)} %shard_map.124), calls=%async_computation.1 | async-start | bytes 4718592 | tf_op jit(solution)/shard_map/all_to_all | solution.py:42
  33.8 39.6 %copy-start.4 = (f32[2,256]{1,0:T(2,128)S(1)}, f32[2,256]{1,0:T(2,128)}, u32[]{:S(2)}) copy-start(f32[2,256]{1,0:T(2,128)} %gain_ref.1) | copy-start | bytes 6148
  65.1 8.2 %collective-permute-start = (bf16[8,152,384]{2,1,0:T(8,128)(2,1)S(1)}, bf16[8,152,384]{2,1,0:T(8,128)(2,1)S(1)}, u32[]{:S(2)}, u32[]{:S(2)}) collective-permute-start(bf16[8,152,384]{2,1,0:T(8,128)(2,1)S(1)} %shard_map.123.own_ref), channel_id=1, source_target_pairs={{0,8},{8,0},{1,9},{9,1},{2,10},{10,2},{3,11},{11,3},{4,12},{12,4},... | collective-permute-start | bytes 2801672 | tf_op jit(solution)/shard_map/ppermute | solution.py:362
  76.2 22.8 %copy-start.6 = (s32[4]{0:T(128)S(1)}, s32[4]{0:T(128)}, u32[]{:S(2)}) copy-start(s32[4]{0:T(128)} %limit_ref.1) | copy-start | bytes 52
  76.2 36.5 %copy-start = (bf16[256,3072]{1,0:T(8,128)(2,1)S(1)}, bf16[256,3072]{1,0:T(8,128)(2,1)}, u32[]{:S(2)}) copy-start(bf16[256,3072]{1,0:T(8,128)(2,1)} %w_ref.1) | copy-start | bytes 4718596
  76.2 36.5 %copy-start.5 = (s32[4]{0:T(128)S(1)}, s32[4]{0:T(128)}, u32[]{:S(2)}) copy-start(s32[4]{0:T(128)} %flag_ref.3) | copy-start | bytes 52
  112.7 23.2 %copy-start.1 = (bf16[4,32,384]{2,1,0:T(8,128)(2,1)S(1)}, bf16[4,32,384]{2,1,0:T(8,128)(2,1)}, u32[]{:S(2)}) copy-start(bf16[4,32,384]{2,1,0:T(8,128)(2,1)} %img_ref.1) | copy-start | bytes 294916
  112.7 23.2 %copy-start.2 = (f32[4,32,384]{2,1,0:T(8,128)S(1)}, f32[4,32,384]{2,1,0:T(8,128)}, u32[]{:S(2)}) copy-start(f32[4,32,384]{2,1,0:T(8,128)} %cache_ref.1) | copy-start | bytes 589828

commit v10 on v9

--- a/solution.py
+++ b/solution.py
@@ -102,7 +102,13 @@
         copy.wait()
 
 
-def join_body(deep, img_half, txt_half, far_ref, got_ref, mod_ref, out_ref, prev_ref):
+def join_body(
+    deep, img_half, txt_half, far_ref, flag_ref, got_ref, mod_ref, out_ref, prev_ref, tail_ref
+):
+    tail_no = jnp.int32(-1)
+    for b in range(mod_ref.shape[1]):
+        tail_no = tail_no + jnp.where(flag_ref[b] == 1, 1, 0)
+    tail_ref[0] = tail_no
     sources = got_ref.shape[0]
     width = got_ref.shape[2]
     for source in range(sources):
@@ -154,24 +160,15 @@
     mod_ref[0, vectors:] = stacked_parts(line, 8).astype(BF16)
 
 
-def project_body(
-    core_ref, own_ref, other_ref, w_hbm, gain_ref, query_ref, pair_ref, w_ref, sems
-):
+def project_body(core_ref, own_ref, other_ref, w_ref, gain_ref, query_ref, pair_ref):
     groups, rows, width = own_ref.shape
     _, sources, deep, columns = w_ref.shape
     near = cores = 2
-    fetches = []
-    for x in range(w_ref.shape[0] // near):
-        at = pl.ds(x * near, near)
-        fetches.append(pltpu.make_async_copy(w_hbm.at[at], w_ref.at[at], sems.at[x]))
-        fetches[-1].start()
     ys = near * sources // cores
     per_group = width // deep
     total = jnp.zeros((2 * rows, columns), F32)
     for g in range(groups):
         pieces = []
-        if g % 2 == 0:
-            fetches[g // 2].wait()
         for step in range(per_group):
             flat = g * per_group + step
             core = flat % cores
@@ -351,12 +348,17 @@
     )(got)
     weight = swap(weight, (X, NEAR)).reshape(around, sources, deep, kinds * HD)
 
-    joined, previous = call(
+    joined, previous, tail_no = call(
         functools.partial(join_body, deep, img_half, txt_half),
-        (shaped(rows, width), shaped(sources * img_half, width)),
-        [SMEM, VMEM, VMEM],
+        (
+            shaped(rows, width),
+            shaped(sources * img_half, width),
+            shaped(1, dtype=jnp.int32),
+        ),
+        [SMEM, SMEM, VMEM, VMEM],
         8,
-    )(far_index, got, modulation)
+        outs=(VMEM, VMEM, SMEM),
+    )(far_index, refresh, got, modulation)
     wide = lax.all_gather(joined, TP, axis=0, tiled=False)
     own = call(norm_body, shaped(tps, rows, width), [SMEM, VMEM, VMEM], 12)(place, wide, previous)
     other = lax.ppermute(own, CORE, [(0, 1), (1, 0)])
@@ -364,13 +366,9 @@
     query, pairs = call(
         project_body,
         (shaped(2, sources * img_half, HD), shaped(around, 2, rows, 2 * HD)),
-        [SMEM, VMEM, VMEM, HBM, VMEM],
+        [SMEM] + [VMEM] * 4,
         16,
-        scratch=[
-            pltpu.VMEM((around, sources, deep, kinds * HD), BF16),
-            pltpu.SemaphoreType.DMA((xs,)),
-        ],
-    )(core_index, own, other, pltpu.with_memory_space_constraint(weight, pltpu.HBM), qk_gain)
+    )(core_index, own, other, weight, qk_gain)
     pairs = swap(pairs, (X, NEAR))
     attended = call(
         functools.partial(attend_body, img_half, txt_half),
@@ -380,23 +378,28 @@
     )(text_len, place, query, pairs)
     attended = swap(attended, (FAR, CORE))
 
-    slots = batch - 1
+    tails = [functools.partial(finish, slots) for slots in range(1, batch)]
+    return lax.switch(tail_no[0], tails, refresh, attended, output_weight, cache, img, modulation)
+
+
+def finish(slots, refresh, attended, output_weight, cache, img, modulation):
+    batch, img_rows, width = img.shape
+    rows = slots * img_rows + 8
     parts = call(
         functools.partial(mix_body, img_rows),
-        shaped(tps, slots * img_rows + 8, width),
+        shaped(lax.axis_size(TP), rows, width),
         [SMEM, VMEM, VMEM],
         12,
     )(refresh, attended, output_weight)
     parts = swap(parts, TP)
-
     whole = shaped(batch, img_rows, width, dtype=F32)
-    return pl.pallas_call(
+    return call(
         final_body,
-        out_shape=(whole, whole, shaped(batch, dtype=F32)),
-        in_specs=[SMEM] + [VMEM] * 4,
-        out_specs=(VMEM, VMEM, SMEM),
-        scratch_shapes=[pltpu.VMEM((slots * img_rows + 8, width), F32)],
-        compiler_params=pltpu.CompilerParams(vmem_limit_bytes=8 << 20),
+        (whole, whole, shaped(batch, dtype=F32)),
+        [SMEM] + [VMEM] * 4,
+        8,
+        outs=(VMEM, VMEM, SMEM),
+        scratch=[pltpu.VMEM((rows, width), F32)],
     )(refresh, parts, cache, img, modulation)
 
 

time: 138 us -> 133 us (0.964)
  the two profiles are of different devices: /device:TPU:1 before, /device:TPU:8 now
where the time goes in v10:
time: 133 us; the launch traced here: 132 us
  blocking collectives  94.9 us (71%)
  Pallas kernels  12.2 us (9%)
  starting transfers between devices  11 us (8%)
  waiting for transfers between devices  10.5 us (8%)
  local copies, waits for them, and re-layouts  2.18 us (2%)
  between operations  1.4 us (1%)
    all_to_all x3, blocking collectives, swap(): return lax.all_to_all(value, axis, 0, 0, tiled=True)  62 us
    all_gather x1, blocking collectives, local(): wide = lax.all_gather(joined, TP, axis=0, tiled=False)  32.8 us
    all_to_all x2, starting transfers between devices, swap(): return lax.all_to_all(value, axis, 0, 0, tiled=True)  9.07 us
    all_to_all x2, waiting for transfers between devices, swap(): return lax.all_to_all(value, axis, 0, 0, tiled=True)  7.99 us
    pallas_call x1, Pallas kernels, local(): call(functools.partial(attend_body, img_half, txt_half), shaped(sources,...  2.9 us
  transfers between devices with their start and end apart: 3, of which 2 were waited for; matrix products, arithmetic and copies ran while one was open for 0% of the time, Pallas kernels for 2%

profile of v10, /device:TPU:8, one launch (start us, length us, event | category | flops | bytes accessed | tf_op | source)
XLA Modules:
  0.0 132.2 jit_solution(4133177958377321223)
XLA Ops:
  0.6 1.1 shard_map.136
  1.7 24.7 %all_to_all.35.got_ref = bf16[8,88,384]{2,1,0:T(8,128)(2,1)S(1)} all-to-all(bf16[8,88,384]{2,1,0:T(8,128)(2,1)S(1)} %shard_map.136), channel_id=1, replica_groups=mesh['seq_0'=4,'seq_1a'=4,'seq_1b'=2,'seq_2'=2,'tp'=8] {'seq_1a','seq_2'}, dimensions={0} | all-to-all | bytes 1081344 | tf_op jit(solution)/shard_map/all_to_all | solution.py:42
  26.4 1.5 %shard_map.139 = bf16[8,384,384]{2,1,0:T(8,128)(2,1)} custom-call(bf16[8,88,384]{2,1,0:T(8,128)(2,1)S(1)} %all_to_all.35.got_ref), custom_call_target="tpu_custom_call" | custom-call | tf_op jit(solution)/shard_map/pallas_call | solution.py:338
  27.9 0.0 copy-start.7
  27.9 0.0 copy-start.8
  28.0 5.7 %all-to-all-start.4 = ((bf16[8,384,384]{2,1,0:T(8,128)(2,1)}), bf16[8,384,384]{2,1,0:T(8,128)(2,1)S(1)}, u32[]{:S(2)}, u32[]{:S(2)}) async-start(bf16[8,384,384]{2,1,0:T(8,128)(2,1)} %shard_map.139), calls=%async_computation.4 | async-start | bytes 4718592 | tf_op jit(solution)/shard_map/all_to_all | solution.py:42
  33.7 0.1 pad_add_fusion.place_ref
  33.7 0.0 copy-done.7
  33.7 0.0 copy-done.8
  33.7 1.1 shard_map.137
  34.8 0.0 copy-start.2
  34.9 32.8 %all-gather = bf16[1216,384]{1,0:T(8,128)(2,1)S(1)} all-gather(bf16[152,384]{1,0:T(8,128)(2,1)S(1)} %get-tuple-element.63), channel_id=2, replica_groups=mesh['seq_0'=4,'seq_1a'=4,'seq_1b'=2,'seq_2'=2,'tp'=8] {'tp'}, dimensions={0}, use_global_device_ids=true | all-gather | bytes 1050624 | tf_op jit(solution)/shard_map/all_gather | solution.py:362
  67.7 1.8 %shard_map.138.own_ref = bf16[8,152,384]{2,1,0:T(8,128)(2,1)S(1)} custom-call(s32[3]{0:T(128)S(1)} %pad_add_fusion.place_ref, bf16[8,152,384]{2,1,0:T(8,128)(2,1)S(1)} %bitcast.8, bf16[128,384]{1,0:T(8,128)(2,1)S(1)} %get-tuple-element.64.prev_ref), custom_call_target="tpu_custom_call" | custom-call | tf_op jit(solution)/shard_map/pallas_call | solution.py:363
  69.5 1.9 %collective-permute-start = (bf16[8,152,384]{2,1,0:T(8,128)(2,1)S(1)}, bf16[8,152,384]{2,1,0:T(8,128)(2,1)S(1)}, u32[]{:S(2)}, u32[]{:S(2)}) collective-permute-start(bf16[8,152,384]{2,1,0:T(8,128)(2,1)S(1)} %shard_map.138.own_ref), channel_id=1, source_target_pairs={{0,8},{8,0},{1,9},{9,1},{2,10},{10,2},{3,11},{11,3},{4,12},{12,4},... | collective-permute-start | bytes 2801672 | tf_op jit(solution)/shard_map/ppermute | solution.py:364
  71.4 2.5 %collective-permute-done.other_ref = bf16[8,152,384]{2,1,0:T(8,128)(2,1)S(1)} collective-permute-done((bf16[8,152,384]{2,1,0:T(8,128)(2,1)S(1)}, bf16[8,152,384]{2,1,0:T(8,128)(2,1)S(1)}, u32[]{:S(2)}, u32[]{:S(2)}) %collective-permute-start) | collective-permute-done | bytes 933920 | tf_op jit(solution)/shard_map/ppermute | solution.py:364
  73.9 0.0 copy-start
  73.9 1.0 copy-done
  74.8 0.0 all-to-all-done.4
  74.8 0.0 copy-done.2
  74.8 0.0 copy-start.1
  74.8 1.2 copy-done.1
  76.0 1.5 %shard_map.140 = (bf16[2,128,128]{2,1,0:T(8,128)(2,1)S(1)}, bf16[8,2,152,256]{3,2,1,0:T(8,128)(2,1)S(1)}) custom-call(s32[1]{0:T(128)} %bitcast.4.core_ref, bf16[8,152,384]{2,1,0:T(8,128)(2,1)S(1)} %shard_map.138.own_ref, bf16[8,152,384]{2,1,0:T(8,128)(2,1)S(1)} %copy-done.1, bf16[8,8,48,384]{3,2,1,0:T(8,128)(2,1)S(1)} %bitcast.7, f32[2,256]{1,0:T(2,128)S(1)} %copy-done.2), custom_call_target="tpu_custom_call" | custom-call | tf_op jit(solution)/shard_map/pallas_call | solution.py:366
  77.6 0.0 copy-start.3
  77.6 0.0 copy-start.4
  77.6 0.0 copy-start.5
  77.6 0.0 copy-start.6
  77.6 22.6 %all_to_all.36.pair_ref = bf16[8,2,152,256]{3,2,1,0:T(8,128)(2,1)S(1)} all-to-all(bf16[8,2,152,256]{3,2,1,0:T(8,128)(2,1)S(1)} %get-tuple-element.66), channel_id=1, replica_groups=mesh['seq_0'=4,'seq_1a'=4,'seq_1b'=2,'seq_2'=2,'tp'=8] {'seq_0','seq_1b'}, dimensions={0} | all-to-all | bytes 2490368 | tf_op jit(solution)/shard_map/all_to_all | solution.py:42
  100.2 0.0 copy-done.3
  100.2 2.9 %shard_map.141 = bf16[8,40,128]{2,1,0:T(8,128)(2,1)} custom-call(s32[4]{0:T(128)S(1)} %copy-done.3, s32[3]{0:T(128)S(1)} %pad_add_fusion.place_ref, bf16[2,128,128]{2,1,0:T(8,128)(2,1)S(1)} %get-tuple-element.65.query_ref, bf16[8,2,152,256]{3,2,1,0:T(8,128)(2,1)S(1)} %all_to_all.36.pair_ref), custom_call_target="tpu_custom_call" | custom-call | tf_op jit(solution)/shard_map/pallas_call | solution.py:373
  103.1 3.4 %all-to-all-start.6 = ((bf16[8,40,128]{2,1,0:T(8,128)(2,1)}), bf16[8,40,128]{2,1,0:T(8,128)(2,1)S(1)}, u32[]{:S(2)}, u32[]{:S(2)}) async-start(bf16[8,40,128]{2,1,0:T(8,128)(2,1)} %shard_map.141), calls=%async_computation.6 | async-start | bytes 163840 | tf_op jit(solution)/shard_map/all_to_all | solution.py:42
  107.1 8.0 %all-to-all-done.6 = bf16[8,40,128]{2,1,0:T(8,128)(2,1)S(1)} async-done(((bf16[8,40,128]{2,1,0:T(8,128)(2,1)}), bf16[8,40,128]{2,1,0:T(8,128)(2,1)S(1)}, u32[]{:S(2)}, u32[]{:S(2)}) %all-to-all-start.6) | async-done | bytes 81952 | tf_op jit(solution)/shard_map/all_to_all | solution.py:42
  115.1 0.0 copy-done.4
  115.1 0.0 copy-done.5
  115.1 0.0 copy-done.6
  115.1 17.0 %conditional.1 = ((f32[4,32,384]{2,1,0:T(8,128)}, f32[4,32,384]{2,1,0:T(8,128)}, f32[4]{0:T(128)})) conditional(s32[]{:T(128)} %bitcast.2, (s32[4]{0:T(128)S(1)}, bf16[8,40,128]{2,1,0:T(8,128)(2,1)S(1)}, bf16[256,3072]{1,0:T(8,128)(2,1)S(1)}, f32[4,32,384]{2,1,0:T(8,128)S(1)}, bf16[4,32,384]{2,1,0:T(8,128)(2,1)S(1)}, ...), branch_computations={%region_0.0_spmd, %region_1.0_spmd, %region_2.0_spmd} | conditional | bytes 1277960 | solution.py:382
  115.1 0.9 branch_0_fun.2
  116.0 14.7 %all_to_all.32.part_ref = bf16[8,40,384]{2,1,0:T(8,128)(2,1)S(1)} all-to-all(bf16[8,40,384]{2,1,0:T(8,128)(2,1)S(1)} %branch_0_fun.2), channel_id=1, replica_groups=mesh['seq_0'=4,'seq_1a'=4,'seq_1b'=2,'seq_2'=2,'tp'=8] {'tp'}, dimensions={0} | all-to-all | bytes 491520 | tf_op jit(solution)/shard_map/cond/branch_0_fun/all_to_all | solution.py:42
  130.7 1.4 %branch_0_fun.3 = (f32[4,32,384]{2,1,0:T(8,128)}, f32[4,32,384]{2,1,0:T(8,128)}, f32[4]{0:T(128)}) custom-call(s32[4]{0:T(128)S(1)} %get-tuple-element.36.flag_ref, bf16[8,40,384]{2,1,0:T(8,128)(2,1)S(1)} %all_to_all.32.part_ref, f32[4,32,384]{2,1,0:T(8,128)S(1)} %get-tuple-element.88.cache_ref, bf16[4,32,384]{2,1,0:T(8,128)(2,1)S(1)} %get-tuple-element.40.img_ref, ...), custom_call_target="tpu_custom_call" | custom-call | tf_op jit(solution)/shard_map/cond/branch_0_fun/pallas_call | solution.py:396
Async XLA Ops:
  27.9 5.8 %copy-start.7 = (bf16[3,4,384]{2,1,0:T(4,128)(2,1)S(1)}, bf16[3,4,384]{2,1,0:T(4,128)(2,1)}, u32[]{:S(2)}) copy-start(bf16[3,4,384]{2,1,0:T(4,128)(2,1)} %mod_ref.1) | copy-start | bytes 27652
  27.9 5.8 %copy-start.8 = (s32[4]{0:T(128)S(1)}, s32[4]{0:T(128)}, u32[]{:S(2)}) copy-start(s32[4]{0:T(128)} %flag_ref.1) | copy-start | bytes 52
  28.0 46.9 %all-to-all-start.4 = ((bf16[8,384,384]{2,1,0:T(8,128)(2,1)}), bf16[8,384,384]{2,1,0:T(8,128)(2,1)S(1)}, u32[]{:S(2)}, u32[]{:S(2)}) async-start(bf16[8,384,384]{2,1,0:T(8,128)(2,1)} %shard_map.139), calls=%async_computation.4 | async-start | bytes 4718592 | tf_op jit(solution)/shard_map/all_to_all | solution.py:42
  34.8 40.0 %copy-start.2 = (f32[2,256]{1,0:T(2,128)S(1)}, f32[2,256]{1,0:T(2,128)}, u32[]{:S(2)}) copy-start(f32[2,256]{1,0:T(2,128)} %gain_ref.1) | copy-start | bytes 6148
  69.5 4.4 %collective-permute-start = (bf16[8,152,384]{2,1,0:T(8,128)(2,1)S(1)}, bf16[8,152,384]{2,1,0:T(8,128)(2,1)S(1)}, u32[]{:S(2)}, u32[]{:S(2)}) collective-permute-start(bf16[8,152,384]{2,1,0:T(8,128)(2,1)S(1)} %shard_map.138.own_ref), channel_id=1, source_target_pairs={{0,8},{8,0},{1,9},{9,1},{2,10},{10,2},{3,11},{11,3},{4,12},{12,4},... | collective-permute-start | bytes 2801672 | tf_op jit(solution)/shard_map/ppermute | solution.py:364
  73.9 1.0 copy-start
  74.8 1.2 copy-start.1
  77.6 22.7 %copy-start.3 = (s32[4]{0:T(128)S(1)}, s32[4]{0:T(128)}, u32[]{:S(2)}) copy-start(s32[4]{0:T(128)} %limit_ref.1) | copy-start | bytes 52
  77.6 37.5 %copy-start.4 = (bf16[256,3072]{1,0:T(8,128)(2,1)S(1)}, bf16[256,3072]{1,0:T(8,128)(2,1)}, u32[]{:S(2)}) copy-start(bf16[256,3072]{1,0:T(8,128)(2,1)} %param.20) | copy-start | bytes 4718596
  77.6 37.5 %copy-start.5 = (f32[4,32,384]{2,1,0:T(8,128)S(1)}, f32[4,32,384]{2,1,0:T(8,128)}, u32[]{:S(2)}) copy-start(f32[4,32,384]{2,1,0:T(8,128)} %param.16) | copy-start | bytes 589828
  77.6 37.5 %copy-start.6 = (bf16[4,32,384]{2,1,0:T(8,128)(2,1)S(1)}, bf16[4,32,384]{2,1,0:T(8,128)(2,1)}, u32[]{:S(2)}) copy-start(bf16[4,32,384]{2,1,0:T(8,128)(2,1)} %img_hbm.1) | copy-start | bytes 294916
  103.1 12.0 %all-to-all-start.6 = ((bf16[8,40,128]{2,1,0:T(8,128)(2,1)}), bf16[8,40,128]{2,1,0:T(8,128)(2,1)S(1)}, u32[]{:S(2)}, u32[]{:S(2)}) async-start(bf16[8,40,128]{2,1,0:T(8,128)(2,1)} %shard_map.141), calls=%async_computation.6 | async-start | bytes 163840 | tf_op jit(solution)/shard_map/all_to_all | solution.py:42

commit v11 on v10

--- a/solution.py
+++ b/solution.py
@@ -55,16 +55,32 @@
     return jnp.where(row == 0, high, jnp.where(row == 1, middle, jnp.where(row == 2, low, 0.0)))
 
 
-def pack_body(w_hbm, img_hbm, prev_hbm, txt_hbm, out_ref, w_ref, img_ref, prev_ref, txt_ref, sems):
+def pack_body(
+    w_hbm, img_hbm, prev_hbm, txt_hbm, flag_hbm, out_ref, tail_hbm,
+    w_ref, img_ref, prev_ref, txt_ref, flag_ref, tail_ref, sems,
+):
     copies = [
         pltpu.make_async_copy(source, target, sems.at[i])
         for i, (source, target) in enumerate(
-            ((w_hbm, w_ref), (img_hbm, img_ref), (prev_hbm, prev_ref), (txt_hbm, txt_ref))
+            (
+                (flag_hbm, flag_ref),
+                (w_hbm, w_ref),
+                (img_hbm, img_ref),
+                (prev_hbm, prev_ref),
+                (txt_hbm, txt_ref),
+            )
         )
     ]
     for copy in copies:
         copy.start()
-    for copy in copies:
+    copies[0].wait()
+    tail_no = jnp.int32(-1)
+    for b in range(img_ref.shape[0]):
+        tail_no = tail_no + jnp.where(flag_ref[b] == 1, 1, 0)
+    tail_ref[0] = tail_no
+    tell = pltpu.make_async_copy(tail_ref, tail_hbm, sems.at[len(copies)])
+    tell.start()
+    for copy in copies[1:]:
         copy.wait()
     kinds, deep, columns = w_ref.shape
     batch, img_rows, width = img_ref.shape
@@ -85,6 +101,7 @@
             text = txt_ref[b].astype(F32)[c * txt_half : (c + 1) * txt_half]
             text = jnp.concatenate([text, jnp.zeros((8 - txt_half, width), F32)], axis=0)
             out_ref[to, at : at + 8] = text.astype(BF16)
+    tell.wait()
 
 
 def spread_body(got_ref, out_hbm, block_ref, sems):
@@ -102,13 +119,8 @@
         copy.wait()
 
 
-def join_body(
-    deep, img_half, txt_half, far_ref, flag_ref, got_ref, mod_ref, out_ref, prev_ref, tail_ref
-):
-    tail_no = jnp.int32(-1)
-    for b in range(mod_ref.shape[1]):
-        tail_no = tail_no + jnp.where(flag_ref[b] == 1, 1, 0)
-    tail_ref[0] = tail_no
+def join_body(deep, img_half, txt_half, got_ref, mod_ref, out_ref, prev_ref):
+    far = lax.axis_index(FAR)
     sources = got_ref.shape[0]
     width = got_ref.shape[2]
     for source in range(sources):
@@ -124,33 +136,32 @@
     for which in range(2):
         chosen = mod_ref[which, 0:1].astype(F32)
         for b in range(1, mod_ref.shape[1]):
-            chosen = jnp.where(far_ref[0] == b, mod_ref[which, b : b + 1].astype(F32), chosen)
+            chosen = jnp.where(far == b, mod_ref[which, b : b + 1].astype(F32), chosen)
         vectors.append(chosen)
     tail = jnp.concatenate(texts + vectors + [jnp.zeros((6, width), F32)], axis=0)
     out_ref[sources * img_half :] = tail.astype(BF16)
 
 
-def norm_body(place_ref, x_ref, prev_ref, mod_ref):
+def norm_body(x_ref, prev_ref, mod_ref):
     groups, rows, width = x_ref.shape
     vectors = rows - 8
     features = groups * width
-    sums = jnp.zeros((rows, 1), F32)
-    for g in range(groups):
-        sums = sums + jnp.sum(x_ref[g].astype(F32), axis=1, keepdims=True)
-    center = sums / features
-    squares = jnp.zeros((rows, 1), F32)
-    for g in range(groups):
-        squares = squares + jnp.sum(
-            jnp.square(x_ref[g].astype(F32) - center), axis=1, keepdims=True
-        )
+    sums = x_ref[0].astype(F32)
+    for g in range(1, groups):
+        sums = sums + x_ref[g].astype(F32)
+    center = jnp.sum(sums, axis=1, keepdims=True) / features
+    squares = jnp.square(x_ref[0].astype(F32) - center)
+    for g in range(1, groups):
+        squares = squares + jnp.square(x_ref[g].astype(F32) - center)
+    squares = jnp.sum(squares, axis=1, keepdims=True)
     inv = lax.rsqrt(squares / features + EPS)
     for g in range(groups):
         values = x_ref[g].astype(F32)
         shift = values[vectors : vectors + 1]
         scale = values[vectors + 1 : vectors + 2]
         mod_ref[g] = ((values - center) * inv * (1.0 + scale) + shift).astype(BF16)
-    far = place_ref[0]
-    own = mod_ref.at[place_ref[1]]
+    far = lax.axis_index(FAR)
+    own = mod_ref.at[lax.axis_index(TP)]
     previous = prev_ref[...].astype(F32)
     numer = jnp.abs(own[: prev_ref.shape[0]].astype(F32) - previous)
     denom = jnp.abs(previous)
@@ -160,7 +171,7 @@
     mod_ref[0, vectors:] = stacked_parts(line, 8).astype(BF16)
 
 
-def project_body(core_ref, own_ref, other_ref, w_ref, gain_ref, query_ref, pair_ref):
+def project_body(own_ref, other_ref, w_ref, gain_ref, query_ref, pair_ref):
     groups, rows, width = own_ref.shape
     _, sources, deep, columns = w_ref.shape
     near = cores = 2
@@ -183,7 +194,7 @@
     for kind in range(2):
         part = total[:, kind * HD : (kind + 1) * HD]
         gain = jnp.where(
-            core_ref[0] == 0, gain_ref[kind : kind + 1, :HD], gain_ref[kind : kind + 1, HD:]
+            lax.axis_index(CORE) == 0, gain_ref[kind : kind + 1, :HD], gain_ref[kind : kind + 1, HD:]
         )
         mean = jnp.mean(jnp.square(part), axis=1, keepdims=True)
         parts.append(part * lax.rsqrt(mean + EPS) * gain)
@@ -201,13 +212,13 @@
             pair_ref[copy, half, :, HD:] = valued[at : at + rows]
 
 
-def attend_body(img_half, txt_half, limit_ref, place_ref, query_ref, pair_ref, out_ref):
+def attend_body(img_half, txt_half, limit_ref, query_ref, pair_ref, out_ref):
     blocks, halves, rows, _ = pair_ref.shape
     sources = out_ref.shape[0]
     img = sources * img_half
     txt = sources * txt_half
     count = blocks * rows
-    far, core = place_ref[0], place_ref[2]
+    far, core = lax.axis_index(FAR), lax.axis_index(CORE)
     query = query_ref[...].reshape(2 * img, HD)
     index = lax.broadcasted_iota(jnp.int32, (1, count), 1)
     slot = index % rows
@@ -321,19 +332,20 @@
     around = xs * nears
     img_half, txt_half = img_rows // cores, txt.shape[1] // cores
     rows = sources * (img_half + txt_half) + 8
-    place = jnp.stack([lax.axis_index(a) for a in (FAR, TP, CORE)]).astype(jnp.int32)
-    core_index = lax.axis_index(CORE).astype(jnp.int32)[None]
-    far_index = lax.axis_index(FAR).astype(jnp.int32)[None]
-
     arrays = (w_qkv.transpose(1, 0, 2), img, prev_mod, txt)
-    got = call(
+    smem = lambda *shape: pltpu.SMEM(shape, jnp.int32)
+    got, tail_no = call(
         pack_body,
-        shaped(sources, deep + 2 * img_half + 8, width),
-        [HBM] * 4,
+        (
+            shaped(sources, deep + 2 * img_half + 8, width),
+            pltpu.HBM((1,), jnp.int32),
+        ),
+        [HBM] * 5,
         8,
+        outs=(VMEM, HBM),
         scratch=[pltpu.VMEM(a.shape, a.dtype) for a in arrays]
-        + [pltpu.SemaphoreType.DMA((len(arrays),))],
-    )(*(pltpu.with_memory_space_constraint(a, pltpu.HBM) for a in arrays))
+        + [smem(batch), smem(1), pltpu.SemaphoreType.DMA((len(arrays) + 2,))],
+    )(*(pltpu.with_memory_space_constraint(a, pltpu.HBM) for a in arrays + (refresh,)))
     got = swap(got, (FAR, CORE))
     weight = call(
         spread_body,
@@ -348,34 +360,29 @@
     )(got)
     weight = swap(weight, (X, NEAR)).reshape(around, sources, deep, kinds * HD)
 
-    joined, previous, tail_no = call(
+    joined, previous = call(
         functools.partial(join_body, deep, img_half, txt_half),
-        (
-            shaped(rows, width),
-            shaped(sources * img_half, width),
-            shaped(1, dtype=jnp.int32),
-        ),
-        [SMEM, SMEM, VMEM, VMEM],
+        (shaped(rows, width), shaped(sources * img_half, width)),
+        [VMEM] * 2,
         8,
-        outs=(VMEM, VMEM, SMEM),
-    )(far_index, refresh, got, modulation)
+    )(got, modulation)
     wide = lax.all_gather(joined, TP, axis=0, tiled=False)
-    own = call(norm_body, shaped(tps, rows, width), [SMEM, VMEM, VMEM], 12)(place, wide, previous)
+    own = call(norm_body, shaped(tps, rows, width), [VMEM] * 2, 12)(wide, previous)
     other = lax.ppermute(own, CORE, [(0, 1), (1, 0)])
 
     query, pairs = call(
         project_body,
         (shaped(2, sources * img_half, HD), shaped(around, 2, rows, 2 * HD)),
-        [SMEM] + [VMEM] * 4,
+        [VMEM] * 4,
         16,
-    )(core_index, own, other, weight, qk_gain)
+    )(own, other, weight, qk_gain)
     pairs = swap(pairs, (X, NEAR))
     attended = call(
         functools.partial(attend_body, img_half, txt_half),
         shaped(sources, img_rows + 8, HD),
-        [SMEM, SMEM, VMEM, VMEM],
+        [SMEM, VMEM, VMEM],
         24,
-    )(text_len, place, query, pairs)
+    )(text_len, query, pairs)
     attended = swap(attended, (FAR, CORE))
 
     tails = [functools.partial(finish, slots) for slots in range(1, batch)]

time: 133 us -> 131 us (0.985)
  Pallas kernels: 12.2 us -> 10.5 us
  transfers between devices with their start and end apart: 3 -> 3, of which waited for: 2 -> 2; matrix products, arithmetic and copies ran while one was open for 0% -> 0% of each run, Pallas kernels for 2% -> 1%
where the time goes in v11:
time: 131 us
  blocking collectives  94.9 us (72%)
  starting transfers between devices  11 us (8%)
  Pallas kernels  10.5 us (8%)
  waiting for transfers between devices  10.5 us (8%)
  local copies, waits for them, and re-layouts  2.18 us (2%)
  between operations  1.4 us (1%)
    all_to_all x3, blocking collectives, swap(): return lax.all_to_all(value, axis, 0, 0, tiled=True)  62.2 us
    all_gather x1, blocking collectives, local(): wide = lax.all_gather(joined, TP, axis=0, tiled=False)  32.8 us
    all_to_all x2, starting transfers between devices, swap(): return lax.all_to_all(value, axis, 0, 0, tiled=True)  9.07 us
    all_to_all x2, waiting for transfers between devices, swap(): return lax.all_to_all(value, axis, 0, 0, tiled=True)  7.99 us
    pallas_call x1, Pallas kernels, local(): call(functools.partial(attend_body, img_half, txt_half), shaped(sources,...  2.86 us
  transfers between devices with their start and end apart: 3, of which 2 were waited for; matrix products, arithmetic and copies ran while one was open for 0% of the time, Pallas kernels for 1%

profile of v11, /device:TPU:8, one launch (start us, length us, event | category | flops | bytes accessed | tf_op | source)
XLA Modules:
  0.0 130.5 jit_solution(12883154075808735645)
XLA Ops:
  0.6 1.2 shard_map.136
  1.9 24.7 %all_to_all.35.got_ref = bf16[8,88,384]{2,1,0:T(8,128)(2,1)S(1)} all-to-all(bf16[8,88,384]{2,1,0:T(8,128)(2,1)S(1)} %get-tuple-element.64), channel_id=1, replica_groups=mesh['seq_0'=4,'seq_1a'=4,'seq_1b'=2,'seq_2'=2,'tp'=8] {'seq_1a','seq_2'}, dimensions={0} | all-to-all | bytes 1081344 | tf_op jit(solution)/shard_map/all_to_all | solution.py:42
  26.6 1.5 %shard_map.139 = bf16[8,384,384]{2,1,0:T(8,128)(2,1)} custom-call(bf16[8,88,384]{2,1,0:T(8,128)(2,1)S(1)} %all_to_all.35.got_ref), custom_call_target="tpu_custom_call" | custom-call | tf_op jit(solution)/shard_map/pallas_call | solution.py:350
  28.1 0.0 copy-start.7
  28.1 5.7 %all-to-all-start.4 = ((bf16[8,384,384]{2,1,0:T(8,128)(2,1)}), bf16[8,384,384]{2,1,0:T(8,128)(2,1)S(1)}, u32[]{:S(2)}, u32[]{:S(2)}) async-start(bf16[8,384,384]{2,1,0:T(8,128)(2,1)} %shard_map.139), calls=%async_computation.4 | async-start | bytes 4718592 | tf_op jit(solution)/shard_map/all_to_all | solution.py:42
  33.8 0.0 copy-done.7
  33.9 0.0 copy-start.2
  33.9 32.8 %all-gather = bf16[1216,384]{1,0:T(8,128)(2,1)S(1)} all-gather(bf16[152,384]{1,0:T(8,128)(2,1)S(1)} %get-tuple-element.65), channel_id=2, replica_groups=mesh['seq_0'=4,'seq_1a'=4,'seq_1b'=2,'seq_2'=2,'tp'=8] {'tp'}, dimensions={0}, use_global_device_ids=true | all-gather | bytes 1050624 | tf_op jit(solution)/shard_map/all_gather | solution.py:369
  66.6 1.1 shard_map.138.own_ref
  67.7 1.9 %collective-permute-start = (bf16[8,152,384]{2,1,0:T(8,128)(2,1)S(1)}, bf16[8,152,384]{2,1,0:T(8,128)(2,1)S(1)}, u32[]{:S(2)}, u32[]{:S(2)}) collective-permute-start(bf16[8,152,384]{2,1,0:T(8,128)(2,1)S(1)} %shard_map.138.own_ref), channel_id=1, source_target_pairs={{0,8},{8,0},{1,9},{9,1},{2,10},{10,2},{3,11},{11,3},{4,12},{12,4},... | collective-permute-start | bytes 2801672 | tf_op jit(solution)/shard_map/ppermute | solution.py:371
  69.6 2.5 %collective-permute-done.other_ref = bf16[8,152,384]{2,1,0:T(8,128)(2,1)S(1)} collective-permute-done((bf16[8,152,384]{2,1,0:T(8,128)(2,1)S(1)}, bf16[8,152,384]{2,1,0:T(8,128)(2,1)S(1)}, u32[]{:S(2)}, u32[]{:S(2)}) %collective-permute-start) | collective-permute-done | bytes 933920 | tf_op jit(solution)/shard_map/ppermute | solution.py:371
  72.1 0.0 copy-start
  72.1 0.9 copy-done
  73.1 0.0 all-to-all-done.4
  73.1 0.0 copy-done.2
  73.1 0.0 copy-start.1
  73.1 1.2 copy-done.1
  74.2 1.5 %shard_map.140 = (bf16[2,128,128]{2,1,0:T(8,128)(2,1)S(1)}, bf16[8,2,152,256]{3,2,1,0:T(8,128)(2,1)S(1)}) custom-call(bf16[8,152,384]{2,1,0:T(8,128)(2,1)S(1)} %shard_map.138.own_ref, bf16[8,152,384]{2,1,0:T(8,128)(2,1)S(1)} %copy-done.1, bf16[8,8,48,384]{3,2,1,0:T(8,128)(2,1)S(1)} %bitcast.4, f32[2,256]{1,0:T(2,128)S(1)} %copy-done.2), custom_call_target="tpu_custom_call" | custom-call | tf_op jit(solution)/shard_map/pallas_call | solution.py:373
  75.8 0.0 copy-start.3
  75.8 0.0 copy-start.4
  75.8 0.0 copy-start.5
  75.8 0.0 copy-start.6
  75.9 0.0 copy-start.8
  75.9 22.8 %all_to_all.36.pair_ref = bf16[8,2,152,256]{3,2,1,0:T(8,128)(2,1)S(1)} all-to-all(bf16[8,2,152,256]{3,2,1,0:T(8,128)(2,1)S(1)} %get-tuple-element.68), channel_id=1, replica_groups=mesh['seq_0'=4,'seq_1a'=4,'seq_1b'=2,'seq_2'=2,'tp'=8] {'seq_0','seq_1b'}, dimensions={0} | all-to-all | bytes 2490368 | tf_op jit(solution)/shard_map/all_to_all | solution.py:42
  98.7 0.0 copy-done.3
  98.7 2.9 %shard_map.141 = bf16[8,40,128]{2,1,0:T(8,128)(2,1)} custom-call(s32[4]{0:T(128)S(1)} %copy-done.3, bf16[2,128,128]{2,1,0:T(8,128)(2,1)S(1)} %get-tuple-element.67.query_ref, bf16[8,2,152,256]{3,2,1,0:T(8,128)(2,1)S(1)} %all_to_all.36.pair_ref), custom_call_target="tpu_custom_call" | custom-call | tf_op jit(solution)/shard_map/pallas_call | solution.py:380
  101.5 3.4 %all-to-all-start.6 = ((bf16[8,40,128]{2,1,0:T(8,128)(2,1)}), bf16[8,40,128]{2,1,0:T(8,128)(2,1)S(1)}, u32[]{:S(2)}, u32[]{:S(2)}) async-start(bf16[8,40,128]{2,1,0:T(8,128)(2,1)} %shard_map.141), calls=%async_computation.6 | async-start | bytes 163840 | tf_op jit(solution)/shard_map/all_to_all | solution.py:42
  105.6 8.0 %all-to-all-done.6 = bf16[8,40,128]{2,1,0:T(8,128)(2,1)S(1)} async-done(((bf16[8,40,128]{2,1,0:T(8,128)(2,1)}), bf16[8,40,128]{2,1,0:T(8,128)(2,1)S(1)}, u32[]{:S(2)}, u32[]{:S(2)}) %all-to-all-start.6) | async-done | bytes 81952 | tf_op jit(solution)/shard_map/all_to_all | solution.py:42
  113.5 0.0 copy-done.4
  113.5 0.0 copy-done.5
  113.5 0.0 copy-done.6
  113.6 0.0 copy-done.8
  113.6 17.0 %conditional.1 = ((f32[4,32,384]{2,1,0:T(8,128)}, f32[4,32,384]{2,1,0:T(8,128)}, f32[4]{0:T(128)})) conditional(s32[]{:T(128)} %bitcast.1, (s32[4]{0:T(128)S(1)}, bf16[8,40,128]{2,1,0:T(8,128)(2,1)S(1)}, bf16[256,3072]{1,0:T(8,128)(2,1)S(1)}, f32[4,32,384]{2,1,0:T(8,128)S(1)}, bf16[4,32,384]{2,1,0:T(8,128)(2,1)S(1)}, ...), branch_computations={%region_0.0_spmd, %region_1.0_spmd, %region_2.0_spmd} | conditional | bytes 1277960 | solution.py:389
  113.6 0.9 branch_0_fun.2
  114.4 14.7 %all_to_all.32.part_ref = bf16[8,40,384]{2,1,0:T(8,128)(2,1)S(1)} all-to-all(bf16[8,40,384]{2,1,0:T(8,128)(2,1)S(1)} %branch_0_fun.2), channel_id=1, replica_groups=mesh['seq_0'=4,'seq_1a'=4,'seq_1b'=2,'seq_2'=2,'tp'=8] {'tp'}, dimensions={0} | all-to-all | bytes 491520 | tf_op jit(solution)/shard_map/cond/branch_0_fun/all_to_all | solution.py:42
  129.1 1.4 %branch_0_fun.3 = (f32[4,32,384]{2,1,0:T(8,128)}, f32[4,32,384]{2,1,0:T(8,128)}, f32[4]{0:T(128)}) custom-call(s32[4]{0:T(128)S(1)} %get-tuple-element.36.flag_ref, bf16[8,40,384]{2,1,0:T(8,128)(2,1)S(1)} %all_to_all.32.part_ref, f32[4,32,384]{2,1,0:T(8,128)S(1)} %get-tuple-element.90.cache_ref, bf16[4,32,384]{2,1,0:T(8,128)(2,1)S(1)} %get-tuple-element.40.img_ref, ...), custom_call_target="tpu_custom_call" | custom-call | tf_op jit(solution)/shard_map/cond/branch_0_fun/pallas_call | solution.py:403
  (1 shorter events, 0.0 us)
Async XLA Ops:
  28.1 5.7 %copy-start.7 = (bf16[3,4,384]{2,1,0:T(4,128)(2,1)S(1)}, bf16[3,4,384]{2,1,0:T(4,128)(2,1)}, u32[]{:S(2)}) copy-start(bf16[3,4,384]{2,1,0:T(4,128)(2,1)} %mod_ref.1) | copy-start | bytes 27652
  28.1 45.0 %all-to-all-start.4 = ((bf16[8,384,384]{2,1,0:T(8,128)(2,1)}), bf16[8,384,384]{2,1,0:T(8,128)(2,1)S(1)}, u32[]{:S(2)}, u32[]{:S(2)}) async-start(bf16[8,384,384]{2,1,0:T(8,128)(2,1)} %shard_map.139), calls=%async_computation.4 | async-start | bytes 4718592 | tf_op jit(solution)/shard_map/all_to_all | solution.py:42
  33.9 39.2 %copy-start.2 = (f32[2,256]{1,0:T(2,128)S(1)}, f32[2,256]{1,0:T(2,128)}, u32[]{:S(2)}) copy-start(f32[2,256]{1,0:T(2,128)} %gain_ref.1) | copy-start | bytes 6148
  67.7 4.4 %collective-permute-start = (bf16[8,152,384]{2,1,0:T(8,128)(2,1)S(1)}, bf16[8,152,384]{2,1,0:T(8,128)(2,1)S(1)}, u32[]{:S(2)}, u32[]{:S(2)}) collective-permute-start(bf16[8,152,384]{2,1,0:T(8,128)(2,1)S(1)} %shard_map.138.own_ref), channel_id=1, source_target_pairs={{0,8},{8,0},{1,9},{9,1},{2,10},{10,2},{3,11},{11,3},{4,12},{12,4},... | collective-permute-start | bytes 2801672 | tf_op jit(solution)/shard_map/ppermute | solution.py:371
  72.1 0.9 copy-start
  73.1 1.2 copy-start.1
  75.8 22.9 %copy-start.3 = (s32[4]{0:T(128)S(1)}, s32[4]{0:T(128)}, u32[]{:S(2)}) copy-start(s32[4]{0:T(128)} %limit_ref.1) | copy-start | bytes 52
  75.8 37.7 %copy-start.4 = (bf16[256,3072]{1,0:T(8,128)(2,1)S(1)}, bf16[256,3072]{1,0:T(8,128)(2,1)}, u32[]{:S(2)}) copy-start(bf16[256,3072]{1,0:T(8,128)(2,1)} %param.20) | copy-start | bytes 4718596
  75.8 37.7 %copy-start.5 = (f32[4,32,384]{2,1,0:T(8,128)S(1)}, f32[4,32,384]{2,1,0:T(8,128)}, u32[]{:S(2)}) copy-start(f32[4,32,384]{2,1,0:T(8,128)} %param.16) | copy-start | bytes 589828
  75.8 37.7 %copy-start.6 = (bf16[4,32,384]{2,1,0:T(8,128)(2,1)S(1)}, bf16[4,32,384]{2,1,0:T(8,128)(2,1)}, u32[]{:S(2)}) copy-start(bf16[4,32,384]{2,1,0:T(8,128)(2,1)} %img_hbm.1) | copy-start | bytes 294916
  75.9 37.7 %copy-start.8 = (s32[4]{0:T(128)S(1)}, s32[4]{0:T(128)}, u32[]{:S(2)}) copy-start(s32[4]{0:T(128)} %flag_hbm.1) | copy-start | bytes 52
  101.5 12.0 %all-to-all-start.6 = ((bf16[8,40,128]{2,1,0:T(8,128)(2,1)}), bf16[8,40,128]{2,1,0:T(8,128)(2,1)S(1)}, u32[]{:S(2)}, u32[]{:S(2)}) async-start(bf16[8,40,128]{2,1,0:T(8,128)(2,1)} %shard_map.141), calls=%async_computation.6 | async-start | bytes 163840 | tf_op jit(solution)/shard_map/all_to_all | solution.py:42

commit v12 on v11

--- a/solution.py
+++ b/solution.py
@@ -175,6 +175,7 @@
     groups, rows, width = own_ref.shape
     _, sources, deep, columns = w_ref.shape
     near = cores = 2
+    xs = w_ref.shape[0] // near
     ys = near * sources // cores
     per_group = width // deep
     total = jnp.zeros((2 * rows, columns), F32)
@@ -185,7 +186,7 @@
             core = flat % cores
             y = flat // cores % ys
             x = flat // cores // ys
-            pieces.append(w_ref[x * near + y % near, y // near * cores + core])
+            pieces.append(w_ref[y % near * xs + x, y // near * cores + core])
         left = jnp.concatenate([own_ref[g], other_ref[g]], axis=0)
         total = total + jnp.dot(
             left, jnp.concatenate(pieces, axis=0), preferred_element_type=F32
@@ -224,8 +225,8 @@
     slot = index % rows
     block = index // rows
     source = (slot - img) // txt_half
-    y = source // 2 * 2 + block % 2
-    device = (block // 2 * 8 + y) * 2 + source % 2
+    y = source // 2 * 2 + block // 4
+    device = (block % 4 * 8 + y) * 2 + source % 2
     scores_of, valid_of = [], []
     rel = jnp.zeros((1, HD), F32)
     for half in range(halves):
@@ -358,7 +359,7 @@
             pltpu.SemaphoreType.DMA((around,)),
         ],
     )(got)
-    weight = swap(weight, (X, NEAR)).reshape(around, sources, deep, kinds * HD)
+    weight = swap(weight, (NEAR, X)).reshape(around, sources, deep, kinds * HD)
 
     joined, previous = call(
         functools.partial(join_body, deep, img_half, txt_half),
@@ -376,7 +377,7 @@
         [VMEM] * 4,
         16,
     )(own, other, weight, qk_gain)
-    pairs = swap(pairs, (X, NEAR))
+    pairs = swap(pairs, (NEAR, X))
     attended = call(
         functools.partial(attend_body, img_half, txt_half),
         shaped(sources, img_rows + 8, HD),

time: 131 us -> 131 us (level)
  no operation moved by 1% of the time
where the time goes in v12:
time: 131 us
  blocking collectives  94.8 us (72%)
  starting transfers between devices  11 us (8%)
  Pallas kernels  10.6 us (8%)
  waiting for transfers between devices  10.6 us (8%)
  local copies, waits for them, and re-layouts  2.18 us (2%)
  between operations  1.4 us (1%)
    all_to_all x3, blocking collectives, swap(): return lax.all_to_all(value, axis, 0, 0, tiled=True)  62 us
    all_gather x1, blocking collectives, local(): wide = lax.all_gather(joined, TP, axis=0, tiled=False)  32.8 us
    all_to_all x2, starting transfers between devices, swap(): return lax.all_to_all(value, axis, 0, 0, tiled=True)  9.07 us
    all_to_all x2, waiting for transfers between devices, swap(): return lax.all_to_all(value, axis, 0, 0, tiled=True)  8.13 us
    pallas_call x1, Pallas kernels, local(): call(functools.partial(attend_body, img_half, txt_half), shaped(sources,...  2.87 us
  transfers between devices with their start and end apart: 3, of which 2 were waited for; matrix products, arithmetic and copies ran while one was open for 0% of the time, Pallas kernels for 1%

profile of v12, /device:TPU:8, one launch (start us, length us, event | category | flops | bytes accessed | tf_op | source)
XLA Modules:
  0.0 130.5 jit_solution(2965585099939661318)
XLA Ops:
  0.6 1.2 shard_map.136
  1.9 24.7 %all_to_all.35.got_ref = bf16[8,88,384]{2,1,0:T(8,128)(2,1)S(1)} all-to-all(bf16[8,88,384]{2,1,0:T(8,128)(2,1)S(1)} %get-tuple-element.64), channel_id=1, replica_groups=mesh['seq_0'=4,'seq_1a'=4,'seq_1b'=2,'seq_2'=2,'tp'=8] {'seq_1a','seq_2'}, dimensions={0} | all-to-all | bytes 1081344 | tf_op jit(solution)/shard_map/all_to_all | solution.py:42
  26.6 1.5 %shard_map.139 = bf16[8,384,384]{2,1,0:T(8,128)(2,1)} custom-call(bf16[8,88,384]{2,1,0:T(8,128)(2,1)S(1)} %all_to_all.35.got_ref), custom_call_target="tpu_custom_call" | custom-call | tf_op jit(solution)/shard_map/pallas_call | solution.py:351
  28.1 0.0 copy-start.7
  28.1 5.7 %all-to-all-start.4 = ((bf16[8,384,384]{2,1,0:T(8,128)(2,1)}), bf16[8,384,384]{2,1,0:T(8,128)(2,1)S(1)}, u32[]{:S(2)}, u32[]{:S(2)}) async-start(bf16[8,384,384]{2,1,0:T(8,128)(2,1)} %shard_map.139), calls=%async_computation.4 | async-start | bytes 4718592 | tf_op jit(solution)/shard_map/all_to_all | solution.py:42
  33.8 0.0 copy-done.7
  33.9 0.0 copy-start.2
  33.9 32.8 %all-gather = bf16[1216,384]{1,0:T(8,128)(2,1)S(1)} all-gather(bf16[152,384]{1,0:T(8,128)(2,1)S(1)} %get-tuple-element.65), channel_id=2, replica_groups=mesh['seq_0'=4,'seq_1a'=4,'seq_1b'=2,'seq_2'=2,'tp'=8] {'tp'}, dimensions={0}, use_global_device_ids=true | all-gather | bytes 1050624 | tf_op jit(solution)/shard_map/all_gather | solution.py:370
  66.6 1.1 shard_map.138.own_ref
  67.7 1.9 %collective-permute-start = (bf16[8,152,384]{2,1,0:T(8,128)(2,1)S(1)}, bf16[8,152,384]{2,1,0:T(8,128)(2,1)S(1)}, u32[]{:S(2)}, u32[]{:S(2)}) collective-permute-start(bf16[8,152,384]{2,1,0:T(8,128)(2,1)S(1)} %shard_map.138.own_ref), channel_id=1, source_target_pairs={{0,8},{8,0},{1,9},{9,1},{2,10},{10,2},{3,11},{11,3},{4,12},{12,4},... | collective-permute-start | bytes 2801672 | tf_op jit(solution)/shard_map/ppermute | solution.py:372
  69.6 2.5 %collective-permute-done.other_ref = bf16[8,152,384]{2,1,0:T(8,128)(2,1)S(1)} collective-permute-done((bf16[8,152,384]{2,1,0:T(8,128)(2,1)S(1)}, bf16[8,152,384]{2,1,0:T(8,128)(2,1)S(1)}, u32[]{:S(2)}, u32[]{:S(2)}) %collective-permute-start) | collective-permute-done | bytes 933920 | tf_op jit(solution)/shard_map/ppermute | solution.py:372
  72.1 0.0 copy-start
  72.1 0.9 copy-done
  73.1 0.0 all-to-all-done.4
  73.1 0.0 copy-done.2
  73.1 0.0 copy-start.1
  73.1 1.2 copy-done.1
  74.2 1.5 %shard_map.140 = (bf16[2,128,128]{2,1,0:T(8,128)(2,1)S(1)}, bf16[8,2,152,256]{3,2,1,0:T(8,128)(2,1)S(1)}) custom-call(bf16[8,152,384]{2,1,0:T(8,128)(2,1)S(1)} %shard_map.138.own_ref, bf16[8,152,384]{2,1,0:T(8,128)(2,1)S(1)} %copy-done.1, bf16[8,8,48,384]{3,2,1,0:T(8,128)(2,1)S(1)} %bitcast.4, f32[2,256]{1,0:T(2,128)S(1)} %copy-done.2), custom_call_target="tpu_custom_call" | custom-call | tf_op jit(solution)/shard_map/pallas_call | solution.py:374
  75.8 0.0 copy-start.3
  75.8 0.0 copy-start.4
  75.8 0.0 copy-start.5
  75.8 0.0 copy-start.6
  75.9 0.0 copy-start.8
  75.9 22.5 %all_to_all.36.pair_ref = bf16[8,2,152,256]{3,2,1,0:T(8,128)(2,1)S(1)} all-to-all(bf16[8,2,152,256]{3,2,1,0:T(8,128)(2,1)S(1)} %get-tuple-element.68), channel_id=1, replica_groups=mesh['seq_0'=4,'seq_1a'=4,'seq_1b'=2,'seq_2'=2,'tp'=8] {'seq_1b','seq_0'}, dimensions={0} | all-to-all | bytes 2490368 | tf_op jit(solution)/shard_map/all_to_all | solution.py:42
  98.4 0.0 copy-done.3
  98.4 2.9 %shard_map.141 = bf16[8,40,128]{2,1,0:T(8,128)(2,1)} custom-call(s32[4]{0:T(128)S(1)} %copy-done.3, bf16[2,128,128]{2,1,0:T(8,128)(2,1)S(1)} %get-tuple-element.67.query_ref, bf16[8,2,152,256]{3,2,1,0:T(8,128)(2,1)S(1)} %all_to_all.36.pair_ref), custom_call_target="tpu_custom_call" | custom-call | tf_op jit(solution)/shard_map/pallas_call | solution.py:381
  101.3 3.4 %all-to-all-start.6 = ((bf16[8,40,128]{2,1,0:T(8,128)(2,1)}), bf16[8,40,128]{2,1,0:T(8,128)(2,1)S(1)}, u32[]{:S(2)}, u32[]{:S(2)}) async-start(bf16[8,40,128]{2,1,0:T(8,128)(2,1)} %shard_map.141), calls=%async_computation.6 | async-start | bytes 163840 | tf_op jit(solution)/shard_map/all_to_all | solution.py:42
  105.3 8.1 %all-to-all-done.6 = bf16[8,40,128]{2,1,0:T(8,128)(2,1)S(1)} async-done(((bf16[8,40,128]{2,1,0:T(8,128)(2,1)}), bf16[8,40,128]{2,1,0:T(8,128)(2,1)S(1)}, u32[]{:S(2)}, u32[]{:S(2)}) %all-to-all-start.6) | async-done | bytes 81952 | tf_op jit(solution)/shard_map/all_to_all | solution.py:42
  113.4 0.0 copy-done.4
  113.4 0.0 copy-done.5
  113.4 0.0 copy-done.6
  113.4 0.0 copy-done.8
  113.4 17.1 %conditional.1 = ((f32[4,32,384]{2,1,0:T(8,128)}, f32[4,32,384]{2,1,0:T(8,128)}, f32[4]{0:T(128)})) conditional(s32[]{:T(128)} %bitcast.1, (s32[4]{0:T(128)S(1)}, bf16[8,40,128]{2,1,0:T(8,128)(2,1)S(1)}, bf16[256,3072]{1,0:T(8,128)(2,1)S(1)}, f32[4,32,384]{2,1,0:T(8,128)S(1)}, bf16[4,32,384]{2,1,0:T(8,128)(2,1)S(1)}, ...), branch_computations={%region_0.0_spmd, %region_1.0_spmd, %region_2.0_spmd} | conditional | bytes 1277960 | solution.py:390
  113.4 0.9 branch_0_fun.2
  114.3 14.8 %all_to_all.32.part_ref = bf16[8,40,384]{2,1,0:T(8,128)(2,1)S(1)} all-to-all(bf16[8,40,384]{2,1,0:T(8,128)(2,1)S(1)} %branch_0_fun.2), channel_id=1, replica_groups=mesh['seq_0'=4,'seq_1a'=4,'seq_1b'=2,'seq_2'=2,'tp'=8] {'tp'}, dimensions={0} | all-to-all | bytes 491520 | tf_op jit(solution)/shard_map/cond/branch_0_fun/all_to_all | solution.py:42
  129.1 1.4 %branch_0_fun.3 = (f32[4,32,384]{2,1,0:T(8,128)}, f32[4,32,384]{2,1,0:T(8,128)}, f32[4]{0:T(128)}) custom-call(s32[4]{0:T(128)S(1)} %get-tuple-element.36.flag_ref, bf16[8,40,384]{2,1,0:T(8,128)(2,1)S(1)} %all_to_all.32.part_ref, f32[4,32,384]{2,1,0:T(8,128)S(1)} %get-tuple-element.90.cache_ref, bf16[4,32,384]{2,1,0:T(8,128)(2,1)S(1)} %get-tuple-element.40.img_ref, ...), custom_call_target="tpu_custom_call" | custom-call | tf_op jit(solution)/shard_map/cond/branch_0_fun/pallas_call | solution.py:404
  (1 shorter events, 0.0 us)
Async XLA Ops:
  28.1 5.7 %copy-start.7 = (bf16[3,4,384]{2,1,0:T(4,128)(2,1)S(1)}, bf16[3,4,384]{2,1,0:T(4,128)(2,1)}, u32[]{:S(2)}) copy-start(bf16[3,4,384]{2,1,0:T(4,128)(2,1)} %mod_ref.1) | copy-start | bytes 27652
  28.1 45.0 %all-to-all-start.4 = ((bf16[8,384,384]{2,1,0:T(8,128)(2,1)}), bf16[8,384,384]{2,1,0:T(8,128)(2,1)S(1)}, u32[]{:S(2)}, u32[]{:S(2)}) async-start(bf16[8,384,384]{2,1,0:T(8,128)(2,1)} %shard_map.139), calls=%async_computation.4 | async-start | bytes 4718592 | tf_op jit(solution)/shard_map/all_to_all | solution.py:42
  33.9 39.2 %copy-start.2 = (f32[2,256]{1,0:T(2,128)S(1)}, f32[2,256]{1,0:T(2,128)}, u32[]{:S(2)}) copy-start(f32[2,256]{1,0:T(2,128)} %gain_ref.1) | copy-start | bytes 6148
  67.7 4.4 %collective-permute-start = (bf16[8,152,384]{2,1,0:T(8,128)(2,1)S(1)}, bf16[8,152,384]{2,1,0:T(8,128)(2,1)S(1)}, u32[]{:S(2)}, u32[]{:S(2)}) collective-permute-start(bf16[8,152,384]{2,1,0:T(8,128)(2,1)S(1)} %shard_map.138.own_ref), channel_id=1, source_target_pairs={{0,8},{8,0},{1,9},{9,1},{2,10},{10,2},{3,11},{11,3},{4,12},{12,4},... | collective-permute-start | bytes 2801672 | tf_op jit(solution)/shard_map/ppermute | solution.py:372
  72.1 0.9 copy-start
  73.1 1.2 copy-start.1
  75.8 22.6 %copy-start.3 = (s32[4]{0:T(128)S(1)}, s32[4]{0:T(128)}, u32[]{:S(2)}) copy-start(s32[4]{0:T(128)} %limit_ref.1) | copy-start | bytes 52
  75.8 37.6 %copy-start.4 = (bf16[256,3072]{1,0:T(8,128)(2,1)S(1)}, bf16[256,3072]{1,0:T(8,128)(2,1)}, u32[]{:S(2)}) copy-start(bf16[256,3072]{1,0:T(8,128)(2,1)} %param.20) | copy-start | bytes 4718596
  75.8 37.6 %copy-start.5 = (f32[4,32,384]{2,1,0:T(8,128)S(1)}, f32[4,32,384]{2,1,0:T(8,128)}, u32[]{:S(2)}) copy-start(f32[4,32,384]{2,1,0:T(8,128)} %param.16) | copy-start | bytes 589828
  75.8 37.6 %copy-start.6 = (bf16[4,32,384]{2,1,0:T(8,128)(2,1)S(1)}, bf16[4,32,384]{2,1,0:T(8,128)(2,1)}, u32[]{:S(2)}) copy-start(bf16[4,32,384]{2,1,0:T(8,128)(2,1)} %img_hbm.1) | copy-start | bytes 294916
  75.9 37.6 %copy-start.8 = (s32[4]{0:T(128)S(1)}, s32[4]{0:T(128)}, u32[]{:S(2)}) copy-start(s32[4]{0:T(128)} %flag_hbm.1) | copy-start | bytes 52
  101.3 12.1 %all-to-all-start.6 = ((bf16[8,40,128]{2,1,0:T(8,128)(2,1)}), bf16[8,40,128]{2,1,0:T(8,128)(2,1)S(1)}, u32[]{:S(2)}, u32[]{:S(2)}) async-start(bf16[8,40,128]{2,1,0:T(8,128)(2,1)} %shard_map.141), calls=%async_computation.6 | async-start | bytes 163840 | tf_op jit(solution)/shard_map/all_to_all | solution.py:42

commit v13 on v12

--- a/solution.py
+++ b/solution.py
@@ -1,4 +1,5 @@
 import functools
+import math
 
 import jax
 import jax.numpy as jnp
@@ -227,28 +228,26 @@
     source = (slot - img) // txt_half
     y = source // 2 * 2 + block // 4
     device = (block % 4 * 8 + y) * 2 + source % 2
-    scores_of, valid_of = [], []
+    raw_of = []
     rel = jnp.zeros((1, HD), F32)
     for half in range(halves):
         actual = jnp.where(half == 0, core, 1 - core)
         keys = pair_ref[:, half, :, :HD].reshape(count, HD)
-        scores = lax.dot_general(
+        raw = lax.dot_general(
             query, keys, (((1,), (1,)), ((), ())), preferred_element_type=F32
-        ) * (1.0 / HD**0.5)
+        )
         text = device * 4 + actual * txt_half + (slot - img) % txt_half
         valid = (slot < img) | ((slot < img + txt) & (text < limit_ref[far]))
-        scores_of.append(jnp.where(valid, scores, NEG))
-        valid_of.append(valid)
+        raw_of.append(raw + jnp.where(valid, 0.0, NEG))
         for b in range(blocks):
             carried = pair_ref[b, half, rows - 8 :, :HD].astype(F32)
             rel = rel + jnp.sum(carried, axis=0, keepdims=True)
-    top = functools.reduce(
-        jnp.maximum, [jnp.max(s, axis=1, keepdims=True) for s in scores_of]
-    )
+    factor = math.log2(math.e) / HD**0.5
+    top = functools.reduce(jnp.maximum, [jnp.max(r, axis=1, keepdims=True) for r in raw_of])
     total = jnp.zeros((2 * img, 1), F32)
     summed = jnp.zeros((2 * img, HD), F32)
     for half in range(halves):
-        weights = jnp.where(valid_of[half], jnp.exp(scores_of[half] - top), 0.0)
+        weights = jnp.exp2((raw_of[half] - top) * factor)
         total = total + jnp.sum(weights, axis=1, keepdims=True)
         values = pair_ref[:, half, :, HD:].reshape(count, HD)
         summed = summed + jnp.dot(weights.astype(BF16), values, preferred_element_type=F32)
@@ -300,7 +299,10 @@
         out_ref[g, rows - 8 :] = tail
 
 
-def final_body(flag_ref, part_ref, cache_ref, img_ref, mod_ref, out_ref, new_ref, rel_ref, sum_ref):
+def final_body(
+    flag_ref, part_ref, cache_ref, img_ref, mod_ref, out_hbm, new_hbm, rel_ref,
+    sum_ref, out_ref, new_ref, sems,
+):
     groups, rows, _ = part_ref.shape
     batch, img_rows, _ = img_ref.shape
     slots = (rows - 8) // img_rows
@@ -309,6 +311,7 @@
         mixed = mixed + part_ref[g].astype(F32)
     sum_ref[...] = mixed
     _, slot = slots_of(flag_ref, batch, slots)
+    copies = []
     for b in range(batch):
         gate = mod_ref[2, b : b + 1].astype(F32)
         at = pl.multiple_of(jnp.minimum(slot[b], slots - 1) * img_rows, img_rows)
@@ -316,12 +319,17 @@
         fresh = jnp.where(flag_ref[b] == 1, resid, cache_ref[b])
         new_ref[b] = fresh
         out_ref[b] = img_ref[b].astype(F32) + fresh
+        for i, (source, target) in enumerate(((new_ref, new_hbm), (out_ref, out_hbm))):
+            copies.append(pltpu.make_async_copy(source.at[b], target.at[b], sems.at[i, b]))
+            copies[-1].start()
     sums = jnp.sum(mixed[rows - 8 :, :HD], axis=0, keepdims=True)
     lane = lax.broadcasted_iota(jnp.int32, (1, HD), 1)
     for b in range(batch):
         numer = jnp.sum(jnp.where(lane == b, sums, 0.0))
         denom = jnp.sum(jnp.where(lane == 4 + b, sums, 0.0))
         rel_ref[b] = numer / jnp.maximum(denom, 1.0)
+    for copy in copies:
+        copy.wait()
 
 
 def local(img, txt, prev_mod, cache, modulation, w_qkv, qk_gain, output_weight, text_len, refresh):
@@ -400,14 +408,16 @@
         12,
     )(refresh, attended, output_weight)
     parts = swap(parts, TP)
-    whole = shaped(batch, img_rows, width, dtype=F32)
+    whole = pltpu.HBM((batch, img_rows, width), F32)
     return call(
         final_body,
         (whole, whole, shaped(batch, dtype=F32)),
         [SMEM] + [VMEM] * 4,
         8,
-        outs=(VMEM, VMEM, SMEM),
-        scratch=[pltpu.VMEM((rows, width), F32)],
+        outs=(HBM, HBM, SMEM),
+        scratch=[pltpu.VMEM((rows, width), F32)]
+        + [pltpu.VMEM((batch, img_rows, width), F32)] * 2
+        + [pltpu.SemaphoreType.DMA((2, batch))],
     )(refresh, parts, cache, img, modulation)
 
 

time: 131 us -> 132 us (level)
  no operation moved by 1% of the time
where the time goes in v13:
time: 132 us; the launch traced here: 131 us
  blocking collectives  94.8 us (72%)
  Pallas kernels  11 us (8%)
  starting transfers between devices  11 us (8%)
  waiting for transfers between devices  10.6 us (8%)
  local copies, waits for them, and re-layouts  2.18 us (2%)
  between operations  1.4 us (1%)
    all_to_all x3, blocking collectives, swap(): return lax.all_to_all(value, axis, 0, 0, tiled=True)  62 us
    all_gather x1, blocking collectives, local(): wide = lax.all_gather(joined, TP, axis=0, tiled=False)  32.8 us
    all_to_all x2, starting transfers between devices, swap(): return lax.all_to_all(value, axis, 0, 0, tiled=True)  9.07 us
    all_to_all x2, waiting for transfers between devices, swap(): return lax.all_to_all(value, axis, 0, 0, tiled=True)  8.13 us
    pallas_call x1, Pallas kernels, local(): call(functools.partial(attend_body, img_half, txt_half), shaped(sources,...  2.69 us
  transfers between devices with their start and end apart: 3, of which 2 were waited for; matrix products, arithmetic and copies ran while one was open for 0% of the time, Pallas kernels for 1%

profile of v13, /device:TPU:8, one launch (start us, length us, event | category | flops | bytes accessed | tf_op | source)
XLA Modules:
  0.0 131.0 jit_solution(16188672684559136758)
XLA Ops:
  0.6 1.2 shard_map.136
  1.9 24.7 %all_to_all.35.got_ref = bf16[8,88,384]{2,1,0:T(8,128)(2,1)S(1)} all-to-all(bf16[8,88,384]{2,1,0:T(8,128)(2,1)S(1)} %get-tuple-element.64), channel_id=1, replica_groups=mesh['seq_0'=4,'seq_1a'=4,'seq_1b'=2,'seq_2'=2,'tp'=8] {'seq_1a','seq_2'}, dimensions={0} | all-to-all | bytes 1081344 | tf_op jit(solution)/shard_map/all_to_all | solution.py:43
  26.6 1.5 %shard_map.139 = bf16[8,384,384]{2,1,0:T(8,128)(2,1)} custom-call(bf16[8,88,384]{2,1,0:T(8,128)(2,1)S(1)} %all_to_all.35.got_ref), custom_call_target="tpu_custom_call" | custom-call | tf_op jit(solution)/shard_map/pallas_call | solution.py:359
  28.1 0.0 copy-start.7
  28.1 5.7 %all-to-all-start.4 = ((bf16[8,384,384]{2,1,0:T(8,128)(2,1)}), bf16[8,384,384]{2,1,0:T(8,128)(2,1)S(1)}, u32[]{:S(2)}, u32[]{:S(2)}) async-start(bf16[8,384,384]{2,1,0:T(8,128)(2,1)} %shard_map.139), calls=%async_computation.4 | async-start | bytes 4718592 | tf_op jit(solution)/shard_map/all_to_all | solution.py:43
  33.8 0.0 copy-done.7
  33.9 0.0 copy-start.2
  33.9 32.8 %all-gather = bf16[1216,384]{1,0:T(8,128)(2,1)S(1)} all-gather(bf16[152,384]{1,0:T(8,128)(2,1)S(1)} %get-tuple-element.65), channel_id=2, replica_groups=mesh['seq_0'=4,'seq_1a'=4,'seq_1b'=2,'seq_2'=2,'tp'=8] {'tp'}, dimensions={0}, use_global_device_ids=true | all-gather | bytes 1050624 | tf_op jit(solution)/shard_map/all_gather | solution.py:378
  66.6 1.1 shard_map.138.own_ref
  67.7 1.9 %collective-permute-start = (bf16[8,152,384]{2,1,0:T(8,128)(2,1)S(1)}, bf16[8,152,384]{2,1,0:T(8,128)(2,1)S(1)}, u32[]{:S(2)}, u32[]{:S(2)}) collective-permute-start(bf16[8,152,384]{2,1,0:T(8,128)(2,1)S(1)} %shard_map.138.own_ref), channel_id=1, source_target_pairs={{0,8},{8,0},{1,9},{9,1},{2,10},{10,2},{3,11},{11,3},{4,12},{12,4},... | collective-permute-start | bytes 2801672 | tf_op jit(solution)/shard_map/ppermute | solution.py:380
  69.6 2.5 %collective-permute-done.other_ref = bf16[8,152,384]{2,1,0:T(8,128)(2,1)S(1)} collective-permute-done((bf16[8,152,384]{2,1,0:T(8,128)(2,1)S(1)}, bf16[8,152,384]{2,1,0:T(8,128)(2,1)S(1)}, u32[]{:S(2)}, u32[]{:S(2)}) %collective-permute-start) | collective-permute-done | bytes 933920 | tf_op jit(solution)/shard_map/ppermute | solution.py:380
  72.1 0.0 copy-start
  72.1 0.9 copy-done
  73.1 0.0 all-to-all-done.4
  73.1 0.0 copy-done.2
  73.1 0.0 copy-start.1
  73.1 1.2 copy-done.1
  74.2 1.5 %shard_map.140 = (bf16[2,128,128]{2,1,0:T(8,128)(2,1)S(1)}, bf16[8,2,152,256]{3,2,1,0:T(8,128)(2,1)S(1)}) custom-call(bf16[8,152,384]{2,1,0:T(8,128)(2,1)S(1)} %shard_map.138.own_ref, bf16[8,152,384]{2,1,0:T(8,128)(2,1)S(1)} %copy-done.1, bf16[8,8,48,384]{3,2,1,0:T(8,128)(2,1)S(1)} %bitcast.4, f32[2,256]{1,0:T(2,128)S(1)} %copy-done.2), custom_call_target="tpu_custom_call" | custom-call | tf_op jit(solution)/shard_map/pallas_call | solution.py:382
  75.8 0.0 copy-start.3
  75.8 0.0 copy-start.4
  75.8 0.0 copy-start.5
  75.8 0.0 copy-start.6
  75.9 0.0 copy-start.8
  75.9 22.5 %all_to_all.36.pair_ref = bf16[8,2,152,256]{3,2,1,0:T(8,128)(2,1)S(1)} all-to-all(bf16[8,2,152,256]{3,2,1,0:T(8,128)(2,1)S(1)} %get-tuple-element.68), channel_id=1, replica_groups=mesh['seq_0'=4,'seq_1a'=4,'seq_1b'=2,'seq_2'=2,'tp'=8] {'seq_1b','seq_0'}, dimensions={0} | all-to-all | bytes 2490368 | tf_op jit(solution)/shard_map/all_to_all | solution.py:43
  98.4 0.0 copy-done.3
  98.4 2.7 %shard_map.141 = bf16[8,40,128]{2,1,0:T(8,128)(2,1)} custom-call(s32[4]{0:T(128)S(1)} %copy-done.3, bf16[2,128,128]{2,1,0:T(8,128)(2,1)S(1)} %get-tuple-element.67.query_ref, bf16[8,2,152,256]{3,2,1,0:T(8,128)(2,1)S(1)} %all_to_all.36.pair_ref), custom_call_target="tpu_custom_call" | custom-call | tf_op jit(solution)/shard_map/pallas_call | solution.py:389
  101.1 3.4 %all-to-all-start.6 = ((bf16[8,40,128]{2,1,0:T(8,128)(2,1)}), bf16[8,40,128]{2,1,0:T(8,128)(2,1)S(1)}, u32[]{:S(2)}, u32[]{:S(2)}) async-start(bf16[8,40,128]{2,1,0:T(8,128)(2,1)} %shard_map.141), calls=%async_computation.6 | async-start | bytes 163840 | tf_op jit(solution)/shard_map/all_to_all | solution.py:43
  105.1 8.1 %all-to-all-done.6 = bf16[8,40,128]{2,1,0:T(8,128)(2,1)S(1)} async-done(((bf16[8,40,128]{2,1,0:T(8,128)(2,1)}), bf16[8,40,128]{2,1,0:T(8,128)(2,1)S(1)}, u32[]{:S(2)}, u32[]{:S(2)}) %all-to-all-start.6) | async-done | bytes 81952 | tf_op jit(solution)/shard_map/all_to_all | solution.py:43
  113.2 0.0 copy-done.4
  113.2 0.0 copy-done.5
  113.2 0.0 copy-done.6
  113.2 0.0 copy-done.8
  113.3 17.7 %conditional.1 = ((f32[4,32,384]{2,1,0:T(8,128)}, f32[4,32,384]{2,1,0:T(8,128)}, f32[4]{0:T(128)})) conditional(s32[]{:T(128)} %bitcast.1, (s32[4]{0:T(128)S(1)}, bf16[8,40,128]{2,1,0:T(8,128)(2,1)S(1)}, bf16[256,3072]{1,0:T(8,128)(2,1)S(1)}, f32[4,32,384]{2,1,0:T(8,128)S(1)}, bf16[4,32,384]{2,1,0:T(8,128)(2,1)S(1)}, ...), branch_computations={%region_0.0_spmd, %region_1.0_spmd, %region_2.0_spmd} | conditional | bytes 1277960 | solution.py:398
  113.3 0.9 branch_0_fun.2
  114.1 14.8 %all_to_all.32.part_ref = bf16[8,40,384]{2,1,0:T(8,128)(2,1)S(1)} all-to-all(bf16[8,40,384]{2,1,0:T(8,128)(2,1)S(1)} %branch_0_fun.2), channel_id=1, replica_groups=mesh['seq_0'=4,'seq_1a'=4,'seq_1b'=2,'seq_2'=2,'tp'=8] {'tp'}, dimensions={0} | all-to-all | bytes 491520 | tf_op jit(solution)/shard_map/cond/branch_0_fun/all_to_all | solution.py:43
  128.9 2.1 %branch_0_fun.3 = (f32[4,32,384]{2,1,0:T(8,128)}, f32[4,32,384]{2,1,0:T(8,128)}, f32[4]{0:T(128)}) custom-call(s32[4]{0:T(128)S(1)} %get-tuple-element.36.flag_ref, bf16[8,40,384]{2,1,0:T(8,128)(2,1)S(1)} %all_to_all.32.part_ref, f32[4,32,384]{2,1,0:T(8,128)S(1)} %get-tuple-element.90.cache_ref, bf16[4,32,384]{2,1,0:T(8,128)(2,1)S(1)} %get-tuple-element.40.img_ref, ...), custom_call_target="tpu_custom_call" | custom-call | tf_op jit(solution)/shard_map/cond/branch_0_fun/pallas_call | solution.py:412
  (1 shorter events, 0.0 us)
Async XLA Ops:
  28.1 5.7 %copy-start.7 = (bf16[3,4,384]{2,1,0:T(4,128)(2,1)S(1)}, bf16[3,4,384]{2,1,0:T(4,128)(2,1)}, u32[]{:S(2)}) copy-start(bf16[3,4,384]{2,1,0:T(4,128)(2,1)} %mod_ref.1) | copy-start | bytes 27652
  28.1 45.0 %all-to-all-start.4 = ((bf16[8,384,384]{2,1,0:T(8,128)(2,1)}), bf16[8,384,384]{2,1,0:T(8,128)(2,1)S(1)}, u32[]{:S(2)}, u32[]{:S(2)}) async-start(bf16[8,384,384]{2,1,0:T(8,128)(2,1)} %shard_map.139), calls=%async_computation.4 | async-start | bytes 4718592 | tf_op jit(solution)/shard_map/all_to_all | solution.py:43
  33.9 39.2 %copy-start.2 = (f32[2,256]{1,0:T(2,128)S(1)}, f32[2,256]{1,0:T(2,128)}, u32[]{:S(2)}) copy-start(f32[2,256]{1,0:T(2,128)} %gain_ref.1) | copy-start | bytes 6148
  67.7 4.4 %collective-permute-start = (bf16[8,152,384]{2,1,0:T(8,128)(2,1)S(1)}, bf16[8,152,384]{2,1,0:T(8,128)(2,1)S(1)}, u32[]{:S(2)}, u32[]{:S(2)}) collective-permute-start(bf16[8,152,384]{2,1,0:T(8,128)(2,1)S(1)} %shard_map.138.own_ref), channel_id=1, source_target_pairs={{0,8},{8,0},{1,9},{9,1},{2,10},{10,2},{3,11},{11,3},{4,12},{12,4},... | collective-permute-start | bytes 2801672 | tf_op jit(solution)/shard_map/ppermute | solution.py:380
  72.1 0.9 copy-start
  73.1 1.2 copy-start.1
  75.8 22.6 %copy-start.3 = (s32[4]{0:T(128)S(1)}, s32[4]{0:T(128)}, u32[]{:S(2)}) copy-start(s32[4]{0:T(128)} %limit_ref.1) | copy-start | bytes 52
  75.8 37.4 %copy-start.4 = (bf16[256,3072]{1,0:T(8,128)(2,1)S(1)}, bf16[256,3072]{1,0:T(8,128)(2,1)}, u32[]{:S(2)}) copy-start(bf16[256,3072]{1,0:T(8,128)(2,1)} %param.20) | copy-start | bytes 4718596
  75.8 37.4 %copy-start.5 = (f32[4,32,384]{2,1,0:T(8,128)S(1)}, f32[4,32,384]{2,1,0:T(8,128)}, u32[]{:S(2)}) copy-start(f32[4,32,384]{2,1,0:T(8,128)} %param.16) | copy-start | bytes 589828
  75.8 37.4 %copy-start.6 = (bf16[4,32,384]{2,1,0:T(8,128)(2,1)S(1)}, bf16[4,32,384]{2,1,0:T(8,128)(2,1)}, u32[]{:S(2)}) copy-start(bf16[4,32,384]{2,1,0:T(8,128)(2,1)} %img_hbm.1) | copy-start | bytes 294916
  75.9 37.4 %copy-start.8 = (s32[4]{0:T(128)S(1)}, s32[4]{0:T(128)}, u32[]{:S(2)}) copy-start(s32[4]{0:T(128)} %flag_hbm.1) | copy-start | bytes 52
  101.1 12.1 %all-to-all-start.6 = ((bf16[8,40,128]{2,1,0:T(8,128)(2,1)}), bf16[8,40,128]{2,1,0:T(8,128)(2,1)S(1)}, u32[]{:S(2)}, u32[]{:S(2)}) async-start(bf16[8,40,128]{2,1,0:T(8,128)(2,1)} %shard_map.141), calls=%async_computation.6 | async-start | bytes 163840 | tf_op jit(solution)/shard_map/all_to_all | solution.py:43

commit v14 on v12

--- a/solution.py
+++ b/solution.py
@@ -1,4 +1,5 @@
 import functools
+import math
 
 import jax
 import jax.numpy as jnp
@@ -227,28 +228,26 @@
     source = (slot - img) // txt_half
     y = source // 2 * 2 + block // 4
     device = (block % 4 * 8 + y) * 2 + source % 2
-    scores_of, valid_of = [], []
+    raw_of = []
     rel = jnp.zeros((1, HD), F32)
     for half in range(halves):
         actual = jnp.where(half == 0, core, 1 - core)
         keys = pair_ref[:, half, :, :HD].reshape(count, HD)
-        scores = lax.dot_general(
+        raw = lax.dot_general(
             query, keys, (((1,), (1,)), ((), ())), preferred_element_type=F32
-        ) * (1.0 / HD**0.5)
+        )
         text = device * 4 + actual * txt_half + (slot - img) % txt_half
         valid = (slot < img) | ((slot < img + txt) & (text < limit_ref[far]))
-        scores_of.append(jnp.where(valid, scores, NEG))
-        valid_of.append(valid)
+        raw_of.append(raw + jnp.where(valid, 0.0, NEG))
         for b in range(blocks):
             carried = pair_ref[b, half, rows - 8 :, :HD].astype(F32)
             rel = rel + jnp.sum(carried, axis=0, keepdims=True)
-    top = functools.reduce(
-        jnp.maximum, [jnp.max(s, axis=1, keepdims=True) for s in scores_of]
-    )
+    factor = math.log2(math.e) / HD**0.5
+    top = functools.reduce(jnp.maximum, [jnp.max(r, axis=1, keepdims=True) for r in raw_of])
     total = jnp.zeros((2 * img, 1), F32)
     summed = jnp.zeros((2 * img, HD), F32)
     for half in range(halves):
-        weights = jnp.where(valid_of[half], jnp.exp(scores_of[half] - top), 0.0)
+        weights = jnp.exp2((raw_of[half] - top) * factor)
         total = total + jnp.sum(weights, axis=1, keepdims=True)
         values = pair_ref[:, half, :, HD:].reshape(count, HD)
         summed = summed + jnp.dot(weights.astype(BF16), values, preferred_element_type=F32)

time: 131 us -> 131 us (level)
  no operation moved by 1% of the time
where the time goes in v14:
time: 131 us; the launch traced here: 130 us
  blocking collectives  94.8 us (72%)
  starting transfers between devices  11 us (8%)
  waiting for transfers between devices  10.6 us (8%)
  Pallas kernels  10.4 us (8%)
  local copies, waits for them, and re-layouts  2.18 us (2%)
  between operations  1.4 us (1%)
    all_to_all x3, blocking collectives, swap(): return lax.all_to_all(value, axis, 0, 0, tiled=True)  62 us
    all_gather x1, blocking collectives, local(): wide = lax.all_gather(joined, TP, axis=0, tiled=False)  32.8 us
    all_to_all x2, starting transfers between devices, swap(): return lax.all_to_all(value, axis, 0, 0, tiled=True)  9.07 us
    all_to_all x2, waiting for transfers between devices, swap(): return lax.all_to_all(value, axis, 0, 0, tiled=True)  8.13 us
    pallas_call x1, Pallas kernels, local(): call(functools.partial(attend_body, img_half, txt_half), shaped(sources,...  2.69 us
  transfers between devices with their start and end apart: 3, of which 2 were waited for; matrix products, arithmetic and copies ran while one was open for 0% of the time, Pallas kernels for 1%

profile of v14, /device:TPU:8, one launch (start us, length us, event | category | flops | bytes accessed | tf_op | source)
XLA Modules:
  0.0 130.3 jit_solution(10877406324734400593)
XLA Ops:
  0.6 1.2 shard_map.136
  1.9 24.7 %all_to_all.35.got_ref = bf16[8,88,384]{2,1,0:T(8,128)(2,1)S(1)} all-to-all(bf16[8,88,384]{2,1,0:T(8,128)(2,1)S(1)} %get-tuple-element.64), channel_id=1, replica_groups=mesh['seq_0'=4,'seq_1a'=4,'seq_1b'=2,'seq_2'=2,'tp'=8] {'seq_1a','seq_2'}, dimensions={0} | all-to-all | bytes 1081344 | tf_op jit(solution)/shard_map/all_to_all | solution.py:43
  26.6 1.5 %shard_map.139 = bf16[8,384,384]{2,1,0:T(8,128)(2,1)} custom-call(bf16[8,88,384]{2,1,0:T(8,128)(2,1)S(1)} %all_to_all.35.got_ref), custom_call_target="tpu_custom_call" | custom-call | tf_op jit(solution)/shard_map/pallas_call | solution.py:350
  28.1 0.0 copy-start.7
  28.1 5.7 %all-to-all-start.4 = ((bf16[8,384,384]{2,1,0:T(8,128)(2,1)}), bf16[8,384,384]{2,1,0:T(8,128)(2,1)S(1)}, u32[]{:S(2)}, u32[]{:S(2)}) async-start(bf16[8,384,384]{2,1,0:T(8,128)(2,1)} %shard_map.139), calls=%async_computation.4 | async-start | bytes 4718592 | tf_op jit(solution)/shard_map/all_to_all | solution.py:43
  33.8 0.0 copy-done.7
  33.9 0.0 copy-start.2
  33.9 32.8 %all-gather = bf16[1216,384]{1,0:T(8,128)(2,1)S(1)} all-gather(bf16[152,384]{1,0:T(8,128)(2,1)S(1)} %get-tuple-element.65), channel_id=2, replica_groups=mesh['seq_0'=4,'seq_1a'=4,'seq_1b'=2,'seq_2'=2,'tp'=8] {'tp'}, dimensions={0}, use_global_device_ids=true | all-gather | bytes 1050624 | tf_op jit(solution)/shard_map/all_gather | solution.py:369
  66.6 1.1 shard_map.138.own_ref
  67.7 1.9 %collective-permute-start = (bf16[8,152,384]{2,1,0:T(8,128)(2,1)S(1)}, bf16[8,152,384]{2,1,0:T(8,128)(2,1)S(1)}, u32[]{:S(2)}, u32[]{:S(2)}) collective-permute-start(bf16[8,152,384]{2,1,0:T(8,128)(2,1)S(1)} %shard_map.138.own_ref), channel_id=1, source_target_pairs={{0,8},{8,0},{1,9},{9,1},{2,10},{10,2},{3,11},{11,3},{4,12},{12,4},... | collective-permute-start | bytes 2801672 | tf_op jit(solution)/shard_map/ppermute | solution.py:371
  69.6 2.5 %collective-permute-done.other_ref = bf16[8,152,384]{2,1,0:T(8,128)(2,1)S(1)} collective-permute-done((bf16[8,152,384]{2,1,0:T(8,128)(2,1)S(1)}, bf16[8,152,384]{2,1,0:T(8,128)(2,1)S(1)}, u32[]{:S(2)}, u32[]{:S(2)}) %collective-permute-start) | collective-permute-done | bytes 933920 | tf_op jit(solution)/shard_map/ppermute | solution.py:371
  72.1 0.0 copy-start
  72.1 0.9 copy-done
  73.1 0.0 all-to-all-done.4
  73.1 0.0 copy-done.2
  73.1 0.0 copy-start.1
  73.1 1.2 copy-done.1
  74.2 1.5 %shard_map.140 = (bf16[2,128,128]{2,1,0:T(8,128)(2,1)S(1)}, bf16[8,2,152,256]{3,2,1,0:T(8,128)(2,1)S(1)}) custom-call(bf16[8,152,384]{2,1,0:T(8,128)(2,1)S(1)} %shard_map.138.own_ref, bf16[8,152,384]{2,1,0:T(8,128)(2,1)S(1)} %copy-done.1, bf16[8,8,48,384]{3,2,1,0:T(8,128)(2,1)S(1)} %bitcast.4, f32[2,256]{1,0:T(2,128)S(1)} %copy-done.2), custom_call_target="tpu_custom_call" | custom-call | tf_op jit(solution)/shard_map/pallas_call | solution.py:373
  75.8 0.0 copy-start.3
  75.8 0.0 copy-start.4
  75.8 0.0 copy-start.5
  75.8 0.0 copy-start.6
  75.9 0.0 copy-start.8
  75.9 22.5 %all_to_all.36.pair_ref = bf16[8,2,152,256]{3,2,1,0:T(8,128)(2,1)S(1)} all-to-all(bf16[8,2,152,256]{3,2,1,0:T(8,128)(2,1)S(1)} %get-tuple-element.68), channel_id=1, replica_groups=mesh['seq_0'=4,'seq_1a'=4,'seq_1b'=2,'seq_2'=2,'tp'=8] {'seq_1b','seq_0'}, dimensions={0} | all-to-all | bytes 2490368 | tf_op jit(solution)/shard_map/all_to_all | solution.py:43
  98.4 0.0 copy-done.3
  98.4 2.7 %shard_map.141 = bf16[8,40,128]{2,1,0:T(8,128)(2,1)} custom-call(s32[4]{0:T(128)S(1)} %copy-done.3, bf16[2,128,128]{2,1,0:T(8,128)(2,1)S(1)} %get-tuple-element.67.query_ref, bf16[8,2,152,256]{3,2,1,0:T(8,128)(2,1)S(1)} %all_to_all.36.pair_ref), custom_call_target="tpu_custom_call" | custom-call | tf_op jit(solution)/shard_map/pallas_call | solution.py:380
  101.1 3.4 %all-to-all-start.6 = ((bf16[8,40,128]{2,1,0:T(8,128)(2,1)}), bf16[8,40,128]{2,1,0:T(8,128)(2,1)S(1)}, u32[]{:S(2)}, u32[]{:S(2)}) async-start(bf16[8,40,128]{2,1,0:T(8,128)(2,1)} %shard_map.141), calls=%async_computation.6 | async-start | bytes 163840 | tf_op jit(solution)/shard_map/all_to_all | solution.py:43
  105.1 8.1 %all-to-all-done.6 = bf16[8,40,128]{2,1,0:T(8,128)(2,1)S(1)} async-done(((bf16[8,40,128]{2,1,0:T(8,128)(2,1)}), bf16[8,40,128]{2,1,0:T(8,128)(2,1)S(1)}, u32[]{:S(2)}, u32[]{:S(2)}) %all-to-all-start.6) | async-done | bytes 81952 | tf_op jit(solution)/shard_map/all_to_all | solution.py:43
  113.2 0.0 copy-done.4
  113.2 0.0 copy-done.5
  113.2 0.0 copy-done.6
  113.2 0.0 copy-done.8
  113.3 17.1 %conditional.1 = ((f32[4,32,384]{2,1,0:T(8,128)}, f32[4,32,384]{2,1,0:T(8,128)}, f32[4]{0:T(128)})) conditional(s32[]{:T(128)} %bitcast.1, (s32[4]{0:T(128)S(1)}, bf16[8,40,128]{2,1,0:T(8,128)(2,1)S(1)}, bf16[256,3072]{1,0:T(8,128)(2,1)S(1)}, f32[4,32,384]{2,1,0:T(8,128)S(1)}, bf16[4,32,384]{2,1,0:T(8,128)(2,1)S(1)}, ...), branch_computations={%region_0.0_spmd, %region_1.0_spmd, %region_2.0_spmd} | conditional | bytes 1277960 | solution.py:389
  113.3 0.9 branch_0_fun.2
  114.1 14.8 %all_to_all.32.part_ref = bf16[8,40,384]{2,1,0:T(8,128)(2,1)S(1)} all-to-all(bf16[8,40,384]{2,1,0:T(8,128)(2,1)S(1)} %branch_0_fun.2), channel_id=1, replica_groups=mesh['seq_0'=4,'seq_1a'=4,'seq_1b'=2,'seq_2'=2,'tp'=8] {'tp'}, dimensions={0} | all-to-all | bytes 491520 | tf_op jit(solution)/shard_map/cond/branch_0_fun/all_to_all | solution.py:43
  128.9 1.4 %branch_0_fun.3 = (f32[4,32,384]{2,1,0:T(8,128)}, f32[4,32,384]{2,1,0:T(8,128)}, f32[4]{0:T(128)}) custom-call(s32[4]{0:T(128)S(1)} %get-tuple-element.36.flag_ref, bf16[8,40,384]{2,1,0:T(8,128)(2,1)S(1)} %all_to_all.32.part_ref, f32[4,32,384]{2,1,0:T(8,128)S(1)} %get-tuple-element.90.cache_ref, bf16[4,32,384]{2,1,0:T(8,128)(2,1)S(1)} %get-tuple-element.40.img_ref, ...), custom_call_target="tpu_custom_call" | custom-call | tf_op jit(solution)/shard_map/cond/branch_0_fun/pallas_call | solution.py:403
  (1 shorter events, 0.0 us)
Async XLA Ops:
  28.1 5.7 %copy-start.7 = (bf16[3,4,384]{2,1,0:T(4,128)(2,1)S(1)}, bf16[3,4,384]{2,1,0:T(4,128)(2,1)}, u32[]{:S(2)}) copy-start(bf16[3,4,384]{2,1,0:T(4,128)(2,1)} %mod_ref.1) | copy-start | bytes 27652
  28.1 45.0 %all-to-all-start.4 = ((bf16[8,384,384]{2,1,0:T(8,128)(2,1)}), bf16[8,384,384]{2,1,0:T(8,128)(2,1)S(1)}, u32[]{:S(2)}, u32[]{:S(2)}) async-start(bf16[8,384,384]{2,1,0:T(8,128)(2,1)} %shard_map.139), calls=%async_computation.4 | async-start | bytes 4718592 | tf_op jit(solution)/shard_map/all_to_all | solution.py:43
  33.9 39.2 %copy-start.2 = (f32[2,256]{1,0:T(2,128)S(1)}, f32[2,256]{1,0:T(2,128)}, u32[]{:S(2)}) copy-start(f32[2,256]{1,0:T(2,128)} %gain_ref.1) | copy-start | bytes 6148
  67.7 4.4 %collective-permute-start = (bf16[8,152,384]{2,1,0:T(8,128)(2,1)S(1)}, bf16[8,152,384]{2,1,0:T(8,128)(2,1)S(1)}, u32[]{:S(2)}, u32[]{:S(2)}) collective-permute-start(bf16[8,152,384]{2,1,0:T(8,128)(2,1)S(1)} %shard_map.138.own_ref), channel_id=1, source_target_pairs={{0,8},{8,0},{1,9},{9,1},{2,10},{10,2},{3,11},{11,3},{4,12},{12,4},... | collective-permute-start | bytes 2801672 | tf_op jit(solution)/shard_map/ppermute | solution.py:371
  72.1 0.9 copy-start
  73.1 1.2 copy-start.1
  75.8 22.6 %copy-start.3 = (s32[4]{0:T(128)S(1)}, s32[4]{0:T(128)}, u32[]{:S(2)}) copy-start(s32[4]{0:T(128)} %limit_ref.1) | copy-start | bytes 52
  75.8 37.4 %copy-start.4 = (bf16[256,3072]{1,0:T(8,128)(2,1)S(1)}, bf16[256,3072]{1,0:T(8,128)(2,1)}, u32[]{:S(2)}) copy-start(bf16[256,3072]{1,0:T(8,128)(2,1)} %param.20) | copy-start | bytes 4718596
  75.8 37.4 %copy-start.5 = (f32[4,32,384]{2,1,0:T(8,128)S(1)}, f32[4,32,384]{2,1,0:T(8,128)}, u32[]{:S(2)}) copy-start(f32[4,32,384]{2,1,0:T(8,128)} %param.16) | copy-start | bytes 589828
  75.8 37.4 %copy-start.6 = (bf16[4,32,384]{2,1,0:T(8,128)(2,1)S(1)}, bf16[4,32,384]{2,1,0:T(8,128)(2,1)}, u32[]{:S(2)}) copy-start(bf16[4,32,384]{2,1,0:T(8,128)(2,1)} %img_hbm.1) | copy-start | bytes 294916
  75.9 37.4 %copy-start.8 = (s32[4]{0:T(128)S(1)}, s32[4]{0:T(128)}, u32[]{:S(2)}) copy-start(s32[4]{0:T(128)} %flag_hbm.1) | copy-start | bytes 52
  101.1 12.1 %all-to-all-start.6 = ((bf16[8,40,128]{2,1,0:T(8,128)(2,1)}), bf16[8,40,128]{2,1,0:T(8,128)(2,1)S(1)}, u32[]{:S(2)}, u32[]{:S(2)}) async-start(bf16[8,40,128]{2,1,0:T(8,128)(2,1)} %shard_map.141), calls=%async_computation.6 | async-start | bytes 163840 | tf_op jit(solution)/shard_map/all_to_all | solution.py:43

commit v15 on v14

--- a/solution.py
+++ b/solution.py
@@ -203,54 +203,57 @@
     query, keyed = parts
     valued = total[:, 2 * HD :].astype(BF16)
     img = query_ref.shape[1]
+    carried = jnp.zeros((8, HD), F32)
     for half, ref in enumerate((own_ref, other_ref)):
         at = half * rows
         query_ref[half] = query[at : at + img].astype(BF16)
-        carried = ref[0, rows - 8 :, :HD]
         keys = keyed[at : at + rows - 8].astype(BF16)
+        to = slice(half * (rows - 8), (half + 1) * (rows - 8))
         for copy in range(pair_ref.shape[0]):
-            pair_ref[copy, half, : rows - 8, :HD] = keys
-            pair_ref[copy, half, rows - 8 :, :HD] = carried
-            pair_ref[copy, half, :, HD:] = valued[at : at + rows]
+            pair_ref[copy, to, :HD] = keys
+            pair_ref[copy, to, HD:] = valued[at : at + rows - 8]
+        carried = carried + ref[0, rows - 8 :, :HD].astype(F32)
+    tail = stacked_parts(jnp.sum(carried, axis=0, keepdims=True), 8).astype(BF16)
+    for copy in range(pair_ref.shape[0]):
+        pair_ref[copy, 2 * (rows - 8) :, :HD] = tail
+        pair_ref[copy, 2 * (rows - 8) :, HD:] = jnp.zeros((8, HD), BF16)
 
 
 def attend_body(img_half, txt_half, limit_ref, query_ref, pair_ref, out_ref):
-    blocks, halves, rows, _ = pair_ref.shape
+    blocks, rows, _ = pair_ref.shape
+    halves = 2
     sources = out_ref.shape[0]
     img = sources * img_half
     txt = sources * txt_half
     count = blocks * rows
     far, core = lax.axis_index(FAR), lax.axis_index(CORE)
-    query = query_ref[...].reshape(2 * img, HD)
+    query = query_ref[...].reshape(halves * img, HD)
     index = lax.broadcasted_iota(jnp.int32, (1, count), 1)
-    slot = index % rows
+    spot = index % rows
     block = index // rows
+    half = jnp.where(spot >= img + txt, 1, 0)
+    slot = spot - half * (img + txt)
     source = (slot - img) // txt_half
     y = source // 2 * 2 + block // 4
     device = (block % 4 * 8 + y) * 2 + source % 2
-    raw_of = []
+    actual = jnp.where(half == 0, core, 1 - core)
+    text = device * 4 + actual * txt_half + (slot - img) % txt_half
+    valid = (slot < img) | ((slot < img + txt) & (text < limit_ref[far]))
+    bias = jnp.where(valid & (spot < halves * (img + txt)), 0.0, NEG)
+    keys = pair_ref[:, :, :HD].reshape(count, HD)
+    raw = lax.dot_general(
+        query, keys, (((1,), (1,)), ((), ())), preferred_element_type=F32
+    ) + bias
     rel = jnp.zeros((1, HD), F32)
-    for half in range(halves):
-        actual = jnp.where(half == 0, core, 1 - core)
-        keys = pair_ref[:, half, :, :HD].reshape(count, HD)
-        raw = lax.dot_general(
-            query, keys, (((1,), (1,)), ((), ())), preferred_element_type=F32
-        )
-        text = device * 4 + actual * txt_half + (slot - img) % txt_half
-        valid = (slot < img) | ((slot < img + txt) & (text < limit_ref[far]))
-        raw_of.append(raw + jnp.where(valid, 0.0, NEG))
-        for b in range(blocks):
-            carried = pair_ref[b, half, rows - 8 :, :HD].astype(F32)
-            rel = rel + jnp.sum(carried, axis=0, keepdims=True)
+    for b in range(blocks):
+        carried = pair_ref[b, rows - 8 :, :HD].astype(F32)
+        rel = rel + jnp.sum(carried, axis=0, keepdims=True)
     factor = math.log2(math.e) / HD**0.5
-    top = functools.reduce(jnp.maximum, [jnp.max(r, axis=1, keepdims=True) for r in raw_of])
-    total = jnp.zeros((2 * img, 1), F32)
-    summed = jnp.zeros((2 * img, HD), F32)
-    for half in range(halves):
-        weights = jnp.exp2((raw_of[half] - top) * factor)
-        total = total + jnp.sum(weights, axis=1, keepdims=True)
-        values = pair_ref[:, half, :, HD:].reshape(count, HD)
-        summed = summed + jnp.dot(weights.astype(BF16), values, preferred_element_type=F32)
+    top = jnp.max(raw, axis=1, keepdims=True)
+    weights = jnp.exp2((raw - top) * factor)
+    total = jnp.sum(weights, axis=1, keepdims=True)
+    values = pair_ref[:, :, HD:].reshape(count, HD)
+    summed = jnp.dot(weights.astype(BF16), values, preferred_element_type=F32)
     attended = (summed / total).astype(BF16)
     tail = stacked_parts(rel, 8).astype(BF16)
     for half in range(halves):
@@ -372,7 +375,7 @@
 
     query, pairs = call(
         project_body,
-        (shaped(2, sources * img_half, HD), shaped(around, 2, rows, 2 * HD)),
+        (shaped(2, sources * img_half, HD), shaped(around, 2 * rows - 8, 2 * HD)),
         [VMEM] * 4,
         16,
     )(own, other, weight, qk_gain)

time: 131 us -> 130 us (level)
  no operation moved by 1% of the time
where the time goes in v15:
time: 130 us
  blocking collectives  94.4 us (73%)
  starting transfers between devices  11 us (8%)
  waiting for transfers between devices  10.6 us (8%)
  Pallas kernels  10.2 us (8%)
  local copies, waits for them, and re-layouts  2.18 us (2%)
  between operations  1.4 us (1%)
    all_to_all x3, blocking collectives, swap(): return lax.all_to_all(value, axis, 0, 0, tiled=True)  61.6 us
    all_gather x1, blocking collectives, local(): wide = lax.all_gather(joined, TP, axis=0, tiled=False)  32.8 us
    all_to_all x2, starting transfers between devices, swap(): return lax.all_to_all(value, axis, 0, 0, tiled=True)  9.07 us
    all_to_all x2, waiting for transfers between devices, swap(): return lax.all_to_all(value, axis, 0, 0, tiled=True)  8.13 us
  transfers between devices with their start and end apart: 3, of which 2 were waited for; matrix products, arithmetic and copies ran while one was open for 0% of the time, Pallas kernels for 1%

profile of v15, /device:TPU:8, one launch (start us, length us, event | category | flops | bytes accessed | tf_op | source)
XLA Modules:
  0.0 129.8 jit_solution(13943034004832449902)
XLA Ops:
  0.6 1.2 shard_map.136
  1.9 24.7 %all_to_all.35.got_ref = bf16[8,88,384]{2,1,0:T(8,128)(2,1)S(1)} all-to-all(bf16[8,88,384]{2,1,0:T(8,128)(2,1)S(1)} %get-tuple-element.64), channel_id=1, replica_groups=mesh['seq_0'=4,'seq_1a'=4,'seq_1b'=2,'seq_2'=2,'tp'=8] {'seq_1a','seq_2'}, dimensions={0} | all-to-all | bytes 1081344 | tf_op jit(solution)/shard_map/all_to_all | solution.py:43
  26.6 1.5 %shard_map.139 = bf16[8,384,384]{2,1,0:T(8,128)(2,1)} custom-call(bf16[8,88,384]{2,1,0:T(8,128)(2,1)S(1)} %all_to_all.35.got_ref), custom_call_target="tpu_custom_call" | custom-call | tf_op jit(solution)/shard_map/pallas_call | solution.py:353
  28.1 0.0 copy-start.7
  28.1 5.7 %all-to-all-start.4 = ((bf16[8,384,384]{2,1,0:T(8,128)(2,1)}), bf16[8,384,384]{2,1,0:T(8,128)(2,1)S(1)}, u32[]{:S(2)}, u32[]{:S(2)}) async-start(bf16[8,384,384]{2,1,0:T(8,128)(2,1)} %shard_map.139), calls=%async_computation.4 | async-start | bytes 4718592 | tf_op jit(solution)/shard_map/all_to_all | solution.py:43
  33.8 0.0 copy-done.7
  33.9 0.0 copy-start.2
  33.9 32.8 %all-gather = bf16[1216,384]{1,0:T(8,128)(2,1)S(1)} all-gather(bf16[152,384]{1,0:T(8,128)(2,1)S(1)} %get-tuple-element.65), channel_id=2, replica_groups=mesh['seq_0'=4,'seq_1a'=4,'seq_1b'=2,'seq_2'=2,'tp'=8] {'tp'}, dimensions={0}, use_global_device_ids=true | all-gather | bytes 1050624 | tf_op jit(solution)/shard_map/all_gather | solution.py:372
  66.6 1.1 shard_map.138.own_ref
  67.7 1.9 %collective-permute-start = (bf16[8,152,384]{2,1,0:T(8,128)(2,1)S(1)}, bf16[8,152,384]{2,1,0:T(8,128)(2,1)S(1)}, u32[]{:S(2)}, u32[]{:S(2)}) collective-permute-start(bf16[8,152,384]{2,1,0:T(8,128)(2,1)S(1)} %shard_map.138.own_ref), channel_id=1, source_target_pairs={{0,8},{8,0},{1,9},{9,1},{2,10},{10,2},{3,11},{11,3},{4,12},{12,4},... | collective-permute-start | bytes 2801672 | tf_op jit(solution)/shard_map/ppermute | solution.py:374
  69.6 2.5 %collective-permute-done.other_ref = bf16[8,152,384]{2,1,0:T(8,128)(2,1)S(1)} collective-permute-done((bf16[8,152,384]{2,1,0:T(8,128)(2,1)S(1)}, bf16[8,152,384]{2,1,0:T(8,128)(2,1)S(1)}, u32[]{:S(2)}, u32[]{:S(2)}) %collective-permute-start) | collective-permute-done | bytes 933920 | tf_op jit(solution)/shard_map/ppermute | solution.py:374
  72.1 0.0 copy-start
  72.1 0.9 copy-done
  73.1 0.0 all-to-all-done.4
  73.1 0.0 copy-done.2
  73.1 0.0 copy-start.1
  73.1 1.2 copy-done.1
  74.2 1.5 %shard_map.140 = (bf16[2,128,128]{2,1,0:T(8,128)(2,1)S(1)}, bf16[8,296,256]{2,1,0:T(8,128)(2,1)S(1)}) custom-call(bf16[8,152,384]{2,1,0:T(8,128)(2,1)S(1)} %shard_map.138.own_ref, bf16[8,152,384]{2,1,0:T(8,128)(2,1)S(1)} %copy-done.1, bf16[8,8,48,384]{3,2,1,0:T(8,128)(2,1)S(1)} %bitcast.4, f32[2,256]{1,0:T(2,128)S(1)} %copy-done.2), custom_call_target="tpu_custom_call" | custom-call | tf_op jit(solution)/shard_map/pallas_call | solution.py:376
  75.8 0.0 copy-start.3
  75.8 0.0 copy-start.4
  75.8 0.0 copy-start.5
  75.8 0.0 copy-start.6
  75.9 0.0 copy-start.8
  75.9 22.2 %all_to_all.36.pair_ref = bf16[8,296,256]{2,1,0:T(8,128)(2,1)S(1)} all-to-all(bf16[8,296,256]{2,1,0:T(8,128)(2,1)S(1)} %get-tuple-element.68), channel_id=1, replica_groups=mesh['seq_0'=4,'seq_1a'=4,'seq_1b'=2,'seq_2'=2,'tp'=8] {'seq_1b','seq_0'}, dimensions={0} | all-to-all | bytes 2424832 | tf_op jit(solution)/shard_map/all_to_all | solution.py:43
  98.1 0.0 copy-done.3
  98.1 2.5 %shard_map.141 = bf16[8,40,128]{2,1,0:T(8,128)(2,1)} custom-call(s32[4]{0:T(128)S(1)} %copy-done.3, bf16[2,128,128]{2,1,0:T(8,128)(2,1)S(1)} %get-tuple-element.67.query_ref, bf16[8,296,256]{2,1,0:T(8,128)(2,1)S(1)} %all_to_all.36.pair_ref), custom_call_target="tpu_custom_call" | custom-call | tf_op jit(solution)/shard_map/pallas_call | solution.py:383
  100.6 3.4 %all-to-all-start.6 = ((bf16[8,40,128]{2,1,0:T(8,128)(2,1)}), bf16[8,40,128]{2,1,0:T(8,128)(2,1)S(1)}, u32[]{:S(2)}, u32[]{:S(2)}) async-start(bf16[8,40,128]{2,1,0:T(8,128)(2,1)} %shard_map.141), calls=%async_computation.6 | async-start | bytes 163840 | tf_op jit(solution)/shard_map/all_to_all | solution.py:43
  104.6 8.1 %all-to-all-done.6 = bf16[8,40,128]{2,1,0:T(8,128)(2,1)S(1)} async-done(((bf16[8,40,128]{2,1,0:T(8,128)(2,1)}), bf16[8,40,128]{2,1,0:T(8,128)(2,1)S(1)}, u32[]{:S(2)}, u32[]{:S(2)}) %all-to-all-start.6) | async-done | bytes 81952 | tf_op jit(solution)/shard_map/all_to_all | solution.py:43
  112.8 0.0 copy-done.4
  112.8 0.0 copy-done.5
  112.8 0.0 copy-done.6
  112.8 0.0 copy-done.8
  112.8 17.0 %conditional.1 = ((f32[4,32,384]{2,1,0:T(8,128)}, f32[4,32,384]{2,1,0:T(8,128)}, f32[4]{0:T(128)})) conditional(s32[]{:T(128)} %bitcast.1, (s32[4]{0:T(128)S(1)}, bf16[8,40,128]{2,1,0:T(8,128)(2,1)S(1)}, bf16[256,3072]{1,0:T(8,128)(2,1)S(1)}, f32[4,32,384]{2,1,0:T(8,128)S(1)}, bf16[4,32,384]{2,1,0:T(8,128)(2,1)S(1)}, ...), branch_computations={%region_0.0_spmd, %region_1.0_spmd, %region_2.0_spmd} | conditional | bytes 1277960 | solution.py:392
  112.8 0.9 branch_0_fun.2
  113.7 14.7 %all_to_all.32.part_ref = bf16[8,40,384]{2,1,0:T(8,128)(2,1)S(1)} all-to-all(bf16[8,40,384]{2,1,0:T(8,128)(2,1)S(1)} %branch_0_fun.2), channel_id=1, replica_groups=mesh['seq_0'=4,'seq_1a'=4,'seq_1b'=2,'seq_2'=2,'tp'=8] {'tp'}, dimensions={0} | all-to-all | bytes 491520 | tf_op jit(solution)/shard_map/cond/branch_0_fun/all_to_all | solution.py:43
  128.4 1.4 %branch_0_fun.3 = (f32[4,32,384]{2,1,0:T(8,128)}, f32[4,32,384]{2,1,0:T(8,128)}, f32[4]{0:T(128)}) custom-call(s32[4]{0:T(128)S(1)} %get-tuple-element.36.flag_ref, bf16[8,40,384]{2,1,0:T(8,128)(2,1)S(1)} %all_to_all.32.part_ref, f32[4,32,384]{2,1,0:T(8,128)S(1)} %get-tuple-element.90.cache_ref, bf16[4,32,384]{2,1,0:T(8,128)(2,1)S(1)} %get-tuple-element.40.img_ref, ...), custom_call_target="tpu_custom_call" | custom-call | tf_op jit(solution)/shard_map/cond/branch_0_fun/pallas_call | solution.py:406
  (1 shorter events, 0.0 us)
Async XLA Ops:
  28.1 5.7 %copy-start.7 = (bf16[3,4,384]{2,1,0:T(4,128)(2,1)S(1)}, bf16[3,4,384]{2,1,0:T(4,128)(2,1)}, u32[]{:S(2)}) copy-start(bf16[3,4,384]{2,1,0:T(4,128)(2,1)} %mod_ref.1) | copy-start | bytes 27652
  28.1 45.0 %all-to-all-start.4 = ((bf16[8,384,384]{2,1,0:T(8,128)(2,1)}), bf16[8,384,384]{2,1,0:T(8,128)(2,1)S(1)}, u32[]{:S(2)}, u32[]{:S(2)}) async-start(bf16[8,384,384]{2,1,0:T(8,128)(2,1)} %shard_map.139), calls=%async_computation.4 | async-start | bytes 4718592 | tf_op jit(solution)/shard_map/all_to_all | solution.py:43
  33.9 39.2 %copy-start.2 = (f32[2,256]{1,0:T(2,128)S(1)}, f32[2,256]{1,0:T(2,128)}, u32[]{:S(2)}) copy-start(f32[2,256]{1,0:T(2,128)} %gain_ref.1) | copy-start | bytes 6148
  67.7 4.4 %collective-permute-start = (bf16[8,152,384]{2,1,0:T(8,128)(2,1)S(1)}, bf16[8,152,384]{2,1,0:T(8,128)(2,1)S(1)}, u32[]{:S(2)}, u32[]{:S(2)}) collective-permute-start(bf16[8,152,384]{2,1,0:T(8,128)(2,1)S(1)} %shard_map.138.own_ref), channel_id=1, source_target_pairs={{0,8},{8,0},{1,9},{9,1},{2,10},{10,2},{3,11},{11,3},{4,12},{12,4},... | collective-permute-start | bytes 2801672 | tf_op jit(solution)/shard_map/ppermute | solution.py:374
  72.1 0.9 copy-start
  73.1 1.2 copy-start.1
  75.8 22.3 %copy-start.3 = (s32[4]{0:T(128)S(1)}, s32[4]{0:T(128)}, u32[]{:S(2)}) copy-start(s32[4]{0:T(128)} %limit_ref.1) | copy-start | bytes 52
  75.8 37.0 %copy-start.4 = (bf16[256,3072]{1,0:T(8,128)(2,1)S(1)}, bf16[256,3072]{1,0:T(8,128)(2,1)}, u32[]{:S(2)}) copy-start(bf16[256,3072]{1,0:T(8,128)(2,1)} %param.20) | copy-start | bytes 4718596
  75.8 36.9 %copy-start.5 = (f32[4,32,384]{2,1,0:T(8,128)S(1)}, f32[4,32,384]{2,1,0:T(8,128)}, u32[]{:S(2)}) copy-start(f32[4,32,384]{2,1,0:T(8,128)} %param.16) | copy-start | bytes 589828
  75.8 36.9 %copy-start.6 = (bf16[4,32,384]{2,1,0:T(8,128)(2,1)S(1)}, bf16[4,32,384]{2,1,0:T(8,128)(2,1)}, u32[]{:S(2)}) copy-start(bf16[4,32,384]{2,1,0:T(8,128)(2,1)} %img_hbm.1) | copy-start | bytes 294916
  75.9 36.9 %copy-start.8 = (s32[4]{0:T(128)S(1)}, s32[4]{0:T(128)}, u32[]{:S(2)}) copy-start(s32[4]{0:T(128)} %flag_hbm.1) | copy-start | bytes 52
  100.6 12.1 %all-to-all-start.6 = ((bf16[8,40,128]{2,1,0:T(8,128)(2,1)}), bf16[8,40,128]{2,1,0:T(8,128)(2,1)S(1)}, u32[]{:S(2)}, u32[]{:S(2)}) async-start(bf16[8,40,128]{2,1,0:T(8,128)(2,1)} %shard_map.141), calls=%async_computation.6 | async-start | bytes 163840 | tf_op jit(solution)/shard_map/all_to_all | solution.py:43
